TPU v7x, 256 devices: a whole 4x4x8 slice. The times are simulated.
256 devices in a mesh: fsdp: 32 (over z, y), ep: 8 (over x, core).
Axes of the slice: x: 4, y: 4, z: 8, core: 2. Of those that a mesh axis runs over, the one named last changes fastest.
Arguments:
- layer_in: bfloat16 [65536, 1024], P(('fsdp', 'ep'))
- out_grad: bfloat16 [65536, 1024], P(('fsdp', 'ep'))
- expert_ids: int32 [65536, 8], P(('fsdp', 'ep'))
- gate_vals: float32 [65536, 8], P(('fsdp', 'ep'))
- w_one: bfloat16 [128, 1024, 384], P('ep', 'fsdp')
- w_two: bfloat16 [128, 384, 1024], P('ep', None, 'fsdp')
- w_three: bfloat16 [128, 1024, 384], P('ep', 'fsdp')
Outputs:
- output 1: bfloat16 [65536, 1024], P(('fsdp', 'ep'))
- output 2: float32 [65536, 8], P(('fsdp', 'ep'))
- output 3: float32 [128, 1024, 384], P('ep', 'fsdp')
- output 4: float32 [128, 384, 1024], P('ep', None, 'fsdp')
- output 5: float32 [128, 1024, 384], P('ep', 'fsdp')
All inputs are finite; a program needn't handle non-finite values.
Results may differ from a plain program's by a relative error of at most 0.0103394.
Values are sent between devices in bfloat16 or wider.
A program may use at most 768 MiB of HBM per device.

v0:
```python
import jax
import jax.numpy as jnp
from jax import lax
from jax.sharding import PartitionSpec as P


def capacity_of(tok_dev, top_k, experts):
    return max(8, ((tok_dev * top_k * 5) // (4 * experts) + 7) // 8 * 8)


def route_slots(expert_ids, experts, capacity):
    flat_ids = expert_ids.reshape(-1)
    onehot = (flat_ids[:, None] == jnp.arange(experts, dtype=jnp.int32)[None, :]).astype(jnp.int32)
    before = jnp.cumsum(onehot, axis=0) - onehot
    position = jnp.sum(before * onehot, axis=1)
    return jnp.where(position < capacity, flat_ids * capacity + position, experts * capacity)


def slot_sources(slot_of, gate_vals, tok_dev, places):
    top_k = gate_vals.shape[-1]
    token_of = jnp.arange(slot_of.shape[0], dtype=jnp.int32) // top_k
    source = jnp.full((places,), tok_dev, jnp.int32).at[slot_of].set(token_of, mode="drop")
    slot_gate = jnp.zeros((places,), jnp.float32).at[slot_of].set(gate_vals.reshape(-1), mode="drop")
    return source, slot_gate


def take_rows(rows, row_index):
    return jnp.take(rows, row_index, axis=0, mode="fill", fill_value=0)


def expert_grads(x_rows, dy_rows, gate_rows, w_one, w_two, w_three):
    h_one = jnp.einsum("pecd,edf->pecf", x_rows, w_one, preferred_element_type=jnp.float32)
    h_three = jnp.einsum("pecd,edf->pecf", x_rows, w_three, preferred_element_type=jnp.float32)
    sig_one = jax.nn.sigmoid(h_one)
    silu_one = h_one * sig_one
    act_bf = (silu_one * h_three).astype(jnp.bfloat16)
    y_rows = jnp.einsum("pecf,efd->pecd", act_bf, w_two, preferred_element_type=jnp.float32)
    gate_grad = jnp.sum(dy_rows.astype(jnp.float32) * y_rows, axis=-1)
    g_rows = (gate_rows[..., None] * dy_rows.astype(jnp.float32)).astype(jnp.bfloat16)
    d_act = jnp.einsum("pecd,efd->pecf", g_rows, w_two, preferred_element_type=jnp.float32)
    dh_one = (d_act * h_three * sig_one * (1.0 + h_one * (1.0 - sig_one))).astype(jnp.bfloat16)
    dh_three = (d_act * silu_one).astype(jnp.bfloat16)
    dx_rows = (jnp.einsum("pecf,edf->pecd", dh_one, w_one, preferred_element_type=jnp.float32) + jnp.einsum("pecf,edf->pecd", dh_three, w_three, preferred_element_type=jnp.float32)).astype(jnp.bfloat16)
    grad_one = jnp.einsum("pecd,pecf->edf", x_rows, dh_one, preferred_element_type=jnp.float32)
    grad_three = jnp.einsum("pecd,pecf->edf", x_rows, dh_three, preferred_element_type=jnp.float32)
    grad_two = jnp.einsum("pecf,pecd->efd", act_bf, g_rows, preferred_element_type=jnp.float32)
    return dx_rows, gate_grad, grad_one, grad_two, grad_three


def solution(mesh):
    ep_size = mesh.shape["ep"]
    tok_spec = P(("fsdp", "ep"), None)
    up_spec = P("ep", "fsdp", None)
    down_spec = P("ep", None, "fsdp")

    def per_device(layer_in, out_grad, expert_ids, gate_vals, w_one, w_two, w_three):
        tok_dev, hidden = layer_in.shape
        top_k = expert_ids.shape[1]
        local_experts = w_one.shape[0]
        experts = local_experts * ep_size
        capacity = capacity_of(tok_dev, top_k, experts)
        places = experts * capacity
        slot_of = route_slots(expert_ids, experts, capacity)
        source, slot_gate = slot_sources(slot_of, gate_vals, tok_dev, places)
        send_shape = (ep_size, local_experts, capacity, hidden)
        x_send = take_rows(layer_in, source).reshape(send_shape)
        dy_send = take_rows(out_grad, source).reshape(send_shape)
        gate_send = slot_gate.reshape(ep_size, local_experts, capacity)
        x_rows = lax.all_to_all(x_send, "ep", 0, 0, tiled=True)
        dy_rows = lax.all_to_all(dy_send, "ep", 0, 0, tiled=True)
        gate_rows = lax.all_to_all(gate_send, "ep", 0, 0, tiled=True)
        w_one_full = lax.all_gather(w_one, "fsdp", axis=1, tiled=True)
        w_three_full = lax.all_gather(w_three, "fsdp", axis=1, tiled=True)
        w_two_full = lax.all_gather(w_two, "fsdp", axis=2, tiled=True)
        dx_rows, gate_grad, grad_one, grad_two, grad_three = expert_grads(x_rows, dy_rows, gate_rows, w_one_full, w_two_full, w_three_full)
        dx_back = lax.all_to_all(dx_rows, "ep", 0, 0, tiled=True).reshape(places, hidden)
        gate_back = lax.all_to_all(gate_grad, "ep", 0, 0, tiled=True).reshape(places)
        dx_pick = take_rows(dx_back, slot_of).reshape(tok_dev, top_k, hidden)
        in_grad = jnp.sum(dx_pick, axis=1, dtype=jnp.float32).astype(jnp.bfloat16)
        gate_out = take_rows(gate_back, slot_of).reshape(tok_dev, top_k)
        grad_one = lax.psum_scatter(grad_one, "fsdp", scatter_dimension=1, tiled=True)
        grad_three = lax.psum_scatter(grad_three, "fsdp", scatter_dimension=1, tiled=True)
        grad_two = lax.psum_scatter(grad_two, "fsdp", scatter_dimension=2, tiled=True)
        return in_grad, gate_out, grad_one, grad_two, grad_three

    return jax.shard_map(per_device, mesh=mesh, in_specs=(tok_spec, tok_spec, tok_spec, tok_spec, up_spec, down_spec, up_spec), out_specs=(tok_spec, tok_spec, up_spec, down_spec, up_spec), check_vma=False)
```

profile of v0, /device:TPU:1, one launch (start us, length us, event | category | flops | bytes accessed | tf_op | source)
XLA Modules:
  0.0 1207.7 jit_solution(4966368454701263972)
XLA Ops:
  7.2 0.7 all-gather.8.cloned.1.call-update
  8.0 0.7 all-gather.4.cloned.1.call-update
  8.7 0.7 all-gather.6.cloned.1.call-update
  9.4 0.8 copy.53
  10.6 0.1 mul.54
  10.7 0.8 copy.58
  11.6 0.3 fusion.37
  12.1 0.3 copy.56
  12.5 0.6 fusion.36
  13.1 0.6 copy-done.5
  13.7 8.1 scatter_custom_fusion
  21.9 0.7 reshape.174
  22.6 6.4 all-to-all-start
  29.0 8.1 scatter_custom_fusion.1
  37.1 14.0 %gather_fusion.3 = bf16[3072,1024]{1,0:T(8,128)(2,1)} fusion(bf16[256,1024]{1,0:T(8,128)(2,1)S(1)} %copy-done, s32[3072]{0:T(1024)S(1)} %fusion.40), kind=kCustom, calls=%fused_computation.1.clone | custom fusion | bytes 12595200 | tf_op jit(solution)/shard_map/jit(_take)/gather | solution.py:28
  51.1 13.9 %gather_fusion.2 = bf16[3072,1024]{1,0:T(8,128)(2,1)} fusion(bf16[256,1024]{1,0:T(8,128)(2,1)S(1)} %copy-done.2, s32[3072]{0:T(1024)S(1)} %fusion.40), kind=kCustom, calls=%fused_computation.clone | custom fusion | bytes 12595200 | tf_op jit(solution)/shard_map/jit(_take)/gather | solution.py:28
  65.0 10.2 broadcast_select_fusion.1
  75.2 76.3 %all_to_all.25 = bf16[8,16,24,1024]{3,2,1,0:T(8,128)(2,1)} all-to-all(bf16[8,16,24,1024]{3,2,1,0:T(8,128)(2,1)} %bitcast.104), channel_id=1, replica_groups=mesh['fsdp'=32,'ep'=8] {'ep'}, dimensions={0} | all-to-all | bytes 12582912 | tf_op jit(solution)/shard_map/all_to_all | solution.py:69
  151.4 5.8 all-to-all-start.1
  157.2 0.5 reduce-scatter.6.cloned.1.call-start
  157.7 0.6 broadcast.137
  158.3 0.7 reduce.1
  159.2 12.1 fusion.4
  171.2 57.0 %all-to-all-done.1 = bf16[8,16,24,1024]{3,2,1,0:T(8,128)(2,1)} async-done(((bf16[8,16,24,1024]{3,2,1,0:T(8,128)(2,1)}), bf16[8,16,24,1024]{3,2,1,0:T(8,128)(2,1)}, u32[]{:S(2)}, u32[]{:S(2)}) %all-to-all-start.1) | async-done | bytes 6291488 | tf_op jit(solution)/shard_map/all_to_all | solution.py:70
  228.3 21.5 %all-gather.4.cloned.1.call-done = bf16[16,384,1024]{1,2,0:T(8,128)(2,1)} async-done(((bf16[16,384,32]{1,2,0:T(8,128)(2,1)}), bf16[16,384,1024]{1,2,0:T(8,128)(2,1)}) %all-gather.4.cloned.1.call-update) | async-done | bytes 12582928 | tf_op jit(solution)/shard_map/all_gather | solution.py:74
  249.7 12.1 fusion.8
  261.8 105.9 %all-gather.6.cloned.1.call-done = bf16[16,1024,384]{2,1,0:T(8,128)(2,1)} async-done(((bf16[16,32,384]{2,1,0:T(8,128)(2,1)}), bf16[16,1024,384]{2,1,0:T(8,128)(2,1)}) %all-gather.6.cloned.1.call-update) | async-done | bytes 12582928 | tf_op jit(solution)/shard_map/all_gather | solution.py:73
  367.6 14.2 %fusion.26 = (bf16[8,16,24,384]{3,2,0,1:T(8,128)(2,1)}, bf16[8,16,24,384]{3,2,0,1:T(8,128)(2,1)}, bf16[8,16,24,384]{3,2,0,1:T(8,128)(2,1)S(1)}) fusion(f32[16,8,24,384]{3,2,1,0:T(8,128)} %fusion.4, f32[16,8,24,384]{3,2,1,0:T(8,128)} %fusion.8, bf16[16,1024,384]{2,1,0:T(8,128)(2,1)} %all-gather.6.cloned.1.call-done, bf16[8,16,24,1024]{3,2,1,0:T(8,128)(2,1)} %all_to_all.25), kind=kOutput, calls=%fused_computation.43 | convolution fusion | flops 2433613824 | bytes 35389440 | tf_op jit(solution)/shard_map/pecd,edf->pecf/dot_general | solution.py:33
  381.9 16.5 %convolution_bitcast_fusion.1 = f32[16,384,1024]{1,2,0:T(8,128)} fusion(bf16[8,16,24,384]{3,2,0,1:T(8,128)(2,1)} %get-tuple-element.28, f32[8,16,24]{2,0,1:T(8,128)S(1)} %copy.59, bf16[8,16,24,1024]{3,2,1,0:T(8,128)(2,1)} %all-to-all-done.1), kind=kOutput, calls=%fused_computation.24 | convolution fusion | flops 2425356288 | bytes 33828864 | tf_op jit(solution)/shard_map/pecf,pecd->efd/dot_general | solution.py:46
  398.4 0.3 reduce-scatter.8.cloned.1.call-start
  398.7 15.8 %convolution_bitcast_fusion = f32[16,1024,384]{2,1,0:T(8,128)} fusion(bf16[8,16,24,1024]{3,2,1,0:T(8,128)(2,1)} %all_to_all.25, bf16[8,16,24,384]{3,2,0,1:T(8,128)(2,1)S(1)} %get-tuple-element.30), kind=kOutput, calls=%fused_computation.23 | convolution fusion | flops 2415919104 | bytes 33816576 | tf_op jit(solution)/shard_map/pecd,pecf->edf/dot_general | solution.py:45
  414.5 16.5 %convolution_bitcast_fusion.2 = f32[16,1024,384]{2,1,0:T(8,128)} fusion(bf16[8,16,24,1024]{3,2,1,0:T(8,128)(2,1)} %all_to_all.25, bf16[8,16,24,384]{3,2,0,1:T(8,128)(2,1)} %get-tuple-element.29), kind=kOutput, calls=%fused_computation.25 | convolution fusion | flops 2415919104 | bytes 33816576 | tf_op jit(solution)/shard_map/pecd,pecf->edf/dot_general | solution.py:44
  431.0 10.3 fusion.1
  441.3 0.7 reshape.176
  442.0 6.0 all-to-all-start.4
  448.1 15.3 %fusion.2 = f32[16,8,24,1024]{3,2,1,0:T(8,128)} fusion(bf16[8,16,24,384]{3,2,0,1:T(8,128)(2,1)} %get-tuple-element.29, bf16[16,1024,384]{2,1,0:T(8,128)(2,1)} %all-gather.8.cloned.1.call-done), kind=kOutput, calls=%fused_computation.10 | convolution fusion | flops 2415919104 | bytes 27525120 | tf_op jit(solution)/shard_map/pecf,edf->pecd/dot_general | solution.py:43
  463.4 12.7 %fusion.14 = bf16[8,16,24,1024]{3,2,0,1:T(8,128)(2,1)} fusion(f32[16,8,24,1024]{3,2,1,0:T(8,128)} %fusion.2, bf16[8,16,24,384]{3,2,0,1:T(8,128)(2,1)S(1)} %get-tuple-element.30, bf16[16,1024,384]{2,1,0:T(8,128)(2,1)} %all-gather.6.cloned.1.call-done), kind=kOutput, calls=%fused_computation.26 | convolution fusion | flops 2422210560 | bytes 33816576 | tf_op jit(solution)/shard_map/pecf,edf->pecd/dot_general | solution.py:43
  476.2 6.5 copy.63
  482.7 4.9 all-to-all-start.3
  487.8 0.7 reduce.2
  488.7 11.8 gather_fusion.1
  500.6 0.7 copy.67
  501.3 57.4 %all-to-all-done.3 = bf16[8,16,24,1024]{3,2,1,0:T(8,128)(2,1)} async-done(((bf16[8,16,24,1024]{3,2,1,0:T(8,128)(2,1)}), bf16[8,16,24,1024]{3,2,1,0:T(8,128)(2,1)}, u32[]{:S(2)}, u32[]{:S(2)}) %all-to-all-start.3) | async-done | bytes 6291488 | tf_op jit(solution)/shard_map/all_to_all | solution.py:76
  558.7 14.6 %gather_fusion = bf16[2048,1024]{1,0:T(8,128)(2,1)} fusion(bf16[3072,1024]{1,0:T(8,128)(2,1)} %bitcast.18, s32[2048]{0:T(1024)S(1)} %broadcast_clamp_fusion), kind=kCustom, calls=%fused_computation.2 | custom fusion | bytes 8396800 | tf_op jit(solution)/shard_map/jit(_take)/gather | solution.py:28
  573.3 4.9 fusion.28
  578.3 82.0 %reduce-scatter.6.cloned.1.call-done = f32[16,384,32]{1,2,0:T(8,128)} async-done(((f32[16,384,1024]{1,2,0:T(8,128)}), f32[16,384,32]{1,2,0:T(8,128)}) %reduce-scatter.6.cloned.1.call-update) | async-done | bytes 786448 | tf_op jit(solution)/shard_map/reduce_scatter | solution.py:83
  660.3 270.0 %reduce-scatter.8.cloned.1.call-done = f32[16,32,384]{2,1,0:T(8,128)} async-done(((f32[16,1024,384]{2,1,0:T(8,128)}), f32[16,32,384]{2,1,0:T(8,128)}) %reduce-scatter.8.cloned.1.call-update) | async-done | bytes 786448 | tf_op jit(solution)/shard_map/reduce_scatter | solution.py:82
  930.3 270.2 %reduce-scatter.4.cloned.1.call-done = f32[16,32,384]{2,1,0:T(8,128)} async-done(((f32[16,1024,384]{2,1,0:T(8,128)}), f32[16,32,384]{2,1,0:T(8,128)}) %reduce-scatter.4.cloned.1.call-update) | async-done | bytes 786448 | tf_op jit(solution)/shard_map/reduce_scatter | solution.py:81
  (50 shorter events, 1.5 us)
Async XLA Ops:
  7.2 29.9 %copy-start = (bf16[256,1024]{1,0:T(8,128)(2,1)S(1)}, bf16[256,1024]{1,0:T(8,128)(2,1)}, u32[]{:S(2)}) copy-start(bf16[256,1024]{1,0:T(8,128)(2,1)} %param.9) | copy-start | bytes 1572868
  7.2 152.0 %all-gather.8.cloned.1.call-start = ((), (), s32[]{:S(2)}) async-start(), calls=%async_computation.10 | async-start | bytes 12976128 | tf_op jit(solution)/shard_map/all_gather | solution.py:72
  7.9 241.8 %all-gather.4.cloned.1.call-start = ((), (), s32[]{:S(2)}) async-start(), calls=%async_computation.8 | async-start | bytes 12976128 | tf_op jit(solution)/shard_map/all_gather | solution.py:74
  8.7 359.0 %all-gather.6.cloned.1.call-start = ((), (), s32[]{:S(2)}) async-start(), calls=%async_computation.9 | async-start | bytes 12976128 | tf_op jit(solution)/shard_map/all_gather | solution.py:73
  10.2 1.3 copy-start.3
  13.1 0.6 copy-start.5
  13.7 15.3 %copy-start.7 = (s32[2048,1]{0,1:T(1,128)}, s32[2048,1]{0,1:T(1,128)S(1)}, u32[]{:S(2)}) copy-start(s32[2048,1]{0,1:T(1,128)S(1)} %compare_select_fusion.1) | copy-start | bytes 24580
  22.6 52.6 %all-to-all-start = ((f32[8,1,384]{2,1,0:T(1,128)}), f32[8,1,384]{2,1,0:T(1,128)S(1)}, u32[]{:S(2)}, u32[]{:S(2)}) async-start(f32[8,1,384]{2,1,0:T(1,128)} %reshape.174), calls=%async_computation | async-start | bytes 24576 | tf_op jit(solution)/shard_map/all_to_all | solution.py:71
  37.1 14.0 %copy-start.2 = (bf16[256,1024]{1,0:T(8,128)(2,1)S(1)}, bf16[256,1024]{1,0:T(8,128)(2,1)}, u32[]{:S(2)}) copy-start(bf16[256,1024]{1,0:T(8,128)(2,1)} %param.10) | copy-start | bytes 1572868
  151.4 76.8 %all-to-all-start.1 = ((bf16[8,16,24,1024]{3,2,1,0:T(8,128)(2,1)}), bf16[8,16,24,1024]{3,2,1,0:T(8,128)(2,1)}, u32[]{:S(2)}, u32[]{:S(2)}) async-start(bf16[8,16,24,1024]{3,2,1,0:T(8,128)(2,1)} %bitcast.103), calls=%async_computation.1 | async-start | bytes 12582912 | tf_op jit(solution)/shard_map/all_to_all | solution.py:70
  157.2 503.1 %reduce-scatter.6.cloned.1.call-start = ((), (), s32[]{:S(2)}) async-start(), calls=%async_computation.12 | async-start | bytes 25952256 | tf_op jit(solution)/shard_map/reduce_scatter | solution.py:83
  398.4 531.9 %reduce-scatter.8.cloned.1.call-start = ((), (), s32[]{:S(2)}) async-start(), calls=%async_computation.13 | async-start | bytes 25952256 | tf_op jit(solution)/shard_map/reduce_scatter | solution.py:82
  414.5 786.1 %reduce-scatter.4.cloned.1.call-start = ((), (), s32[]{:S(2)}) async-start(), calls=%async_computation.11 | async-start | bytes 25952256 | tf_op jit(solution)/shard_map/reduce_scatter | solution.py:81
  442.0 40.7 %all-to-all-start.4 = ((f32[8,1,384]{2,1,0:T(1,128)}), f32[8,1,384]{2,1,0:T(1,128)S(1)}, u32[]{:S(2)}, u32[]{:S(2)}) async-start(f32[8,1,384]{2,1,0:T(1,128)} %reshape.176), calls=%async_computation.4 | async-start | bytes 24576 | tf_op jit(solution)/shard_map/all_to_all | solution.py:77
  482.7 5.0 copy-start.6
  482.7 5.1 copy-start.8
  482.7 76.0 %all-to-all-start.3 = ((bf16[8,16,24,1024]{3,2,1,0:T(8,128)(2,1)}), bf16[8,16,24,1024]{3,2,1,0:T(8,128)(2,1)}, u32[]{:S(2)}, u32[]{:S(2)}) async-start(bf16[8,16,24,1024]{3,2,1,0:T(8,128)(2,1)} %copy.63), calls=%async_computation.3 | async-start | bytes 12582912 | tf_op jit(solution)/shard_map/all_to_all | solution.py:76
  487.6 12.9 %copy-start.4 = (s32[256,8]{1,0:T(8,128)S(1)}, s32[256,8]{1,0:T(8,128)}, u32[]{:S(2)}) copy-start(s32[256,8]{1,0:T(8,128)} %copy-done.3) | copy-start | bytes 24580
  558.7 641.9 %copy-start.1 = (bf16[256,1024]{1,0:T(8,128)(2,1)S(1)}, bf16[256,1024]{1,0:T(8,128)(2,1)}, u32[]{:S(2)}) copy-start(bf16[256,1024]{1,0:T(8,128)(2,1)} %param.9) | copy-start | bytes 1572868
Sparse Core Ops, SparseCore 0:
  10.6 121.1 all-gather.7
  134.4 115.2 all-gather.3
  252.3 115.2 all-gather.5
  398.5 261.7 reduce-scatter.5
  664.9 265.4 reduce-scatter.7
  934.9 265.6 reduce-scatter.3
where the time goes:
time: 1220 us; the launch traced here: 1210 us
  waiting for transfers between devices  866 us (71%)
  matrix products  125 us (10%)
  local copies, waits for them, and re-layouts  83.3 us (7%)
  blocking collectives  76.3 us (6%)
  starting transfers between devices  24.1 us (2%)
  other arithmetic  17.7 us (1%)
  between operations  14.7 us (1%)
    reduce_scatter x1, waiting for transfers between devices, per_device(): lax.psum_scatter(grad_one, 'fsdp', scatter_dimension=1, tiled=True)  270 us
    reduce_scatter x1, waiting for transfers between devices, per_device(): lax.psum_scatter(grad_three, 'fsdp', scatter_dimension=1, tiled=True)  270 us
    all_gather x1, waiting for transfers between devices, per_device(): w_three_full = lax.all_gather(w_three, 'fsdp', axis=1, tiled=True)  106 us
    reduce_scatter x1, waiting for transfers between devices, per_device(): lax.psum_scatter(grad_two, 'fsdp', scatter_dimension=2, tiled=True)  82 us
    all_to_all x1, blocking collectives, per_device(): x_rows = lax.all_to_all(x_send, 'ep', 0, 0, tiled=True)  76.3 us
    all_to_all x1, waiting for transfers between devices, per_device(): lax.all_to_all(dx_rows, 'ep', 0, 0, tiled=True).reshape(places, hidden)  57.4 us
    all_to_all x1, waiting for transfers between devices, per_device(): dy_rows = lax.all_to_all(dy_send, 'ep', 0, 0, tiled=True)  57 us
    gather x5, local copies, waits for them, and re-layouts, take_rows(): return jnp.take(rows, row_index, axis=0, mode='fill', fill_value=0)  54.4 us
  transfers between devices with their start and end apart: 10, of which 7 were waited for; matrix products, arithmetic and copies ran while one was open for 16% of the time, Pallas kernels for 0%

commit v1 on v0

v1 whole, which is shorter than its diff:
```python
import jax
import jax.numpy as jnp
from jax import lax
from jax.sharding import Mesh, PartitionSpec as P

NZ, NY, NX, NC = 8, 4, 4, 2
PLANE = ("y", "x", "core")


def capacity_of(tok_dev, top_k, experts):
    return max(8, ((tok_dev * top_k * 5) // (4 * experts) + 7) // 8 * 8)


def route_slots(expert_ids, experts, capacity):
    flat_ids = expert_ids.reshape(-1)
    onehot = (flat_ids[:, None] == jnp.arange(experts, dtype=jnp.int32)[None, :]).astype(jnp.int32)
    before = jnp.cumsum(onehot, axis=0) - onehot
    position = jnp.sum(before * onehot, axis=1)
    return jnp.where(position < capacity, flat_ids * capacity + position, experts * capacity)


def slot_sources(slot_of, gate_vals, tok_dev, places):
    top_k = gate_vals.shape[-1]
    token_of = jnp.arange(slot_of.shape[0], dtype=jnp.int32) // top_k
    source = jnp.full((places,), tok_dev, jnp.int32).at[slot_of].set(token_of, mode="drop")
    slot_gate = jnp.zeros((places,), jnp.float32).at[slot_of].set(gate_vals.reshape(-1), mode="drop")
    return source, slot_gate


def take_rows(rows, row_index):
    return jnp.take(rows, row_index, axis=0, mode="fill", fill_value=0)


def dot(spec, a, b):
    return jnp.einsum(spec, a, b, preferred_element_type=jnp.float32)


def expert_grads(x_rows, dy_rows, gate_rows, w_one, w_two_t, w_three):
    h_one = dot("erd,edf->erf", x_rows, w_one)
    h_three = dot("erd,edf->erf", x_rows, w_three)
    sig_one = jax.nn.sigmoid(h_one)
    silu_one = h_one * sig_one
    act_bf = (silu_one * h_three).astype(jnp.bfloat16)
    y_rows = dot("erf,edf->erd", act_bf, w_two_t)
    gate_grad = jnp.sum(dy_rows.astype(jnp.float32) * y_rows, axis=-1)
    g_rows = (gate_rows[..., None] * dy_rows.astype(jnp.float32)).astype(jnp.bfloat16)
    d_act = dot("erd,edf->erf", g_rows, w_two_t)
    dh_one = (d_act * h_three * sig_one * (1.0 + h_one * (1.0 - sig_one))).astype(jnp.bfloat16)
    dh_three = (d_act * silu_one).astype(jnp.bfloat16)
    dx_rows = (dot("erf,edf->erd", dh_one, w_one) + dot("erf,edf->erd", dh_three, w_three)).astype(jnp.bfloat16)
    grad_one = dot("erd,erf->edf", x_rows, dh_one)
    grad_three = dot("erd,erf->edf", x_rows, dh_three)
    grad_two_t = dot("erd,erf->edf", g_rows, act_bf)
    return dx_rows, gate_grad, grad_one, grad_two_t, grad_three


def solution(mesh):
    mesh4 = Mesh(mesh.devices.reshape(NZ, NY, NX, NC), ("z", "y", "x", "core"))
    tok_spec = P(("z", "y", "x", "core"), None)
    up_spec = P(("x", "core"), ("z", "y"), None)
    down_spec = P(("x", "core"), None, ("z", "y"))

    def per_device(layer_in, out_grad, expert_ids, gate_vals, w_one, w_two, w_three):
        tok_dev, hidden = layer_in.shape
        top_k = expert_ids.shape[1]
        local_experts, d_loc, ff = w_one.shape
        ep = NX * NC
        own = local_experts // NY
        experts = local_experts * ep
        capacity = capacity_of(tok_dev, top_k, experts)
        places = experts * capacity
        group = NY * ep
        w_all = jnp.stack([w_one, w_three, w_two.swapaxes(1, 2)]).reshape(3, NY, own, d_loc, ff)
        w_all = lax.all_to_all(w_all.swapaxes(0, 1), "y", 0, 0, tiled=True)
        w_all = lax.all_gather(w_all, "z", axis=0)
        w_full = w_all.transpose(2, 3, 0, 1, 4, 5).reshape(3, own, hidden, ff)

        ids = expert_ids
        ids = (ids % local_experts) // own * (ep * own) + ids // local_experts * own + ids % own
        slot_of = route_slots(ids, experts, capacity)
        source, slot_gate = slot_sources(slot_of, gate_vals, tok_dev, places)
        x_send = take_rows(layer_in, source).reshape(group, own * capacity, hidden)
        dy_send = take_rows(out_grad, source).reshape(group, own * capacity, hidden)
        gate_send = slot_gate.reshape(group, own * capacity)

        def exchange(v):
            return lax.all_to_all(v, PLANE, 0, 0, tiled=True)

        def by_expert(v):
            v = v.reshape((group, own, capacity) + v.shape[2:])
            return v.swapaxes(0, 1).reshape((own, group * capacity) + v.shape[3:])

        def by_source(v):
            v = v.reshape((own, group, capacity) + v.shape[2:])
            return v.swapaxes(0, 1).reshape((group, own * capacity) + v.shape[3:])

        x_rows = by_expert(exchange(x_send))
        dy_rows = by_expert(exchange(dy_send))
        gate_rows = by_expert(exchange(gate_send))
        dx_rows, gate_grad, grad_one, grad_two_t, grad_three = expert_grads(x_rows, dy_rows, gate_rows, w_full[0], w_full[2], w_full[1])

        def home(grad):
            grad = lax.psum_scatter(grad, "z", scatter_dimension=1, tiled=True)
            return grad.reshape(own, NY, d_loc, ff).swapaxes(0, 1)

        grads = jnp.stack([home(grad_one), home(grad_three), home(grad_two_t)], axis=1)
        grads = lax.all_to_all(grads, "y", 0, 0, tiled=True)

        dx_back = exchange(by_source(dx_rows)).reshape(places, hidden)
        gate_back = exchange(by_source(gate_grad)).reshape(places)
        dx_pick = take_rows(dx_back, slot_of).reshape(tok_dev, top_k, hidden)
        in_grad = jnp.sum(dx_pick, axis=1, dtype=jnp.float32).astype(jnp.bfloat16)
        gate_out = take_rows(gate_back, slot_of).reshape(tok_dev, top_k)

        grads = grads.swapaxes(0, 1).reshape(3, local_experts, d_loc, ff)
        return in_grad, gate_out, grads[0], grads[2].swapaxes(1, 2), grads[1]

    return jax.shard_map(per_device, mesh=mesh4, in_specs=(tok_spec, tok_spec, tok_spec, tok_spec, up_spec, down_spec, up_spec), out_specs=(tok_spec, tok_spec, up_spec, down_spec, up_spec), check_vma=False)
```

time: 1220 us -> 608 us (0.50)
  waiting for transfers between devices: 866 us -> 219 us
  matrix products: 125 us -> 70.8 us
  local copies, waits for them, and re-layouts: 83.3 us -> 120 us
  blocking collectives: 76.3 us -> 105 us
  other arithmetic: 17.7 us -> 37.9 us
    reduce_scatter x3, waiting for transfers between devices: 622 us -> 160 us  [home(): grad = lax.psum_scatter(grad, 'z', scatter_dimension=1, tiled=True)]
    all_gather x3 -> x1, waiting for transfers between devices: 127 us -> 0.01 us  [per_device(): w_all = lax.all_gather(w_all, 'z', axis=0)]
    all_to_all x4 -> x5, waiting for transfers between devices: 114 us -> 58.8 us  [the longest x4 58.8 us: exchange(): return lax.all_to_all(v, PLANE, 0, 0, tiled=True)]
    dot_general x9, matrix products: 125 us -> 70.8 us  [dot(): return jnp.einsum(spec, a, b, preferred_element_type=jnp.float32)]
    all_to_all x1 -> x2, blocking collectives: 76.3 us -> 105 us  [the longest x1 85 us: exchange(): return lax.all_to_all(v, PLANE, 0, 0, tiled=True)]
    convert_element_type x0 -> x2, other arithmetic: none -> 16.8 us  [the longest x1 8.84 us: expert_grads(): dy_rows.astype(jnp.float32)]
    all_to_all x4 -> x5, starting transfers between devices: 23.1 us -> 34.3 us  [the longest x4 30.3 us: exchange(): return lax.all_to_all(v, PLANE, 0, 0, tiled=True)]
  transfers between devices with their start and end apart: 10 -> 9, of which waited for: 7 -> 4; matrix products, arithmetic and copies ran while one was open for 16% -> 30% of each run, Pallas kernels for 0% -> 0%
where the time goes in v1:
time: 608 us; the launch traced here: 602 us
  waiting for transfers between devices  219 us (36%)
  local copies, waits for them, and re-layouts  120 us (20%)
  blocking collectives  105 us (17%)
  matrix products  70.8 us (12%)
  other arithmetic  37.9 us (6%)
  starting transfers between devices  35.2 us (6%)
  between operations  14.4 us (2%)
    reduce_scatter x3, waiting for transfers between devices, home(): grad = lax.psum_scatter(grad, 'z', scatter_dimension=1, tiled=True)  160 us
    all_to_all x1, blocking collectives, exchange(): return lax.all_to_all(v, PLANE, 0, 0, tiled=True)  85 us
    dot_general x9, matrix products, dot(): return jnp.einsum(spec, a, b, preferred_element_type=jnp.float32)  70.8 us
    all_to_all x4, waiting for transfers between devices, exchange(): return lax.all_to_all(v, PLANE, 0, 0, tiled=True)  58.8 us
    gather x5, local copies, waits for them, and re-layouts, take_rows(): return jnp.take(rows, row_index, axis=0, mode='fill', fill_value=0)  54.3 us
    all_to_all x4, starting transfers between devices, exchange(): return lax.all_to_all(v, PLANE, 0, 0, tiled=True)  30.3 us
    all_to_all x1, blocking collectives, per_device(): w_all = lax.all_to_all(w_all.swapaxes(0, 1), 'y', 0, 0, tiled=True)  19.7 us
  transfers between devices with their start and end apart: 9, of which 4 were waited for; matrix products, arithmetic and copies ran while one was open for 30% of the time, Pallas kernels for 0%

profile of v1, /device:TPU:1, one launch (start us, length us, event | category | flops | bytes accessed | tf_op | source)
XLA Modules:
  0.0 601.6 jit_solution(2194786014371172436)
XLA Ops:
  7.2 1.4 maximum_bitcast_fusion
  8.7 19.7 %all_to_all.43 = bf16[4,3,4,32,384]{4,3,2,1,0:T(8,128)(2,1)} all-to-all(bf16[4,3,4,32,384]{4,3,2,1,0:T(8,128)(2,1)S(1)} %maximum_bitcast_fusion), channel_id=1, replica_groups=mesh['z'=8,'y'=4,'x'=4,'core'=2] {'y'}, dimensions={0} | all-to-all | bytes 2359296 | tf_op jit(solution)/shard_map/all_to_all | solution.py:74
  31.4 8.1 %scatter_custom_fusion = f32[3072]{0:T(1024)S(1)} fusion(s32[2048]{0:T(1024)S(1)} %bitcast.132, f32[2048]{0:T(1024)S(1)} %reshape.217, f32[]{:T(128)} %constant.114.clone.1), kind=kCustom, calls=%fused_computation.77 | custom fusion | bytes 12292 | tf_op jit(solution)/shard_map/scatter | solution.py:26
  39.5 0.7 all_to_all.27
  40.2 7.7 %all-to-all-start = ((f32[32,1,96]{2,1,0:T(1,128)}), f32[32,1,96]{2,1,0:T(1,128)S(1)}, u32[]{:S(2)}, u32[]{:S(2)}) async-start(f32[32,1,96]{2,1,0:T(1,128)} %all_to_all.27), calls=%async_computation | async-start | bytes 32768 | tf_op jit(solution)/shard_map/all_to_all | solution.py:87
  47.8 8.1 %scatter_custom_fusion.1 = s32[3072]{0:T(1024)S(1)} fusion(s32[2048]{0:T(1024)S(1)} %bitcast.133, s32[2048]{0:T(1024)S(1)} %add_select_fusion.4, s32[]{:T(128)} %constant.115.clone.1), kind=kCustom, calls=%fused_computation.75 | custom fusion | bytes 12292 | tf_op jit(solution)/shard_map/scatter | solution.py:25
  56.0 13.9 %gather_fusion.2 = bf16[3072,1024]{1,0:T(8,128)(2,1)} fusion(bf16[256,1024]{1,0:T(8,128)(2,1)S(1)} %copy-done, s32[3072]{0:T(1024)S(1)} %fusion.18), kind=kCustom, calls=%fused_computation.clone | custom fusion | bytes 12595200 | tf_op jit(solution)/shard_map/jit(_take)/gather | solution.py:31
  69.9 13.9 %gather_fusion.3 = bf16[3072,1024]{1,0:T(8,128)(2,1)} fusion(bf16[256,1024]{1,0:T(8,128)(2,1)S(1)} %copy-done.2, s32[3072]{0:T(1024)S(1)} %fusion.18), kind=kCustom, calls=%fused_computation.1.clone | custom fusion | bytes 12595200 | tf_op jit(solution)/shard_map/jit(_take)/gather | solution.py:31
  83.8 10.3 %broadcast_select_fusion.1 = (bf16[3072,1024]{1,0:T(8,128)(2,1)}, bf16[3072,1024]{1,0:T(8,128)(2,1)}) fusion(bf16[3072,1024]{1,0:T(8,128)(2,1)} %gather_fusion.2, pred[3072]{0:T(1024)(128)(4,1)S(1)} %compare_and_fusion.1, bf16[3072,1024]{1,0:T(8,128)(2,1)} %gather_fusion.3), kind=kLoop, calls=%fused_computation.14 | loop fusion | flops 6291456 | bytes 25168896 | tf_op jit(solution)/shard_map/jit(_take)/select_n | solution.py:31
  94.1 85.0 %all_to_all.44 = bf16[32,96,1024]{2,1,0:T(8,128)(2,1)} all-to-all(bf16[32,96,1024]{2,1,0:T(8,128)(2,1)} %bitcast.107), channel_id=1, replica_groups=mesh['z'=8,'y'=4,'x'=4,'core'=2] {'y','x','core'}, dimensions={0} | all-to-all | bytes 12582912 | tf_op jit(solution)/shard_map/all_to_all | solution.py:87
  179.1 7.5 %all-to-all-start.3 = ((bf16[32,96,1024]{2,1,0:T(8,128)(2,1)}), bf16[32,96,1024]{2,1,0:T(8,128)(2,1)}, u32[]{:S(2)}, u32[]{:S(2)}) async-start(bf16[32,96,1024]{2,1,0:T(8,128)(2,1)} %bitcast.105), calls=%async_computation.3 | async-start | bytes 12582912 | tf_op jit(solution)/shard_map/all_to_all | solution.py:87
  187.7 0.7 reduce.7
  188.6 8.8 %convert_bitcast_fusion = f32[4,32,24,1024]{3,2,0,1:T(8,128)} fusion(bf16[32,4,24,1024]{3,2,1,0:T(8,128)(2,1)} %bitcast.106), kind=kLoop, calls=%fused_computation.6 | loop fusion | flops 3145728 | bytes 18874368 | tf_op jit(solution)/shard_map/convert_element_type | solution.py:46
  197.4 11.8 %copy.69 = f32[4,32,24,1024]{3,2,1,0:T(8,128)} copy(f32[4,32,24,1024]{3,2,0,1:T(8,128)} %convert_bitcast_fusion) | data formatting | bytes 25165824 | tf_op jit(solution)/shard_map/convert_element_type | solution.py:46
  209.3 58.8 %all-to-all-done.3 = bf16[32,96,1024]{2,1,0:T(8,128)(2,1)} async-done(((bf16[32,96,1024]{2,1,0:T(8,128)(2,1)}), bf16[32,96,1024]{2,1,0:T(8,128)(2,1)}, u32[]{:S(2)}, u32[]{:S(2)}) %all-to-all-start.3) | async-done | bytes 6291488 | tf_op jit(solution)/shard_map/all_to_all | solution.py:87
  268.0 6.4 %copy.71 = bf16[4,32,24,1024]{3,2,1,0:T(8,128)(2,1)} copy(bf16[4,32,24,1024]{3,2,0,1:T(8,128)(2,1)} %bitcast.20) | data formatting | bytes 12582912 | tf_op jit(solution)/shard_map/transpose | solution.py:91
  274.5 7.9 %fusion = bf16[4,768,1024]{2,1,0:T(8,128)(2,1)} fusion(f32[4,32,24,1024]{3,2,1,0:T(8,128)} %copy.69, f32[4,768]{1,0:T(4,128)S(1)} %mul.70), kind=kLoop, calls=%fused_computation.9 | loop fusion | flops 6291456 | bytes 18886656 | tf_op jit(solution)/shard_map/convert_element_type | solution.py:46
  282.4 9.3 %copy.89 = bf16[8,4,3,4,32,384]{5,4,1,0,3,2:T(8,128)(2,1)} copy(bf16[8,4,3,4,32,384]{5,4,3,2,1,0:T(8,128)(2,1)} %bitcast.115) | data formatting | bytes 18874368 | tf_op jit(solution)/shard_map/all_gather | solution.py:75
  291.7 4.6 fusion.27
  296.4 0.9 copy-done.3
  297.3 5.0 fusion.29
  302.3 5.0 fusion.30
  307.4 9.1 %multiply_convert_fusion = (bf16[4,768,384]{2,1,0:T(8,128)(2,1)}, bf16[4,768,384]{2,1,0:T(8,128)(2,1)}, bf16[4,768,384]{2,1,0:T(8,128)(2,1)S(1)}) fusion(f32[4,768,384]{2,1,0:T(8,128)} %fusion.30, f32[4,768,384]{2,1,0:T(8,128)} %fusion.29, bf16[4,768,1024]{2,1,0:T(8,128)(2,1)S(1)} %bitcast.101, bf16[4,1024,384]{2,1,0:T(8,128)(2,1)S(1)} %bitcast.111), kind=kOutput, calls=%fused_computation.15 | convolution fusion | flops 2433613824 | bytes 25952256 | tf_op jit(solution)/shard_map/erd,edf->erf/dot_general | solution.py:35
  316.5 1.4 copy-done.8
  317.9 5.4 fusion.33
  323.3 1.6 copy-done.5
  324.9 8.8 %fusion.32 = f32[4,1024,384]{2,1,0:T(8,128)} fusion(bf16[4,768,1024]{2,1,0:T(8,128)(2,1)} %bitcast.97, bf16[4,768,384]{2,1,0:T(8,128)(2,1)S(1)} %copy-done.5), kind=kOutput, calls=%fused_computation.85 | convolution fusion | flops 2415919104 | bytes 14942208 | tf_op jit(solution)/shard_map/erd,erf->edf/dot_general | solution.py:35
  334.0 9.6 %fusion.34 = f32[4,1024,384]{2,1,0:T(8,128)} fusion(bf16[4,768,1024]{2,1,0:T(8,128)(2,1)} %fusion, bf16[4,768,384]{2,1,0:T(8,128)(2,1)} %get-tuple-element.25), kind=kOutput, calls=%fused_computation.87 | convolution fusion | flops 2415919104 | bytes 14942208 | tf_op jit(solution)/shard_map/erd,erf->edf/dot_general | solution.py:35
  343.7 9.8 %fusion.1 = f32[4,768]{1,0:T(4,128)S(1)} fusion(f32[4,32,24,1024]{3,2,1,0:T(8,128)} %copy.69, bf16[4,768,384]{2,1,0:T(8,128)(2,1)} %get-tuple-element.25, bf16[4,1024,384]{2,1,0:T(8,128)(2,1)} %bitcast.114), kind=kOutput, calls=%fused_computation.10 | convolution fusion | flops 2422207488 | bytes 18100224 | tf_op jit(solution)/shard_map/erf,edf->erd/dot_general | solution.py:35
  353.6 0.7 all_to_all.33
  354.3 7.3 %all-to-all-start.5 = ((f32[32,1,96]{2,1,0:T(1,128)}), f32[32,1,96]{2,1,0:T(1,128)S(1)}, u32[]{:S(2)}, u32[]{:S(2)}) async-start(f32[32,1,96]{2,1,0:T(1,128)} %bitcast.30), calls=%async_computation.5 | async-start | bytes 32768 | tf_op jit(solution)/shard_map/all_to_all | solution.py:87
  361.7 8.3 %fusion.31 = f32[4,768,1024]{2,1,0:T(8,128)} fusion(bf16[4,768,384]{2,1,0:T(8,128)(2,1)S(1)} %copy-done.5, bf16[4,1024,384]{2,1,0:T(8,128)(2,1)} %bitcast.110), kind=kOutput, calls=%fused_computation.84 | convolution fusion | flops 2415919104 | bytes 18087936 | tf_op jit(solution)/shard_map/erf,edf->erd/dot_general | solution.py:35
  369.9 9.7 %add_convert_fusion = bf16[4,768,1024]{2,1,0:T(8,128)(2,1)S(1)} fusion(f32[4,768,1024]{2,1,0:T(8,128)} %fusion.31, bf16[4,768,384]{2,1,0:T(8,128)(2,1)} %copy-done.8, bf16[4,1024,384]{2,1,0:T(8,128)(2,1)} %bitcast.112), kind=kOutput, calls=%fused_computation.11 | convolution fusion | flops 2422210560 | bytes 24379392 | tf_op jit(solution)/shard_map/erf,edf->erd/dot_general | solution.py:35
  379.6 3.4 copy.72
  383.0 7.9 %all-to-all-start.4 = ((bf16[32,96,1024]{2,1,0:T(8,128)(2,1)}), bf16[32,96,1024]{2,1,0:T(8,128)(2,1)}, u32[]{:S(2)}, u32[]{:S(2)}) async-start(bf16[32,96,1024]{2,1,0:T(8,128)(2,1)} %bitcast.104), calls=%async_computation.4 | async-start | bytes 12582912 | tf_op jit(solution)/shard_map/all_to_all | solution.py:87
  390.9 10.0 %reduce-scatter.6.cloned.1.call-done = f32[4,128,384]{2,1,0:T(8,128)} async-done(((f32[4,1024,384]{2,1,0:T(8,128)}), f32[4,128,384]{2,1,0:T(8,128)}) %reduce-scatter.6.cloned.1.call-update) | async-done | bytes 786448 | tf_op jit(solution)/shard_map/reduce_scatter | solution.py:103
  400.9 1.2 copy.91
  402.1 75.2 %reduce-scatter.4.cloned.1.call-done = f32[4,128,384]{2,1,0:T(8,128)} async-done(((f32[4,1024,384]{2,1,0:T(8,128)}), f32[4,128,384]{2,1,0:T(8,128)}) %reduce-scatter.4.cloned.1.call-update) | async-done | bytes 786448 | tf_op jit(solution)/shard_map/reduce_scatter | solution.py:103
  477.2 1.2 copy.92
  478.4 75.0 %reduce-scatter.8.cloned.1.call-done = f32[4,128,384]{2,1,0:T(8,128)} async-done(((f32[4,1024,384]{2,1,0:T(8,128)}), f32[4,128,384]{2,1,0:T(8,128)}) %reduce-scatter.8.cloned.1.call-update) | async-done | bytes 786448 | tf_op jit(solution)/shard_map/reduce_scatter | solution.py:103
  553.4 1.2 copy.90
  554.6 1.6 pad_maximum_fusion
  556.2 4.0 all-to-all-start.6
  560.4 0.7 reduce.8
  561.1 11.8 %gather_fusion.1 = f32[2048]{0:T(1024)S(1)} fusion(f32[3072]{0:T(1024)S(1)} %reshape.175, s32[2048]{0:T(1024)S(1)} %broadcast_clamp_fusion), kind=kCustom, calls=%fused_computation.3 | custom fusion | bytes 24576 | tf_op jit(solution)/shard_map/jit(_take)/gather | solution.py:31
  573.8 14.6 %gather_fusion = bf16[2048,1024]{1,0:T(8,128)(2,1)} fusion(bf16[3072,1024]{1,0:T(8,128)(2,1)} %bitcast.27, s32[2048]{0:T(1024)S(1)} %broadcast_clamp_fusion), kind=kCustom, calls=%fused_computation.2 | custom fusion | bytes 8396800 | tf_op jit(solution)/shard_map/jit(_take)/gather | solution.py:31
  588.4 5.0 fusion.3
  593.4 1.5 fusion.28
  (72 shorter events, 5.8 us)
Async XLA Ops:
  7.2 48.8 %copy-start = (bf16[256,1024]{1,0:T(8,128)(2,1)S(1)}, bf16[256,1024]{1,0:T(8,128)(2,1)}, u32[]{:S(2)}) copy-start(bf16[256,1024]{1,0:T(8,128)(2,1)} %param.10) | copy-start | bytes 1572868
  7.2 21.2 %copy-start.11 = (s32[256,8]{0,1:T(8,128)S(1)}, s32[256,8]{0,1:T(8,128)}, u32[]{:S(2)}) copy-start(s32[256,8]{0,1:T(8,128)} %param.11) | copy-start | bytes 24580
  7.2 275.2 %all-gather.3.cloned.1.call-start = ((), (), s32[]{:S(2)}) async-start(), calls=%async_computation.13 | async-start | bytes 10616832 | tf_op jit(solution)/shard_map/all_gather | solution.py:75
  8.7 21.8 %copy-start.12 = (f32[256,8]{0,1:T(8,128)S(1)}, f32[256,8]{0,1:T(8,128)}, u32[]{:S(2)}) copy-start(f32[256,8]{0,1:T(8,128)} %param.12) | copy-start | bytes 24580
  28.8 0.7 copy-start.9
  40.2 53.9 %all-to-all-start = ((f32[32,1,96]{2,1,0:T(1,128)}), f32[32,1,96]{2,1,0:T(1,128)S(1)}, u32[]{:S(2)}, u32[]{:S(2)}) async-start(f32[32,1,96]{2,1,0:T(1,128)} %all_to_all.27), calls=%async_computation | async-start | bytes 32768 | tf_op jit(solution)/shard_map/all_to_all | solution.py:87
  55.9 13.9 %copy-start.2 = (bf16[256,1024]{1,0:T(8,128)(2,1)S(1)}, bf16[256,1024]{1,0:T(8,128)(2,1)}, u32[]{:S(2)}) copy-start(bf16[256,1024]{1,0:T(8,128)(2,1)} %param.9) | copy-start | bytes 1572868
  179.1 89.0 %all-to-all-start.3 = ((bf16[32,96,1024]{2,1,0:T(8,128)(2,1)}), bf16[32,96,1024]{2,1,0:T(8,128)(2,1)}, u32[]{:S(2)}, u32[]{:S(2)}) async-start(bf16[32,96,1024]{2,1,0:T(8,128)(2,1)} %bitcast.105), calls=%async_computation.3 | async-start | bytes 12582912 | tf_op jit(solution)/shard_map/all_to_all | solution.py:87
  186.6 214.3 %reduce-scatter.6.cloned.1.call-start = ((), (), s32[]{:S(2)}) async-start(), calls=%async_computation.11 | async-start | bytes 7077888 | tf_op jit(solution)/shard_map/reduce_scatter | solution.py:103
  282.4 19.9 %slice-start = ((s8[6291456]{0:T(1024)(128)(4,1)}), s8[2097152]{0:T(1024)(128)(4,1)S(1)}, s32[]{:S(2)}) async-start(s8[6291456]{0:T(1024)(128)(4,1)} %bitcast.98), calls=%async_computation.14 | async-start | bytes 4194304
  291.7 5.6 copy-start.3
  291.7 10.6 %slice-start.1 = ((s8[6291456]{0:T(1024)(128)(4,1)}), s8[4194304]{0:T(1024)(128)(4,1)S(1)}, s32[]{:S(2)}) async-start(s8[6291456]{0:T(1024)(128)(4,1)} %bitcast.98), calls=%async_computation.15 | async-start | bytes 8388608
  296.3 6.0 copy-start.7
  296.4 5.9 copy-start.4
  296.4 11.0 %copy-start.6 = (bf16[1,4,8,4,32,384]{5,4,3,2,1,0:T(8,128)(2,1)}, bf16[1,4,8,4,32,384]{5,4,3,2,1,0:T(8,128)(2,1)S(1)}, u32[]{:S(2)}) copy-start(bf16[1,4,8,4,32,384]{5,4,3,2,1,0:T(8,128)(2,1)S(1)} %get-tuple-element.28) | copy-start | bytes 9437188
  316.5 1.4 copy-start.8
  323.2 1.7 copy-start.5
  323.3 153.9 %reduce-scatter.4.cloned.1.call-start = ((), (), s32[]{:S(2)}) async-start(), calls=%async_computation.10 | async-start | bytes 7077888 | tf_op jit(solution)/shard_map/reduce_scatter | solution.py:103
  333.8 219.6 %reduce-scatter.8.cloned.1.call-start = ((), (), s32[]{:S(2)}) async-start(), calls=%async_computation.12 | async-start | bytes 7077888 | tf_op jit(solution)/shard_map/reduce_scatter | solution.py:103
  354.3 28.7 %all-to-all-start.5 = ((f32[32,1,96]{2,1,0:T(1,128)}), f32[32,1,96]{2,1,0:T(1,128)S(1)}, u32[]{:S(2)}, u32[]{:S(2)}) async-start(f32[32,1,96]{2,1,0:T(1,128)} %bitcast.30), calls=%async_computation.5 | async-start | bytes 32768 | tf_op jit(solution)/shard_map/all_to_all | solution.py:87
  383.0 173.2 %all-to-all-start.4 = ((bf16[32,96,1024]{2,1,0:T(8,128)(2,1)}), bf16[32,96,1024]{2,1,0:T(8,128)(2,1)}, u32[]{:S(2)}, u32[]{:S(2)}) async-start(bf16[32,96,1024]{2,1,0:T(8,128)(2,1)} %bitcast.104), calls=%async_computation.4 | async-start | bytes 12582912 | tf_op jit(solution)/shard_map/all_to_all | solution.py:87
  556.2 37.1 %all-to-all-start.6 = ((f32[4,3,4,32,384]{4,3,2,1,0:T(8,128)}), f32[4,3,4,32,384]{4,3,2,1,0:T(8,128)S(1)}, u32[]{:S(2)}, u32[]{:S(2)}) async-start(f32[4,3,4,32,384]{4,3,2,1,0:T(8,128)} %pad_maximum_fusion), calls=%async_computation.9 | async-start | bytes 4718592 | tf_op jit(solution)/shard_map/all_to_all | solution.py:107
  560.2 12.8 %copy-start.10 = (s32[256,8]{1,0:T(8,128)S(1)}, s32[256,8]{1,0:T(8,128)}, u32[]{:S(2)}) copy-start(s32[256,8]{1,0:T(8,128)} %copy-done.9) | copy-start | bytes 24580
  588.4 6.4 %copy-start.1 = (bf16[256,1024]{1,0:T(8,128)(2,1)S(1)}, bf16[256,1024]{1,0:T(8,128)(2,1)}, u32[]{:S(2)}) copy-start(bf16[256,1024]{1,0:T(8,128)(2,1)} %param.10) | copy-start | bytes 1572868
Sparse Core Ops, SparseCore 0:
  28.5 106.4 all-gather.2
  323.4 77.4 reduce-scatter.5
  403.4 73.7 reduce-scatter.3
  479.6 73.7 reduce-scatter.7

commit v2 on v1

v2 whole, which is shorter than its diff:
```python
import functools

import jax
import jax.numpy as jnp
from jax import lax
from jax.experimental import pallas as pl
from jax.experimental.pallas import tpu as pltpu
from jax.sharding import Mesh, PartitionSpec as P

NZ, NY, NX, NC = 8, 4, 4, 2
GROUP = NY * NX * NC
PLANE = ("y", "x", "core")
OWN = 4
F32, BF16 = jnp.float32, jnp.bfloat16
MESH = pl.DeviceIdType.MESH
ANY = pl.BlockSpec(memory_space=pl.ANY)
VMEM = pl.BlockSpec(memory_space=pltpu.VMEM)


def capacity_of(tok_dev, top_k, experts):
    return max(8, ((tok_dev * top_k * 5) // (4 * experts) + 7) // 8 * 8)


def dot(a, b, ca=1, cb=0):
    return lax.dot_general(a, b, (((ca,), (cb,)), ((), ())), preferred_element_type=F32)


def expert_base():
    ep = lax.axis_index("x") * NC + lax.axis_index("core")
    return ep * (NY * OWN) + lax.axis_index("y") * OWN


def strict_upper(n):
    rows = lax.broadcasted_iota(jnp.int32, (n, n), 0)
    cols = lax.broadcasted_iota(jnp.int32, (n, n), 1)
    return (rows < cols).astype(F32).astype(BF16)


RATE, D2D, HOP = 46600.0, 300000.0, 2.0


def gather_order(block_bytes, piece_bytes):
    free, heap, order, have = {}, [], [], {}

    def send(now, name, part, link, arrives, nbytes):
        rate = D2D if link == "core" else RATE
        t = max(now, free.get(link, 0.0)) + nbytes / rate
        free[link] = t
        if arrives is not None:
            heap.append((t + HOP, len(order), len(heap), arrives))
        return (name, part, link)

    def on_block(now, kind, dy, dx):
        out = []
        first, second = ("x", "y") if kind == "X" else ("y", "x")
        d = {"x": dx, "y": dy}

        def go(axis, sign, part):
            nd = dict(d)
            nd[axis] = (d[axis] - sign) % 4
            key = (kind, nd["y"], nd["x"])
            out.append(send(now, (kind, dy, dx), part, axis + ("+" if sign > 0 else "-"), key + (part,), block_bytes / (2 if part is not None else 1)))

        if d[second] == 0:
            if d[first] == 0:
                go(first, 1, None)
                go(first, -1, None)
            elif d[first] == 3:
                go(first, 1, 0)
            elif d[first] == 1:
                go(first, -1, 1)
            go(second, 1, None)
            go(second, -1, None)
        elif d[second] == 3:
            go(second, 1, 0)
        elif d[second] == 1:
            go(second, -1, 1)
        out.append(send(now, (kind, dy, dx), None, "core", None, block_bytes))
        return out

    def on_piece(now, dz, dy):
        out = []
        if dz == 0 or dz in (6, 7) or (dz == 5 and dy in (0, 1)):
            out.append(send(now, ("W", dz, dy), None, "z+", ("W", (dz - 1) % NZ, dy), piece_bytes))
        if dz == 0 or dz in (1, 2) or (dz == 3 and dy in (2, 3)):
            out.append(send(now, ("W", dz, dy), None, "z-", ("W", (dz + 1) % NZ, dy), piece_bytes))
        return out

    first = []
    for dy, link in ((1, "y+"), (3, "y-"), (2, "y+")):
        first.append(send(0.0, ("w", 0, dy), None, link, ("W", 0, (-dy) % 4), piece_bytes))
    first += on_piece(0.0, 0, 0)
    u = on_block(0.0, "U", 0, 0)
    x = on_block(0.0, "X", 0, 0)
    first += u + x
    order.append((None, first))
    while heap:
        now, _, _, name = heap.pop(heap.index(min(heap)))
        if name[0] == "W":
            order.append((name, on_piece(now, name[1], name[2])))
            continue
        kind, dy, dx, part = name
        key = (kind, dy, dx)
        have[key] = have.get(key, 0) + (2 if part is None else 1)
        order.append((name, on_block(now, kind, dy, dx) if have[key] == 2 else []))
    return order


def gather_kernel(order, x_ref, u_ref, meta_ref, w_ref, xa, ua, ma, wa, recv, wrecv, mrecv, drecv, ssem, msem, lsem):
    z, y, x, c = (lax.axis_index(a) for a in ("z", "y", "x", "core"))
    tok = x_ref.shape[0]
    half = tok // 2

    def place(dy, dx, dc=0):
        return lax.rem(y + dy, NY) * (NX * NC) + lax.rem(x + dx, NX) * NC + lax.rem(c + dc, NC)

    def at_offset(k):
        dy, dx, dc = k // (NX * NC), lax.rem(k // NC, NX), lax.rem(k, NC)
        return {"y": lax.rem(y + dy, NY), "x": lax.rem(x + dx, NX), "core": lax.rem(c + dc, NC)}

    me = place(0, 0)
    barrier = pltpu.get_barrier_semaphore()

    @pl.loop(1, GROUP)
    def _(k):
        pl.semaphore_signal(barrier, inc=1, device_id=at_offset(k), device_id_type=MESH)

    for dz in (1, NZ - 1):
        pl.semaphore_signal(barrier, inc=1, device_id={"z": lax.rem(z + dz, NZ)}, device_id_type=MESH)
    pl.semaphore_wait(barrier, GROUP + 1)

    def remote(src, dst, send_sem, recv_sem, target):
        return pltpu.make_async_remote_copy(src_ref=src, dst_ref=dst, send_sem=send_sem, recv_sem=recv_sem, device_id=target, device_id_type=MESH)

    targets = {
        "x+": {"x": lax.rem(x + 1, NX)}, "x-": {"x": lax.rem(x + NX - 1, NX)},
        "y+": {"y": lax.rem(y + 1, NY)}, "y-": {"y": lax.rem(y + NY - 1, NY)},
        "z+": {"z": lax.rem(z + 1, NZ)}, "z-": {"z": lax.rem(z + NZ - 1, NZ)},
        "core": {"core": 1 - c},
    }
    step = {"x+": (0, 3), "x-": (0, 1), "y+": (3, 0), "y-": (1, 0)}

    def block(kind, dy, dx, part=None):
        ref = (xa if kind == "X" else ua).at[place(dy, dx)]
        return ref if part is None else ref.at[pl.ds(part * half, half)]

    def bsem(kind, dy, dx, part):
        return recv.at[0 if kind == "X" else 1, dy * NX + dx, part or 0]

    copies = []

    def issue(name, part, link):
        sem = ssem.at[len(copies)]
        if name[0] == "w":
            dy = name[2]
            to = lax.rem(y + dy, NY)
            copy = remote(w_ref.at[to], wa.at[z, y], sem, wrecv.at[0, (-dy) % NY], {"y": to})
        elif name[0] == "W":
            _, dz, dy = name
            ndz = (dz - 1) % NZ if link == "z+" else (dz + 1) % NZ
            here = wa.at[lax.rem(z + dz, NZ), lax.rem(y + dy, NY)]
            src = w_ref.at[y] if (dz, dy) == (0, 0) else here
            copy = remote(src, here, sem, wrecv.at[ndz, dy], targets[link])
        else:
            kind, dy, dx = name
            if (dy, dx) == (0, 0):
                src = x_ref if kind == "X" else u_ref
                src = src if part is None else src.at[pl.ds(part * half, half)]
            else:
                src = block(kind, dy, dx, part)
            dst = block(kind, dy, dx, part)
            if link == "core":
                rsem = drecv.at[0 if kind == "X" else 1, dy * NX + dx]
            else:
                sy, sx = step[link]
                rsem = bsem(kind, (dy + sy) % NY, (dx + sx) % NX, part)
            copy = remote(src, dst, sem, rsem, targets[link])
        copy.start()
        copies.append(copy)

    local = [
        pltpu.make_async_copy(x_ref, xa.at[me], lsem.at[0]),
        pltpu.make_async_copy(u_ref, ua.at[me], lsem.at[1]),
        pltpu.make_async_copy(meta_ref, ma.at[me], lsem.at[2]),
        pltpu.make_async_copy(w_ref.at[y], wa.at[z, y], lsem.at[3]),
    ]

    def meta_copy(k):
        return remote(meta_ref, ma.at[me], msem.at[k], mrecv.at[k], at_offset(k))

    for name, sends in order:
        if name is None:
            pass
        elif name[0] == "W":
            _, dz, dy = name
            here = wa.at[lax.rem(z + dz, NZ), lax.rem(y + dy, NY)]
            remote(here, here, ssem.at[0], wrecv.at[dz, dy], targets["core"]).wait_recv()
        else:
            here = block(*name)
            remote(here, here, ssem.at[0], bsem(*name), targets["core"]).wait_recv()
        for send in sends:
            issue(*send)
        if name is None:
            for copy in local:
                copy.start()

            @pl.loop(1, GROUP)
            def _(k):
                meta_copy(k).start()

    for kind in (0, 1):
        for k in range(NY * NX):
            here = (ua if kind else xa).at[place(k // NX, k % NX, 1)]
            remote(here, here, ssem.at[0], drecv.at[kind, k], targets["core"]).wait_recv()

    @pl.loop(1, GROUP)
    def _(k):
        meta_copy(k).wait()

    for copy in copies:
        copy.wait_send()
    for copy in local:
        copy.wait()


def gather(x, u, meta, w):
    tok, hidden = x.shape
    order = gather_order(x.size * 2, w.size * 2 // NY)
    sends = sum(len(s) for _, s in order)
    dma = pltpu.SemaphoreType.DMA
    return pl.pallas_call(
        functools.partial(gather_kernel, order),
        name="gather",
        out_shape=(
            jax.ShapeDtypeStruct((GROUP, tok, hidden), BF16),
            jax.ShapeDtypeStruct((GROUP, tok, hidden), BF16),
            jax.ShapeDtypeStruct((GROUP,) + meta.shape, F32),
            jax.ShapeDtypeStruct((NZ,) + w.shape, BF16),
        ),
        in_specs=[VMEM] * 4,
        out_specs=(ANY,) * 4,
        scratch_shapes=[dma((2, NY * NX, 2)), dma((NZ, NY)), dma((GROUP,)), dma((2, NY * NX)), dma((sends,)), dma((GROUP,)), dma((4,))],
        compiler_params=pltpu.CompilerParams(collective_id=0, has_side_effects=True),
    )(x, u, meta, w)


def hits(ids, expert, values):
    return jnp.sum(jnp.where(ids == expert, values, 0.0), axis=0, keepdims=True)


def dispatch_kernel(cap, x_ref, u_ref, meta_ref, xr_ref, ur_ref, gr_ref, s_ref, tri_ref):
    tok, hidden = x_ref.shape[1:]
    rows = OWN * 2 * cap

    @pl.when(pl.program_id(0) == 0)
    def _():
        tri_ref[...] = strict_upper(tok)

    base = expert_base().astype(F32)
    r8 = lax.broadcasted_iota(jnp.int32, (8, tok), 0)
    r = lax.broadcasted_iota(jnp.int32, (rows, tok), 0)
    place = lax.rem(r, cap).astype(F32)
    e_of, p_of = r // (2 * cap), lax.rem(r // cap, 2)
    pick, gates = [], jnp.zeros((rows, tok), F32)
    for p in range(2):
        ids, gate = meta_ref[p, 0:8, :], meta_ref[p, 8:16, :]
        member = jnp.zeros((8, tok), F32)
        for e in range(OWN):
            member = jnp.where(r8 == e, hits(ids, base + e, 1.0), member)
        before = dot(member.astype(BF16), tri_ref[...])
        key = jnp.where(member > 0.0, before, -1.0)
        mine = jnp.full((rows, tok), -1.0, F32)
        for e in range(OWN):
            here = jnp.logical_and(e_of == e, p_of == p)
            mine = jnp.where(here, jnp.broadcast_to(key[e:e + 1, :], (rows, tok)), mine)
            gates = jnp.where(here, jnp.broadcast_to(hits(ids, base + e, gate), (rows, tok)), gates)
        pick.append((place == mine).astype(F32))
    both = pick[0] + pick[1]
    scale = jnp.sum(both * gates, axis=1, keepdims=True)
    s_ref[...] = both.astype(BF16).reshape(s_ref.shape)
    pick = jnp.concatenate(pick, axis=1).astype(BF16)
    xr_ref[...] = dot(pick, x_ref[...].reshape(2 * tok, hidden)).astype(BF16).reshape(xr_ref.shape)
    u_rows = dot(pick, u_ref[...].reshape(2 * tok, hidden))
    ur_ref[...] = u_rows.astype(BF16).reshape(ur_ref.shape)
    gr_ref[...] = (scale * u_rows).astype(BF16).reshape(gr_ref.shape)


def dispatch(cap, xa, ua, ma):
    _, tok, hidden = xa.shape
    rows = GROUP * cap
    out = lambda lanes: jax.ShapeDtypeStruct((OWN, rows, lanes), BF16)
    ospec = lambda lanes: pl.BlockSpec((OWN, 2 * cap, lanes), lambda i: (0, i, 0))
    ispec = lambda a: pl.BlockSpec((2,) + a.shape[1:], lambda i: (i, 0, 0))
    return pl.pallas_call(
        functools.partial(dispatch_kernel, cap),
        name="dispatch",
        out_shape=(out(hidden), out(hidden), out(hidden), out(tok)),
        grid=(GROUP // 2,),
        in_specs=[ispec(xa), ispec(ua), ispec(ma)],
        out_specs=(ospec(hidden), ospec(hidden), ospec(hidden), ospec(tok)),
        scratch_shapes=[pltpu.VMEM((tok, tok), BF16)],
        cost_estimate=pl.CostEstimate(flops=4 * OWN * rows * 2 * tok * hidden, bytes_accessed=4 * xa.size + 6 * OWN * rows * hidden, transcendentals=0),
    )(xa, ua, ma)


def expert_kernel(cap, x_ref, u_ref, g_ref, s_ref, w_ref, dx_ref, val_ref, g1_ref, g3_ref, g2_ref, a_s, d1_s, d3_s, y_s):
    rows, hidden = x_ref.shape[1:]
    ff = w_ref.shape[-1]
    tok = s_ref.shape[-1]
    w1 = w_ref[:, :, 0, 0].reshape(hidden, ff)
    w3 = w_ref[:, :, 1, 0].reshape(hidden, ff)
    w2 = w_ref[:, :, 2, 0].reshape(hidden, ff)
    tile = 256 if rows % 256 == 0 else rows

    @pl.loop(0, rows // tile)
    def _(i):
        at = pl.ds(pl.multiple_of(i * tile, tile), tile)
        x = x_ref[0, at, :]
        h1, h3 = dot(x, w1), dot(x, w3)
        sig = jax.nn.sigmoid(h1)
        silu = h1 * sig
        act = (silu * h3).astype(BF16)
        a_s[at, :] = act
        y = dot(act, w2, 1, 1)
        y_s[at, :] = jnp.sum(u_ref[0, at, :].astype(F32) * y, axis=1, keepdims=True)
        da = dot(g_ref[0, at, :], w2)
        d1 = (da * h3 * sig * (1.0 + h1 * (1.0 - sig))).astype(BF16)
        d3 = (da * silu).astype(BF16)
        d1_s[at, :] = d1
        d3_s[at, :] = d3
        dx_ref[0, at, :] = (dot(d1, w1, 1, 1) + dot(d3, w3, 1, 1)).astype(BF16)

    val = s_ref[0].astype(F32) * y_s[...]
    val_ref[0] = jnp.sum(val.reshape(rows // cap, cap, tok), axis=1)
    dtile = 256 if hidden % 256 == 0 else hidden

    @pl.loop(0, hidden // dtile)
    def _(i):
        at = pl.ds(pl.multiple_of(i * dtile, dtile), dtile)
        x = x_ref[0, :, at]
        g1_ref[0, at, :] = dot(x, d1_s[...], 0, 0)
        g3_ref[0, at, :] = dot(x, d3_s[...], 0, 0)
        g2_ref[0, at, :] = dot(g_ref[0, :, at], a_s[...], 0, 0)


def run_experts(cap, xr, ur, gr, s, wa):
    _, rows, hidden = xr.shape
    tok, ff = s.shape[-1], wa.shape[-1]
    row_spec = lambda lanes: pl.BlockSpec((1, rows, lanes), lambda e: (e, 0, 0))
    grad = jax.ShapeDtypeStruct((OWN, hidden, ff), F32)
    gspec = pl.BlockSpec((1, hidden, ff), lambda e: (e, 0, 0))
    wspec = pl.BlockSpec(wa.shape[:3] + (1,) + wa.shape[4:], lambda e: (0, 0, 0, e, 0, 0))
    return pl.pallas_call(
        functools.partial(expert_kernel, cap),
        name="experts",
        out_shape=(jax.ShapeDtypeStruct(xr.shape, BF16), jax.ShapeDtypeStruct((OWN, GROUP, tok), F32), grad, grad, grad),
        grid=(OWN,),
        in_specs=[row_spec(hidden), row_spec(hidden), row_spec(hidden), row_spec(tok), wspec],
        out_specs=(row_spec(hidden), pl.BlockSpec((1, GROUP, tok), lambda e: (e, 0, 0)), gspec, gspec, gspec),
        scratch_shapes=[pltpu.VMEM((rows, ff), BF16)] * 3 + [pltpu.VMEM((rows, 1), F32)],
        cost_estimate=pl.CostEstimate(flops=18 * OWN * rows * hidden * ff, bytes_accessed=8 * xr.size + 2 * wa.size + 12 * OWN * hidden * ff, transcendentals=0),
        compiler_params=pltpu.CompilerParams(vmem_limit_bytes=60 << 20),
    )(xr, ur, gr, s, wa)


def combine_kernel(cap, dx_ref, val_ref, meta_ref, out_ref, gate_ref, key_s, s_s, acc_s):
    group, places, hidden = dx_ref.shape
    tok = meta_ref.shape[1]
    ids = meta_ref[0:8, :]
    r = lax.broadcasted_iota(jnp.int32, (group * 8, tok), 0)
    d, e = r // 8, lax.rem(r, 8)
    expert = lax.rem(d, NX * NC) * (NY * OWN) + d // (NX * NC) * OWN + e
    expert = jnp.where(e < OWN, expert, -1).astype(F32)
    member = jnp.zeros((group * 8, tok), F32)
    for j in range(8):
        member = member + (jnp.broadcast_to(ids[j:j + 1, :], member.shape) == expert).astype(F32)
    before = dot(member.astype(BF16), strict_upper(tok))
    key_s[...] = jnp.where(member > 0.0, before, -1.0).reshape(key_s.shape)
    rr = lax.broadcasted_iota(jnp.int32, (places, tok), 0)
    place, e_of = lax.rem(rr, cap).astype(F32), rr // cap
    some = 8
    acc_s[...] = jnp.zeros_like(acc_s)

    @pl.loop(0, group // some)
    def _(i):
        @pl.loop(0, some)
        def _(k):
            key = key_s[i * some + k]
            mine = jnp.full((places, tok), -1.0, F32)
            for e in range(OWN):
                mine = jnp.where(e_of == e, jnp.broadcast_to(key[e:e + 1, :], (places, tok)), mine)
            s_s[pl.ds(pl.multiple_of(k * places, places), places), :] = (place == mine).astype(F32).astype(BF16)

        acc_s[...] += dot(s_s[...], dx_ref[pl.ds(i * some, some)].reshape(some * places, hidden), 0, 0)

    out_ref[...] = acc_s[...].astype(BF16)

    def gate_step(k, total):
        for e in range(OWN):
            number = lax.rem(k, NX * NC) * (NY * OWN) + k // (NX * NC) * OWN + e
            row = val_ref[k, e:e + 1, :]
            total = total + jnp.where(ids == number.astype(F32), jnp.broadcast_to(row, ids.shape), 0.0)
        return total

    gate_ref[...] = lax.fori_loop(0, group, gate_step, jnp.zeros((8, tok), F32))


def combine(cap, dx_back, val_back, meta):
    group, places, hidden = dx_back.shape
    tok = meta.shape[1]
    return pl.pallas_call(
        functools.partial(combine_kernel, cap),
        name="combine",
        out_shape=(jax.ShapeDtypeStruct((tok, hidden), BF16), jax.ShapeDtypeStruct((8, tok), F32)),
        in_specs=[VMEM] * 3,
        out_specs=(VMEM, VMEM),
        scratch_shapes=[pltpu.VMEM((group, 8, tok), F32), pltpu.VMEM((8 * places, tok), BF16), pltpu.VMEM((tok, hidden), F32)],
        cost_estimate=pl.CostEstimate(flops=2 * group * places * tok * hidden, bytes_accessed=2 * dx_back.size, transcendentals=0),
    )(dx_back, val_back, meta)


def solution(mesh):
    mesh4 = Mesh(mesh.devices.reshape(NZ, NY, NX, NC), ("z", "y", "x", "core"))
    tok_spec = P(("z", "y", "x", "core"), None)
    up_spec = P(("x", "core"), ("z", "y"), None)
    down_spec = P(("x", "core"), None, ("z", "y"))

    def per_device(layer_in, out_grad, expert_ids, gate_vals, w_one, w_two, w_three):
        tok_dev, hidden = layer_in.shape
        top_k = expert_ids.shape[1]
        local_experts, d_loc, ff = w_one.shape
        cap = capacity_of(tok_dev, top_k, local_experts * NX * NC)
        w = jnp.stack([w_one, w_three, w_two.swapaxes(1, 2)]).reshape(3, NY, OWN, d_loc, ff).swapaxes(0, 1)
        meta = jnp.concatenate([expert_ids.T.astype(F32), gate_vals.T])
        xa, ua, ma, wa = gather(layer_in, out_grad, meta, w)
        xr, ur, gr, s = dispatch(cap, xa, ua, ma)
        dx, val, g1, g3, g2 = run_experts(cap, xr, ur, gr, s, wa)

        def home(grad):
            grad = lax.psum_scatter(grad, "z", scatter_dimension=1, tiled=True)
            return grad.reshape(OWN, NY, d_loc, ff).swapaxes(0, 1)

        grads = jnp.stack([home(g1), home(g3), home(g2)], axis=1)
        grads = lax.all_to_all(grads, "y", 0, 0, tiled=True)

        dx = dx.reshape(OWN, GROUP, cap, hidden).swapaxes(0, 1).reshape(GROUP, OWN * cap, hidden)
        dx_back = lax.all_to_all(dx, PLANE, 0, 0, tiled=True)
        val_back = lax.all_to_all(val.swapaxes(0, 1), PLANE, 0, 0, tiled=True)
        in_grad, gate_out = combine(cap, dx_back, val_back, meta)

        grads = grads.swapaxes(0, 1).reshape(3, local_experts, d_loc, ff)
        return in_grad, gate_out.T, grads[0], grads[2].swapaxes(1, 2), grads[1]

    return jax.shard_map(per_device, mesh=mesh4, in_specs=(tok_spec, tok_spec, tok_spec, tok_spec, up_spec, down_spec, up_spec), out_specs=(tok_spec, tok_spec, up_spec, down_spec, up_spec), check_vma=False)
```

time: 608 us -> 474 us (0.78)
  Pallas kernels: 0 us -> 200 us
  local copies, waits for them, and re-layouts: 120 us -> 13.1 us
  blocking collectives: 105 us -> 0 us
  matrix products: 70.8 us -> 0 us
  other arithmetic: 37.9 us -> 6.11 us
  starting transfers between devices: 35.2 us -> 16.9 us
    pallas_call x0 -> x4, Pallas kernels: none -> 200 us  [the longest x1 120 us: gather(): pl.pallas_call(functools.partial(gather_kernel, order), name='gather', ou...]
    all_to_all x2 -> x0, blocking collectives: 105 us -> none  [the longest x1 85 us: exchange(): return lax.all_to_all(v, PLANE, 0, 0, tiled=True)]
    dot_general x9 -> x0, matrix products: 70.8 us -> none  [dot(): return jnp.einsum(spec, a, b, preferred_element_type=jnp.float32)]
    all_to_all x4 -> x2, waiting for transfers between devices: 58.8 us -> 0.89 us  [the longest x1 0.88 us: per_device(): val_back = lax.all_to_all(val.swapaxes(0, 1), PLANE, 0, 0, tiled=True)]
    gather x5 -> x0, local copies, waits for them, and re-layouts: 54.3 us -> none  [take_rows(): return jnp.take(rows, row_index, axis=0, mode='fill', fill_value=0)]
    reduce_scatter x3, waiting for transfers between devices: 160 us -> 200 us  [home(): grad = lax.psum_scatter(grad, 'z', scatter_dimension=1, tiled=True)]
    all_to_all x1, waiting for transfers between devices: 0.01 us -> 19.6 us  [per_device(): grads = lax.all_to_all(grads, 'y', 0, 0, tiled=True)]
    all_to_all x4 -> x2, starting transfers between devices: 30.3 us -> 12.7 us  [the longest x1 6.55 us: per_device(): dx_back = lax.all_to_all(dx, PLANE, 0, 0, tiled=True)]
  transfers between devices with their start and end apart: 9 -> 6, of which waited for: 4 -> 5; matrix products, arithmetic and copies ran while one was open for 30% -> 3% of each run, Pallas kernels for 0% -> 2%
where the time goes in v2:
time: 474 us; the launch traced here: 473 us
  waiting for transfers between devices  222 us (47%)
  Pallas kernels  200 us (42%)
  starting transfers between devices  16.9 us (4%)
  between operations  13.8 us (3%)
  local copies, waits for them, and re-layouts  13.1 us (3%)
  other arithmetic  6.11 us (1%)
    reduce_scatter x3, waiting for transfers between devices, home(): grad = lax.psum_scatter(grad, 'z', scatter_dimension=1, tiled=True)  200 us
    pallas_call x1, Pallas kernels, gather(): pl.pallas_call(functools.partial(gather_kernel, order), name='gather', ou...  120 us
    pallas_call x1, Pallas kernels, run_experts(): pl.pallas_call(functools.partial(expert_kernel, cap), name='experts', out...  45.2 us
    pallas_call x1, Pallas kernels, dispatch(): pl.pallas_call(functools.partial(dispatch_kernel, cap), name='dispatch',...  27.4 us
    all_to_all x1, waiting for transfers between devices, per_device(): grads = lax.all_to_all(grads, 'y', 0, 0, tiled=True)  19.6 us
  transfers between devices with their start and end apart: 6, of which 5 were waited for; matrix products, arithmetic and copies ran while one was open for 3% of the time, Pallas kernels for 2%

profile of v2, /device:TPU:1, one launch (start us, length us, event | category | flops | bytes accessed | tf_op | source)
XLA Modules:
  0.0 472.5 jit_solution(876212804132196963)
XLA Ops:
  7.2 0.0 reduce-scatter.4.cloned.1.call-start
  7.2 0.7 convert_bitcast_fusion
  7.9 1.3 pad_maximum_fusion.1.meta_ref
  9.2 2.5 maximum_bitcast_fusion.w_ref
  11.7 119.7 %gather.1 = (bf16[32,256,1024]{2,1,0:T(8,128)(2,1)}, bf16[32,256,1024]{2,1,0:T(8,128)(2,1)}, f32[32,16,256]{2,1,0:T(8,128)}, bf16[8,4,3,4,32,384]{5,4,3,2,1,0:T(8,128)(2,1)}) custom-call(bf16[256,1024]{1,0:T(8,128)(2,1)} %x_ref.1, bf16[256,1024]{1,0:T(8,128)(2,1)} %u_ref.1, f32[16,256]{1,0:T(8,128)} %pad_maximum_fusion.1.meta_ref, ...), custom_call_target="tpu_custom_call" | custom-call | tf_op jit(solution)/shard_map/gather/pallas_call | solution.py:231
  131.4 27.4 %dispatch.1 = (bf16[4,768,1024]{2,1,0:T(8,128)(2,1)}, bf16[4,768,1024]{2,1,0:T(8,128)(2,1)}, bf16[4,768,1024]{2,1,0:T(8,128)(2,1)}, bf16[4,768,256]{2,1,0:T(8,128)(2,1)}) custom-call(bf16[32,256,1024]{2,1,0:T(8,128)(2,1)} %get-tuple-element.20.x_ref, bf16[32,256,1024]{2,1,0:T(8,128)(2,1)} %get-tuple-element.21.u_ref, f32[32,16,256]{2,1,0:T(8,128)} %get-tuple-element.22.meta_ref), custom_call_target="tpu_custom_call" | custom-call | flops 6442450944 | bytes 52428800 | tf_op jit(solution)/shard_map/dispatch/pallas_call | solution.py:294
  158.8 45.2 %experts.1 = (bf16[4,768,1024]{2,1,0:T(8,128)(2,1)}, f32[4,32,256]{2,1,0:T(8,128)}, f32[4,1024,384]{2,1,0:T(8,128)}, f32[4,1024,384]{2,1,0:T(8,128)}, f32[4,1024,384]{2,1,0:T(8,128)}) custom-call(bf16[4,768,1024]{2,1,0:T(8,128)(2,1)} %get-tuple-element.23.x_ref, bf16[4,768,1024]{2,1,0:T(8,128)(2,1)} %get-tuple-element.24.u_ref, ...), custom_call_target="tpu_custom_call" | custom-call | flops 21743271936 | bytes 53477376 | tf_op jit(solution)/shard_map/experts/pallas_call | solution.py:353
  204.0 0.0 reduce-scatter.4.cloned.1.call-update
  204.0 0.0 reduce-scatter.6.cloned.1.call-start
  204.1 0.7 reduce-scatter.6.cloned.1.call-update
  204.8 0.0 reduce-scatter.8.cloned.1.call-start
  204.8 0.0 copy-start.1
  204.8 0.7 reduce-scatter.8.cloned.1.call-update
  205.5 0.2 copy-done.1
  205.7 0.7 copy.29
  206.5 6.2 %all-to-all-start.1 = ((f32[32,4,256]{2,1,0:T(4,128)}), f32[32,4,256]{2,1,0:T(4,128)S(1)}, u32[]{:S(2)}, u32[]{:S(2)}) async-start(f32[32,4,256]{2,1,0:T(4,128)} %bitcast.41), calls=%async_computation.1 | async-start | bytes 262144 | tf_op jit(solution)/shard_map/all_to_all | solution.py:448
  212.7 6.5 %copy.17 = bf16[4,32,24,1024]{3,2,0,1:T(8,128)(2,1)} copy(bf16[4,32,24,1024]{3,2,1,0:T(8,128)(2,1)} %bitcast.44) | data formatting | bytes 12582912 | tf_op jit(solution)/shard_map/reshape | solution.py:446
  219.2 0.9 all-to-all-done.1.val_ref
  220.1 0.0 copy-start
  220.1 0.7 copy-done
  220.7 6.5 %all-to-all-start = ((bf16[32,96,1024]{2,1,0:T(8,128)(2,1)}), bf16[32,96,1024]{2,1,0:T(8,128)(2,1)}, u32[]{:S(2)}, u32[]{:S(2)}) async-start(bf16[32,96,1024]{2,1,0:T(8,128)(2,1)} %bitcast.42), calls=%async_computation | async-start | bytes 12582912 | tf_op jit(solution)/shard_map/all_to_all | solution.py:447
  227.3 50.0 %reduce-scatter.4.cloned.1.call-done = f32[4,128,384]{2,1,0:T(8,128)} async-done(((f32[4,1024,384]{2,1,0:T(8,128)}), f32[4,128,384]{2,1,0:T(8,128)}) %reduce-scatter.4.cloned.1.call-update) | async-done | bytes 786448 | tf_op jit(solution)/shard_map/reduce_scatter | solution.py:440
  277.2 1.2 copy.28
  278.4 75.2 %reduce-scatter.6.cloned.1.call-done = f32[4,128,384]{2,1,0:T(8,128)} async-done(((f32[4,1024,384]{2,1,0:T(8,128)}), f32[4,128,384]{2,1,0:T(8,128)}) %reduce-scatter.6.cloned.1.call-update) | async-done | bytes 786448 | tf_op jit(solution)/shard_map/reduce_scatter | solution.py:440
  353.6 1.2 copy.27
  354.8 75.1 %reduce-scatter.8.cloned.1.call-done = f32[4,128,384]{2,1,0:T(8,128)} async-done(((f32[4,1024,384]{2,1,0:T(8,128)}), f32[4,128,384]{2,1,0:T(8,128)}) %reduce-scatter.8.cloned.1.call-update) | async-done | bytes 786448 | tf_op jit(solution)/shard_map/reduce_scatter | solution.py:440
  429.9 1.2 copy.26
  431.1 1.6 pad_maximum_fusion
  432.7 0.0 all-to-all-done.dx_ref
  432.7 4.0 all-to-all-start.2
  436.8 8.2 %combine.1 = (bf16[256,1024]{1,0:T(8,128)(2,1)}, f32[8,256]{1,0:T(8,128)}) custom-call(bf16[32,96,1024]{2,1,0:T(8,128)(2,1)} %all-to-all-done.dx_ref, f32[32,4,256]{2,1,0:T(4,128)} %copy-done, f32[16,256]{1,0:T(8,128)} %pad_maximum_fusion.1.meta_ref), custom_call_target="tpu_custom_call" | custom-call | flops 1610612736 | bytes 6291456 | tf_op jit(solution)/shard_map/combine/pallas_call | solution.py:411
  444.9 19.6 %all-to-all-done.2 = f32[4,3,4,32,384]{4,3,2,1,0:T(8,128)S(1)} async-done(((f32[4,3,4,32,384]{4,3,2,1,0:T(8,128)}), f32[4,3,4,32,384]{4,3,2,1,0:T(8,128)S(1)}, u32[]{:S(2)}, u32[]{:S(2)}) %all-to-all-start.2) | async-done | bytes 2359328 | tf_op jit(solution)/shard_map/all_to_all | solution.py:444
  464.6 1.5 fusion
Async XLA Ops:
  7.2 270.1 %reduce-scatter.4.cloned.1.call-start = ((), (), s32[]{:S(2)}) async-start(), calls=%async_computation.6 | async-start | bytes 7077888 | tf_op jit(solution)/shard_map/reduce_scatter | solution.py:440
  204.0 149.6 %reduce-scatter.6.cloned.1.call-start = ((), (), s32[]{:S(2)}) async-start(), calls=%async_computation.7 | async-start | bytes 7077888 | tf_op jit(solution)/shard_map/reduce_scatter | solution.py:440
  204.8 225.1 %reduce-scatter.8.cloned.1.call-start = ((), (), s32[]{:S(2)}) async-start(), calls=%async_computation.8 | async-start | bytes 7077888 | tf_op jit(solution)/shard_map/reduce_scatter | solution.py:440
  204.8 0.9 copy-start.1
  206.5 13.6 %all-to-all-start.1 = ((f32[32,4,256]{2,1,0:T(4,128)}), f32[32,4,256]{2,1,0:T(4,128)S(1)}, u32[]{:S(2)}, u32[]{:S(2)}) async-start(f32[32,4,256]{2,1,0:T(4,128)} %bitcast.41), calls=%async_computation.1 | async-start | bytes 262144 | tf_op jit(solution)/shard_map/all_to_all | solution.py:448
  220.1 0.7 copy-start
  220.7 212.0 %all-to-all-start = ((bf16[32,96,1024]{2,1,0:T(8,128)(2,1)}), bf16[32,96,1024]{2,1,0:T(8,128)(2,1)}, u32[]{:S(2)}, u32[]{:S(2)}) async-start(bf16[32,96,1024]{2,1,0:T(8,128)(2,1)} %bitcast.42), calls=%async_computation | async-start | bytes 12582912 | tf_op jit(solution)/shard_map/all_to_all | solution.py:447
  432.7 31.8 %all-to-all-start.2 = ((f32[4,3,4,32,384]{4,3,2,1,0:T(8,128)}), f32[4,3,4,32,384]{4,3,2,1,0:T(8,128)S(1)}, u32[]{:S(2)}, u32[]{:S(2)}) async-start(f32[4,3,4,32,384]{4,3,2,1,0:T(8,128)} %pad_maximum_fusion), calls=%async_computation.5 | async-start | bytes 4718592 | tf_op jit(solution)/shard_map/all_to_all | solution.py:444
Sparse Core Ops, SparseCore 0:
  204.1 73.0 reduce-scatter.3
  279.8 73.7 reduce-scatter.5
  356.1 73.7 reduce-scatter.7

commit v3 on v2

--- a/solution.py
+++ b/solution.py
@@ -303,120 +303,306 @@
     )(xa, ua, ma)
 
 
-def expert_kernel(cap, x_ref, u_ref, g_ref, s_ref, w_ref, dx_ref, val_ref, g1_ref, g3_ref, g2_ref, a_s, d1_s, d3_s, y_s):
-    rows, hidden = x_ref.shape[1:]
-    ff = w_ref.shape[-1]
-    tok = s_ref.shape[-1]
-    w1 = w_ref[:, :, 0, 0].reshape(hidden, ff)
-    w3 = w_ref[:, :, 1, 0].reshape(hidden, ff)
-    w2 = w_ref[:, :, 2, 0].reshape(hidden, ff)
+FAR, SUM3, NEW3, TWO, ONE = range(5)
+
+
+def expert_kernel(cap, xr, ur, gr, sel, wa, meta_ref, grads, in_grad_ref, gate_ref, dxb, valb, dxs,
+                  xb, ub, gb, sb, wb, a_s, d1_s, d3_s, y_s, dx_s, val_s, vb, key_s, acc_s, G, r4, r3, r2, r1,
+                  lsem, wsem, rsend, rrecv, ysend, yrecv, dsend, drecv, vsem, osem):
+    z, y, x, c = (lax.axis_index(a) for a in ("z", "y", "x", "core"))
+    rows, hidden = xb.shape
+    ff, tok = a_s.shape[-1], sb.shape[-1]
+    d_loc = hidden // (NZ * NY)
+    me = y * (NX * NC) + x * NC + c
+
+    def at_offset(k):
+        dy, dx, dc = k // (NX * NC), lax.rem(k // NC, NX), lax.rem(k, NC)
+        return {"y": lax.rem(y + dy, NY), "x": lax.rem(x + dx, NX), "core": lax.rem(c + dc, NC)}
+
+    def place_of(d):
+        return d["y"] * (NX * NC) + d["x"] * NC + d["core"]
+
+    def remote(src, dst, send_sem, recv_sem, target):
+        return pltpu.make_async_remote_copy(src_ref=src, dst_ref=dst, send_sem=send_sem, recv_sem=recv_sem, device_id=target, device_id_type=MESH)
+
+    def row_copies(e):
+        pairs = ((xr, xb), (gr, gb), (ur, ub), (sel, sb))
+        return [pltpu.make_async_copy(src.at[e], dst, lsem.at[i]) for i, (src, dst) in enumerate(pairs)]
+
+    def weight_copies(e, slot):
+        return [pltpu.make_async_copy(wa.at[:, :, m, e], wb.at[slot, m], wsem.at[slot, m]) for m in range(3)]
+
+    for copy in weight_copies(0, 0) + row_copies(0):
+        copy.start()
+
+    barrier = pltpu.get_barrier_semaphore()
+
+    @pl.loop(1, GROUP)
+    def _(k):
+        pl.semaphore_signal(barrier, inc=1, device_id=at_offset(k), device_id_type=MESH)
+
+    for dz in (1, NZ - 1):
+        pl.semaphore_signal(barrier, inc=1, device_id={"z": lax.rem(z + dz, NZ)}, device_id_type=MESH)
+    pl.semaphore_wait(barrier, GROUP + 1)
+
+    def chunk(e, way, dist):
+        return G.at[e, lax.rem(z + (dist if way else NZ - dist), NZ)]
+
+    def hop(e, way, kind):
+        h = way
+        src, dst = {
+            FAR: lambda: (chunk(e, way, 4).at[h], r4.at[way, e]),
+            SUM3: lambda: (r4.at[way, e], r3.at[way, e, h]),
+            NEW3: lambda: (chunk(e, way, 3).at[1 - h], r3.at[way, e, 1 - h]),
+            TWO: lambda: (r3.at[way, e], r2.at[way, e]),
+            ONE: lambda: (r2.at[way, e], r1.at[way, e]),
+        }[kind]()
+        to = lax.rem(z + (1 if way else NZ - 1), NZ)
+        return remote(src, dst, rsend.at[way, e, kind], rrecv.at[way, e, kind], {"z": to})
+
+    def add_into(dst, *others):
+        parts = dst.shape[:-2]
+
+        def flat(ref, i):
+            index = []
+            for n in reversed(parts):
+                index.append(lax.rem(i, n))
+                i = i // n
+            return ref.at[tuple(reversed(index))]
+
+        n = 1
+        for p in parts:
+            n *= p
+
+        @pl.loop(0, n)
+        def _(i):
+            total = flat(dst, i)[...]
+            for other in others:
+                total = total + flat(other, i)[...]
+            flat(dst, i)[...] = total
+
+    def dx_copy(e, k):
+        to = at_offset(k)
+        src = dxs.at[e, pl.ds(pl.multiple_of(place_of(to) * cap, 8), cap)]
+        return remote(src, dxb.at[me, pl.ds(pl.multiple_of(e * cap, 8), cap)], dsend.at[e], drecv.at[e], to)
+
+    def own_dx_copy(e):
+        src = dxs.at[e, pl.ds(pl.multiple_of(me * cap, 8), cap)]
+        return pltpu.make_async_copy(src, dxb.at[me, pl.ds(pl.multiple_of(e * cap, 8), cap)], drecv.at[e])
+
     tile = 256 if rows % 256 == 0 else rows
-
-    @pl.loop(0, rows // tile)
-    def _(i):
-        at = pl.ds(pl.multiple_of(i * tile, tile), tile)
-        x = x_ref[0, at, :]
-        h1, h3 = dot(x, w1), dot(x, w3)
-        sig = jax.nn.sigmoid(h1)
-        silu = h1 * sig
-        act = (silu * h3).astype(BF16)
-        a_s[at, :] = act
-        y = dot(act, w2, 1, 1)
-        y_s[at, :] = jnp.sum(u_ref[0, at, :].astype(F32) * y, axis=1, keepdims=True)
-        da = dot(g_ref[0, at, :], w2)
-        d1 = (da * h3 * sig * (1.0 + h1 * (1.0 - sig))).astype(BF16)
-        d3 = (da * silu).astype(BF16)
-        d1_s[at, :] = d1
-        d3_s[at, :] = d3
-        dx_ref[0, at, :] = (dot(d1, w1, 1, 1) + dot(d3, w3, 1, 1)).astype(BF16)
-
-    val = s_ref[0].astype(F32) * y_s[...]
-    val_ref[0] = jnp.sum(val.reshape(rows // cap, cap, tok), axis=1)
-    dtile = 256 if hidden % 256 == 0 else hidden
-
-    @pl.loop(0, hidden // dtile)
-    def _(i):
-        at = pl.ds(pl.multiple_of(i * dtile, dtile), dtile)
-        x = x_ref[0, :, at]
-        g1_ref[0, at, :] = dot(x, d1_s[...], 0, 0)
-        g3_ref[0, at, :] = dot(x, d3_s[...], 0, 0)
-        g2_ref[0, at, :] = dot(g_ref[0, :, at], a_s[...], 0, 0)
-
-
-def run_experts(cap, xr, ur, gr, s, wa):
-    _, rows, hidden = xr.shape
-    tok, ff = s.shape[-1], wa.shape[-1]
-    row_spec = lambda lanes: pl.BlockSpec((1, rows, lanes), lambda e: (e, 0, 0))
-    grad = jax.ShapeDtypeStruct((OWN, hidden, ff), F32)
-    gspec = pl.BlockSpec((1, hidden, ff), lambda e: (e, 0, 0))
-    wspec = pl.BlockSpec(wa.shape[:3] + (1,) + wa.shape[4:], lambda e: (0, 0, 0, e, 0, 0))
-    return pl.pallas_call(
-        functools.partial(expert_kernel, cap),
-        name="experts",
-        out_shape=(jax.ShapeDtypeStruct(xr.shape, BF16), jax.ShapeDtypeStruct((OWN, GROUP, tok), F32), grad, grad, grad),
-        grid=(OWN,),
-        in_specs=[row_spec(hidden), row_spec(hidden), row_spec(hidden), row_spec(tok), wspec],
-        out_specs=(row_spec(hidden), pl.BlockSpec((1, GROUP, tok), lambda e: (e, 0, 0)), gspec, gspec, gspec),
-        scratch_shapes=[pltpu.VMEM((rows, ff), BF16)] * 3 + [pltpu.VMEM((rows, 1), F32)],
-        cost_estimate=pl.CostEstimate(flops=18 * OWN * rows * hidden * ff, bytes_accessed=8 * xr.size + 2 * wa.size + 12 * OWN * hidden * ff, transcendentals=0),
-        compiler_params=pltpu.CompilerParams(vmem_limit_bytes=60 << 20),
-    )(xr, ur, gr, s, wa)
-
-
-def combine_kernel(cap, dx_ref, val_ref, meta_ref, out_ref, gate_ref, key_s, s_s, acc_s):
-    group, places, hidden = dx_ref.shape
-    tok = meta_ref.shape[1]
+    dtile = 2 * hidden // NZ
+    half = hidden // NZ // 2
+
+    @pl.loop(0, OWN)
+    def _(e):
+        slot = lax.rem(e, 2)
+        for copy in weight_copies(e, slot) + row_copies(e):
+            copy.wait()
+
+        @pl.when(e < OWN - 1)
+        def _():
+            for copy in weight_copies(e + 1, 1 - slot):
+                copy.start()
+
+        def w(m):
+            return wb[slot, m].reshape(hidden, ff)
+
+        @pl.loop(0, rows // tile)
+        def _(i):
+            at = pl.ds(pl.multiple_of(i * tile, tile), tile)
+            x_rows = xb[at, :]
+            h1, h3 = dot(x_rows, w(0)), dot(x_rows, w(1))
+            sig = jax.nn.sigmoid(h1)
+            silu = h1 * sig
+            act = (silu * h3).astype(BF16)
+            a_s[at, :] = act
+            y_rows = dot(act, w(2), 1, 1)
+            y_s[at, :] = jnp.sum(ub[at, :].astype(F32) * y_rows, axis=1, keepdims=True)
+            da = dot(gb[at, :], w(2))
+            d1 = (da * h3 * sig * (1.0 + h1 * (1.0 - sig))).astype(BF16)
+            d3 = (da * silu).astype(BF16)
+            d1_s[at, :] = d1
+            d3_s[at, :] = d3
+            dx_s[at, :] = (dot(d1, w(0), 1, 1) + dot(d3, w(1), 1, 1)).astype(BF16)
+
+        out = pltpu.make_async_copy(dx_s, dxs.at[e], osem.at[0])
+        out.start()
+
+        @pl.loop(0, NZ // 2)
+        def _(i):
+            at = pl.ds(pl.multiple_of(i * dtile, dtile), dtile)
+            x_cols, g_cols = xb[:, at], gb[:, at]
+            for m, part in enumerate((dot(x_cols, d1_s[...], 0, 0), dot(x_cols, d3_s[...], 0, 0), dot(g_cols, a_s[...], 0, 0))):
+                for j in range(4):
+                    G[e, 2 * i + j // 2, j % 2, m] = part[j * half:(j + 1) * half]
+
+        for way in (0, 1):
+            for kind in (FAR, NEW3):
+                hop(e, way, kind).start()
+        val = sb[...].astype(F32) * y_s[...]
+        val_s[e] = jnp.sum(val.reshape(rows // cap, cap, tok), axis=1)
+        out.wait()
+
+        @pl.when(e < OWN - 1)
+        def _():
+            for copy in row_copies(e + 1):
+                copy.start()
+
+        own_dx_copy(e).start()
+
+        @pl.loop(1, GROUP)
+        def _(k):
+            dx_copy(e, k).start()
+
+    def val_copy(k):
+        to = at_offset(k)
+        return remote(val_s.at[:, place_of(to)], valb.at[:, me], vsem.at[0, k], vsem.at[1, k], to)
+
+    own_val = pltpu.make_async_copy(val_s.at[:, me], valb.at[:, me], vsem.at[0, 0])
+    own_val.start()
+
+    @pl.loop(1, GROUP)
+    def _(k):
+        val_copy(k).start()
+
+    def step(arrived, dist, leaves):
+        @pl.loop(0, OWN)
+        def _(e):
+            for way in (0, 1):
+                for kind in arrived:
+                    hop(e, way, kind).wait_recv()
+                if leaves == SUM3:
+                    add_into(r4.at[way, e], chunk(e, way, dist).at[way])
+                else:
+                    add_into((r3 if leaves == TWO else r2).at[way, e], chunk(e, way, dist))
+                hop(e, way, leaves).start()
+
+    step((FAR,), 3, SUM3)
+    step((SUM3, NEW3), 2, TWO)
+
+    group, places = dxb.shape[:2]
     ids = meta_ref[0:8, :]
     r = lax.broadcasted_iota(jnp.int32, (group * 8, tok), 0)
-    d, e = r // 8, lax.rem(r, 8)
-    expert = lax.rem(d, NX * NC) * (NY * OWN) + d // (NX * NC) * OWN + e
-    expert = jnp.where(e < OWN, expert, -1).astype(F32)
+    d_of, e_of = r // 8, lax.rem(r, 8)
+    expert = lax.rem(d_of, NX * NC) * (NY * OWN) + d_of // (NX * NC) * OWN + e_of
+    expert = jnp.where(e_of < OWN, expert, -1).astype(F32)
     member = jnp.zeros((group * 8, tok), F32)
     for j in range(8):
         member = member + (jnp.broadcast_to(ids[j:j + 1, :], member.shape) == expert).astype(F32)
     before = dot(member.astype(BF16), strict_upper(tok))
     key_s[...] = jnp.where(member > 0.0, before, -1.0).reshape(key_s.shape)
     rr = lax.broadcasted_iota(jnp.int32, (places, tok), 0)
-    place, e_of = lax.rem(rr, cap).astype(F32), rr // cap
-    some = 8
-    acc_s[...] = jnp.zeros_like(acc_s)
-
-    @pl.loop(0, group // some)
-    def _(i):
+    place, e_row = lax.rem(rr, cap).astype(F32), rr // cap
+    some = rows // places
+
+    @pl.loop(0, OWN)
+    def _(e):
+        pltpu.make_async_copy(dxb.at[:, pl.ds(pl.multiple_of(e * cap, 8), cap)], dxb.at[:, pl.ds(pl.multiple_of(e * cap, 8), cap)], drecv.at[e]).wait()
+
+    own_val.wait()
+
+    @pl.loop(1, GROUP)
+    def _(k):
+        val_copy(k).wait()
+
+    back = [pltpu.make_async_copy(dxb.at[pl.ds(i * some, some)], (xb if i % 2 == 0 else gb).reshape(some, places, hidden), lsem.at[i % 2]) for i in range(group // some)]
+    vals = pltpu.make_async_copy(valb, vb, lsem.at[2])
+    vals.start()
+    back[0].start()
+    for i in range(group // some):
+        if i + 1 < len(back):
+            back[i + 1].start()
+
         @pl.loop(0, some)
         def _(k):
             key = key_s[i * some + k]
             mine = jnp.full((places, tok), -1.0, F32)
             for e in range(OWN):
-                mine = jnp.where(e_of == e, jnp.broadcast_to(key[e:e + 1, :], (places, tok)), mine)
-            s_s[pl.ds(pl.multiple_of(k * places, places), places), :] = (place == mine).astype(F32).astype(BF16)
-
-        acc_s[...] += dot(s_s[...], dx_ref[pl.ds(i * some, some)].reshape(some * places, hidden), 0, 0)
-
-    out_ref[...] = acc_s[...].astype(BF16)
+                mine = jnp.where(e_row == e, jnp.broadcast_to(key[e:e + 1, :], (places, tok)), mine)
+            sb[pl.ds(pl.multiple_of(k * places, places), places), :] = (place == mine).astype(F32).astype(BF16)
+
+        back[i].wait()
+        part = dot(sb[...], (xb if i % 2 == 0 else gb)[...], 0, 0)
+        acc_s[...] = part if i == 0 else acc_s[...] + part
+
+    in_grad_ref[...] = acc_s[...].astype(BF16)
+    vals.wait()
 
     def gate_step(k, total):
+        number = lax.rem(k, NX * NC) * (NY * OWN) + k // (NX * NC) * OWN
         for e in range(OWN):
-            number = lax.rem(k, NX * NC) * (NY * OWN) + k // (NX * NC) * OWN + e
-            row = val_ref[k, e:e + 1, :]
-            total = total + jnp.where(ids == number.astype(F32), jnp.broadcast_to(row, ids.shape), 0.0)
+            row = vb[e, pl.ds(k, 1), :]
+            total = total + jnp.where(ids == (number + e).astype(F32), jnp.broadcast_to(row, ids.shape), 0.0)
         return total
 
     gate_ref[...] = lax.fori_loop(0, group, gate_step, jnp.zeros((8, tok), F32))
 
-
-def combine(cap, dx_back, val_back, meta):
-    group, places, hidden = dx_back.shape
-    tok = meta.shape[1]
-    return pl.pallas_call(
-        functools.partial(combine_kernel, cap),
-        name="combine",
-        out_shape=(jax.ShapeDtypeStruct((tok, hidden), BF16), jax.ShapeDtypeStruct((8, tok), F32)),
-        in_specs=[VMEM] * 3,
-        out_specs=(VMEM, VMEM),
-        scratch_shapes=[pltpu.VMEM((group, 8, tok), F32), pltpu.VMEM((8 * places, tok), BF16), pltpu.VMEM((tok, hidden), F32)],
-        cost_estimate=pl.CostEstimate(flops=2 * group * places * tok * hidden, bytes_accessed=2 * dx_back.size, transcendentals=0),
-    )(dx_back, val_back, meta)
+    step((TWO,), 1, ONE)
+
+    def keep(e, dy):
+        to = lax.rem(y + dy, NY)
+        src = r1.at[0, e, to // 2, :, pl.ds(pl.multiple_of(lax.rem(to, 2) * d_loc, 8), d_loc)]
+        dst = grads.at[:, y * OWN + e]
+        if dy == 0:
+            return pltpu.make_async_copy(src, dst, ysend.at[e, 0])
+        return remote(src, dst, ysend.at[e, dy], yrecv.at[e, (-dy) % NY], {"y": to})
+
+    @pl.loop(0, OWN)
+    def _(e):
+        for way in (0, 1):
+            hop(e, way, ONE).wait_recv()
+        add_into(r1.at[0, e], r1.at[1, e], G.at[e, z])
+        for dy in range(NY):
+            keep(e, dy).start()
+
+    @pl.loop(0, OWN)
+    def _(e):
+        keep(e, 0).wait()
+        for dy in range(1, NY):
+            remote(grads.at[:, lax.rem(y + dy, NY) * OWN + e], grads.at[:, lax.rem(y + dy, NY) * OWN + e], ysend.at[e, dy], yrecv.at[e, dy], {"y": lax.rem(y + dy, NY)}).wait_recv()
+            keep(e, dy).wait_send()
+        for way in (0, 1):
+            for kind in range(5):
+                hop(e, way, kind).wait_send()
+
+        sent = dxs.at[e, pl.ds(0, (GROUP - 1) * cap)]
+        pltpu.make_async_copy(sent, sent, dsend.at[e]).wait()
+
+
+def run_experts(cap, xr, ur, gr, sel, wa, meta):
+    _, rows, hidden = xr.shape
+    tok, ff = sel.shape[-1], wa.shape[-1]
+    d_loc = hidden // (NZ * NY)
+    half = hidden // NZ // 2
+    dma = pltpu.SemaphoreType.DMA
+    v = pltpu.VMEM
+    shape = jax.ShapeDtypeStruct
+    outs = pl.pallas_call(
+        functools.partial(expert_kernel, cap),
+        name="experts",
+        out_shape=(
+            shape((3, NY * OWN, d_loc, ff), F32),
+            shape((tok, hidden), BF16),
+            shape((8, tok), F32),
+            shape((GROUP, OWN * cap, hidden), BF16),
+            shape((OWN, GROUP, tok), F32),
+            shape((OWN, rows, hidden), BF16),
+        ),
+        in_specs=[ANY] * 5 + [VMEM],
+        out_specs=(ANY, VMEM, VMEM, ANY, ANY, ANY),
+        scratch_shapes=[
+            v((rows, hidden), BF16), v((rows, hidden), BF16), v((rows, hidden), BF16), v((rows, tok), BF16),
+            v((2, 3, NZ, NY, d_loc, ff), BF16), v((rows, ff), BF16), v((rows, ff), BF16), v((rows, ff), BF16), v((rows, 1), F32),
+            v((rows, hidden), BF16), v((OWN, GROUP, tok), F32), v((OWN, GROUP, tok), F32), v((GROUP, 8, tok), F32), v((tok, hidden), F32),
+            v((OWN, NZ, 2, 3, half, ff), F32), v((2, OWN, 3, half, ff), F32),
+            v((2, OWN, 2, 3, half, ff), F32), v((2, OWN, 2, 3, half, ff), F32), v((2, OWN, 2, 3, half, ff), F32),
+            dma((4,)), dma((2, 3)), dma((2, OWN, 5)), dma((2, OWN, 5)), dma((OWN, NY)), dma((OWN, NY)),
+            dma((OWN,)), dma((OWN,)), dma((2, GROUP)), dma((1,)),
+        ],
+        compiler_params=pltpu.CompilerParams(collective_id=1, has_side_effects=True, vmem_limit_bytes=67043328),
+    )(xr, ur, gr, sel, wa, meta)
+    return outs[:3]
 
 
 def solution(mesh):
@@ -434,21 +620,7 @@
         meta = jnp.concatenate([expert_ids.T.astype(F32), gate_vals.T])
         xa, ua, ma, wa = gather(layer_in, out_grad, meta, w)
         xr, ur, gr, s = dispatch(cap, xa, ua, ma)
-        dx, val, g1, g3, g2 = run_experts(cap, xr, ur, gr, s, wa)
-
-        def home(grad):
-            grad = lax.psum_scatter(grad, "z", scatter_dimension=1, tiled=True)
-            return grad.reshape(OWN, NY, d_loc, ff).swapaxes(0, 1)
-
-        grads = jnp.stack([home(g1), home(g3), home(g2)], axis=1)
-        grads = lax.all_to_all(grads, "y", 0, 0, tiled=True)
-
-        dx = dx.reshape(OWN, GROUP, cap, hidden).swapaxes(0, 1).reshape(GROUP, OWN * cap, hidden)
-        dx_back = lax.all_to_all(dx, PLANE, 0, 0, tiled=True)
-        val_back = lax.all_to_all(val.swapaxes(0, 1), PLANE, 0, 0, tiled=True)
-        in_grad, gate_out = combine(cap, dx_back, val_back, meta)
-
-        grads = grads.swapaxes(0, 1).reshape(3, local_experts, d_loc, ff)
+        grads, in_grad, gate_out = run_experts(cap, xr, ur, gr, s, wa, meta)
         return in_grad, gate_out.T, grads[0], grads[2].swapaxes(1, 2), grads[1]
 
     return jax.shard_map(per_device, mesh=mesh4, in_specs=(tok_spec, tok_spec, tok_spec, tok_spec, up_spec, down_spec, up_spec), out_specs=(tok_spec, tok_spec, up_spec, down_spec, up_spec), check_vma=False)

time: 474 us -> 364 us (0.77)
  waiting for transfers between devices: 222 us -> 0 us
  Pallas kernels: 200 us -> 354 us
  starting transfers between devices: 16.9 us -> 0 us
  between operations: 13.8 us -> 0.67 us
  local copies, waits for them, and re-layouts: 13.1 us -> 4.52 us
    reduce_scatter x3 -> x0, waiting for transfers between devices: 200 us -> none  [home(): grad = lax.psum_scatter(grad, 'z', scatter_dimension=1, tiled=True)]
    pallas_call x1, Pallas kernels: 45.2 us -> 207 us  [run_experts(): pl.pallas_call(functools.partial(expert_kernel, cap), name='experts', out...]
    all_to_all x3 -> x0, waiting for transfers between devices: 20.5 us -> none  [the longest x1 19.6 us: per_device(): grads = lax.all_to_all(grads, 'y', 0, 0, tiled=True)]
    all_to_all x3 -> x0, starting transfers between devices: 16.7 us -> none  [the longest x1 6.55 us: per_device(): dx_back = lax.all_to_all(dx, PLANE, 0, 0, tiled=True)]
    reshape x4 -> x0, local copies, waits for them, and re-layouts: 10.1 us -> none  [the longest x1 6.51 us: per_device(): dx.reshape(OWN, GROUP, cap, hidden).swapaxes(0, 1)]
    pallas_call x1 -> x0, Pallas kernels: 8.17 us -> none  [combine(): pl.pallas_call(functools.partial(combine_kernel, cap), name='combine', ou...]
  transfers between devices with their start and end apart: 6 -> 0, of which waited for: 5 -> 0; matrix products, arithmetic and copies ran while one was open for 3% -> 0% of each run, Pallas kernels for 2% -> 0%
where the time goes in v3:
time: 364 us
  Pallas kernels  354 us (97%)
  local copies, waits for them, and re-layouts  4.52 us (1%)
  other arithmetic  4.48 us (1%)
    pallas_call x1, Pallas kernels, run_experts(): pl.pallas_call(functools.partial(expert_kernel, cap), name='experts', out...  207 us
    pallas_call x1, Pallas kernels, gather(): pl.pallas_call(functools.partial(gather_kernel, order), name='gather', ou...  120 us
    pallas_call x1, Pallas kernels, dispatch(): pl.pallas_call(functools.partial(dispatch_kernel, cap), name='dispatch',...  27.3 us

profile of v3, /device:TPU:1, one launch (start us, length us, event | category | flops | bytes accessed | tf_op | source)
XLA Modules:
  0.0 363.6 jit_solution(6736209613366976934)
XLA Ops:
  0.6 0.7 convert_bitcast_fusion
  1.3 1.3 pad_maximum_fusion.meta_ref
  2.6 2.5 maximum_bitcast_fusion.w_ref
  5.1 119.7 %gather.1 = (bf16[32,256,1024]{2,1,0:T(8,128)(2,1)}, bf16[32,256,1024]{2,1,0:T(8,128)(2,1)}, f32[32,16,256]{2,1,0:T(8,128)}, bf16[8,4,3,4,32,384]{5,4,3,2,1,0:T(8,128)(2,1)}) custom-call(bf16[256,1024]{1,0:T(8,128)(2,1)} %x_ref.1, bf16[256,1024]{1,0:T(8,128)(2,1)} %u_ref.1, f32[16,256]{1,0:T(8,128)} %pad_maximum_fusion.meta_ref, ...), custom_call_target="tpu_custom_call" | custom-call | tf_op jit(solution)/shard_map/gather/pallas_call | solution.py:231
  124.8 27.3 %dispatch.1 = (bf16[4,768,1024]{2,1,0:T(8,128)(2,1)}, bf16[4,768,1024]{2,1,0:T(8,128)(2,1)}, bf16[4,768,1024]{2,1,0:T(8,128)(2,1)}, bf16[4,768,256]{2,1,0:T(8,128)(2,1)}) custom-call(bf16[32,256,1024]{2,1,0:T(8,128)(2,1)} %get-tuple-element.16.x_ref, bf16[32,256,1024]{2,1,0:T(8,128)(2,1)} %get-tuple-element.17.u_ref, f32[32,16,256]{2,1,0:T(8,128)} %get-tuple-element.18.meta_ref), custom_call_target="tpu_custom_call" | custom-call | flops 6442450944 | bytes 52428800 | tf_op jit(solution)/shard_map/dispatch/pallas_call | solution.py:294
  152.2 206.9 %experts.1 = (f32[3,16,32,384]{3,2,1,0:T(8,128)}, bf16[256,1024]{1,0:T(8,128)(2,1)}, f32[8,256]{1,0:T(8,128)}, bf16[32,96,1024]{2,1,0:T(8,128)(2,1)}, f32[4,32,2...) custom-call(bf16[4,768,1024]{2,1,0:T(8,128)(2,1)} %get-tuple-element.19.xr, bf16[4,768,1024]{2,1,0:T(8,128)(2,1)} %get-tuple-element.20.ur, ...), custom_call_target="tpu_custom_call" | custom-call | tf_op jit(solution)/shard_map/experts/pallas_call | solution.py:581
  359.1 0.0 copy-start
  359.1 0.0 copy-start.1
  359.1 3.1 slice_bitcast_fusion
  362.2 0.0 copy-done
  362.2 0.8 copy.14
  363.0 0.0 copy-done.1
  363.0 0.6 copy.15
Async XLA Ops:
  359.1 3.1 copy-start
  359.1 3.9 %copy-start.1 = (f32[8,256]{1,0:T(8,128)S(1)}, f32[8,256]{1,0:T(8,128)}, u32[]{:S(2)}) copy-start(f32[8,256]{1,0:T(8,128)} %get-tuple-element.25) | copy-start | bytes 24580

commit v4 on v3

v4 whole, which is shorter than its diff:
```python
import functools

import jax
import jax.numpy as jnp
from jax import lax
from jax.experimental import pallas as pl
from jax.experimental.pallas import tpu as pltpu
from jax.sharding import Mesh, PartitionSpec as P

NZ, NY, NX, NC = 8, 4, 4, 2
GROUP = NY * NX * NC
PLANE = ("y", "x", "core")
OWN = 4
F32, BF16 = jnp.float32, jnp.bfloat16
MESH = pl.DeviceIdType.MESH
ANY = pl.BlockSpec(memory_space=pl.ANY)
VMEM = pl.BlockSpec(memory_space=pltpu.VMEM)


def capacity_of(tok_dev, top_k, experts):
    return max(8, ((tok_dev * top_k * 5) // (4 * experts) + 7) // 8 * 8)


def dot(a, b, ca=1, cb=0):
    return lax.dot_general(a, b, (((ca,), (cb,)), ((), ())), preferred_element_type=F32)


def expert_base():
    ep = lax.axis_index("x") * NC + lax.axis_index("core")
    return ep * (NY * OWN) + lax.axis_index("y") * OWN


def strict_upper(n):
    rows = lax.broadcasted_iota(jnp.int32, (n, n), 0)
    cols = lax.broadcasted_iota(jnp.int32, (n, n), 1)
    return (rows < cols).astype(F32).astype(BF16)


def here():
    return tuple(lax.axis_index(a) for a in ("z", "y", "x", "core"))


def at_offset(k):
    _, y, x, c = here()
    dy, dx, dc = k // (NX * NC), lax.rem(k // NC, NX), lax.rem(k, NC)
    return {"y": lax.rem(y + dy, NY), "x": lax.rem(x + dx, NX), "core": lax.rem(c + dc, NC)}


def place_of(d):
    return d["y"] * (NX * NC) + d["x"] * NC + d["core"]


def z_at(dz):
    return {"z": lax.rem(lax.axis_index("z") + dz, NZ)}


def remote(src, dst, send_sem, recv_sem, target):
    return pltpu.make_async_remote_copy(src_ref=src, dst_ref=dst, send_sem=send_sem, recv_sem=recv_sem, device_id=target, device_id_type=MESH)


def enter():
    barrier = pltpu.get_barrier_semaphore()

    @pl.loop(1, GROUP)
    def _(k):
        pl.semaphore_signal(barrier, device_id=at_offset(k), device_id_type=MESH)

    for dz in (1, NZ - 1):
        pl.semaphore_signal(barrier, device_id=z_at(dz), device_id_type=MESH)
    return lambda: pl.semaphore_wait(barrier, GROUP + 1)


RATE, D2D, HOP, STEP = 46600.0, 300000.0, 2.0, 1.5


def gather_order(rows_bytes, cut, piece_bytes):
    size = {"A": rows_bytes * cut, "B": rows_bytes * (1.0 - cut)}
    free, coming, order, have, ready = {}, [], [], {}, {}

    def send(now, name, part, link, arrives, nbytes):
        rate = D2D if link == "core" else RATE
        t = max(now, free.get(link, 0.0)) + nbytes / rate
        free[link] = t
        coming.append((t + HOP, len(order), len(coming), arrives))
        return (name, part, link)

    def on_rows(now, kind, dy, dx):
        out = []
        first, second = ("x", "y") if kind == "A" else ("y", "x")
        d = {"x": dx, "y": dy}

        def go(axis, sign, part):
            nd = dict(d)
            nd[axis] = (d[axis] - sign) % 4
            arrives = (kind, nd["y"], nd["x"], part)
            out.append(send(now, (kind, dy, dx), part, axis + ("+" if sign > 0 else "-"), arrives, size[kind] / (2 if part is not None else 1)))

        if d[second] == 0:
            if d[first] == 0:
                go(first, 1, None)
                go(first, -1, None)
            elif d[first] == 3:
                go(first, 1, 0)
            elif d[first] == 1:
                go(first, -1, 1)
            go(second, 1, None)
            go(second, -1, None)
        elif d[second] == 3:
            go(second, 1, 0)
        elif d[second] == 1:
            go(second, -1, 1)
        out.append(send(now, (kind, dy, dx), None, "core", ("core", kind, dy, dx), size[kind]))
        return out

    def on_piece(now, dz, dy):
        out = []
        if dz == 0 or dz in (6, 7) or (dz == 5 and dy in (0, 1)):
            out.append(send(now, ("W", dz, dy), None, "z+", ("W", (dz - 1) % NZ, dy, None), piece_bytes))
        if dz == 0 or dz in (1, 2) or (dz == 3 and dy in (2, 3)):
            out.append(send(now, ("W", dz, dy), None, "z-", ("W", (dz + 1) % NZ, dy, None), piece_bytes))
        return out

    def arrived_for(dy, dx, now):
        return all(ready.get((kind, dy, dx), 1e9) <= now and ready.get(("core", kind, dy, dx), 1e9) <= now for kind in "AB")

    first = []
    for dy, link in ((1, "y+"), (3, "y-")):
        first.append(send(0.0, ("w", dy), None, link, ("W", 0, (-dy) % NY, None), piece_bytes))
    for part, link in ((0, "y+"), (1, "y-")):
        first.append(send(0.0, ("w", 2), part, link, ("R", part), piece_bytes / 2))
    first += on_piece(0.0, 0, 0) + on_rows(0.0, "B", 0, 0) + on_rows(0.0, "A", 0, 0)
    ready[("A", 0, 0)] = ready[("B", 0, 0)] = 0.0
    order.append((None, first))
    todo = [(dy, dx) for dy in range(NY) for dx in range(NX)]
    now = 0.0
    while coming or todo:
        coming.sort()
        place = next((p for p in todo if arrived_for(*p, now)), None)
        if place is not None and not (coming and coming[0][0] <= now):
            todo.remove(place)
            order.append((("place",) + place, []))
            now += STEP
            continue
        t, _, _, name = coming.pop(0)
        now = max(now, t)
        if name[0] == "core":
            ready[name] = now
        elif name[0] == "R":
            part = name[1]
            order.append((name, [send(now, ("R",), part, "y+" if part == 0 else "y-", ("W", 0, 2, part), piece_bytes / 2)]))
        else:
            key, part = name[:3], name[3]
            have[key] = have.get(key, 0) + (2 if part is None else 1)
            whole = have[key] == 2
            if name[0] == "W":
                order.append((name, on_piece(now, name[1], name[2]) if whole else []))
            else:
                if whole:
                    ready[key] = now
                order.append((name, on_rows(now, *key) if whole else []))
    return order


def hits(ids, expert, values):
    return jnp.sum(jnp.where(ids == expert, values, 0.0), axis=0, keepdims=True)


def gather_kernel(order, cap, cut, x_hbm, u_hbm, ids_ref, gate_ref, w1_hbm, w3_hbm, w2_hbm, xr, ur, gr, sel, wa,
                  rows, metas, wown, wv, relay, tri, sx, su, sg, ss,
                  recv, core_recv, wrecv, relay_recv, mrecv, send_sem, msend, load_sem, store_sem, wstore):
    z, y, x, c = here()
    tok = x_hbm.shape[0]
    own = wv.shape[3]

    def place(dy, dx, dc=0):
        return place_of(at_offset(dy * (NX * NC) + dx * NC + dc))

    me = place(0, 0)
    loads = [
        pltpu.make_async_copy(x_hbm, rows.at[me, pl.ds(0, tok)], load_sem.at[0]),
        pltpu.make_async_copy(u_hbm, rows.at[me, pl.ds(tok, tok)], load_sem.at[1]),
    ]
    for m, w in enumerate((w1_hbm, w3_hbm, w2_hbm)):
        loads.append(pltpu.make_async_copy(w.reshape(NY, own, *w.shape[1:]), wown.at[:, m], load_sem.at[2 + m]))
    for copy in loads:
        copy.start()
    metas[me, 0:8, :] = ids_ref[...].astype(F32)
    metas[me, 8:16, :] = gate_ref[...]

    all_in = enter()
    tri[...] = strict_upper(tok)
    for copy in loads:
        copy.wait()
    all_in()

    targets = {"core": {"core": 1 - c}}
    for sign, n in (("+", 1), ("-", -1)):
        targets["x" + sign] = {"x": lax.rem(x + n + NX, NX)}
        targets["y" + sign] = {"y": lax.rem(y + n + NY, NY)}
        targets["z" + sign] = z_at(n + NZ)
    step = {"x+": (0, 3), "x-": (0, 1), "y+": (3, 0), "y-": (1, 0)}
    spans = {"A": (0, cut), "B": (cut, 2 * tok - cut)}

    def block(kind, dy, dx, part=None, dc=0):
        start, size = spans[kind]
        if part is not None:
            size //= 2
            start += part * size
        return rows.at[place(dy, dx, dc), pl.ds(start, size)]

    def bsem(kind, dy, dx, part):
        return recv.at[0 if kind == "A" else 1, dy * NX + dx, part or 0]

    def piece(dz, dy, part=None):
        here = wv.at[lax.rem(z + dz, NZ), lax.rem(y + dy, NY)]
        return here if part is None else here.at[:, pl.ds(part * (own // 2), own // 2)]

    copies = []

    def issue(name, part, link):
        sem = send_sem.at[len(copies)]
        if name[0] == "w":
            dy = name[1]
            src = wown.at[lax.rem(y + dy, NY)]
            if part is None:
                copy = remote(src, piece(0, 0), sem, wrecv.at[0, (-dy) % NY, 0], targets[link])
            else:
                src = src.at[:, pl.ds(part * (own // 2), own // 2)]
                copy = remote(src, relay.at[part], sem, relay_recv.at[part], targets[link])
        elif name[0] == "R":
            dst = piece(0, 3 if part == 0 else 1, part)
            copy = remote(relay.at[part], dst, sem, wrecv.at[0, 2, part], targets[link])
        elif name[0] == "W":
            _, dz, dy = name
            ndz = (dz - 1) % NZ if link == "z+" else (dz + 1) % NZ
            src = wown.at[y] if (dz, dy) == (0, 0) else piece(dz, dy)
            copy = remote(src, piece(dz, dy), sem, wrecv.at[ndz, dy, 0], targets[link])
        else:
            kind, dy, dx = name
            here = block(kind, dy, dx, part)
            if link == "core":
                rsem = core_recv.at[0 if kind == "A" else 1, dy * NX + dx]
            else:
                oy, ox = step[link]
                rsem = bsem(kind, (dy + oy) % NY, (dx + ox) % NX, part)
            copy = remote(here, here, sem, rsem, targets[link])
        copy.start()
        copies.append(copy)

    def wait(here, sem):
        remote(here, here, send_sem.at[0], sem, targets["core"]).wait_recv()

    def meta_copy(k):
        return remote(metas.at[me], metas.at[me], msend.at[k], mrecv.at[k], at_offset(k))

    base = expert_base().astype(F32)
    n_rows = OWN * 2 * cap
    stores = []

    def put(dy, dx):
        n = len(stores)
        slot = n % 2
        if n >= 2:
            for copy in stores[n - 2]:
                copy.wait()
        for dc in (0, 1):
            if (dy, dx, dc) != (0, 0, 0):
                k = ((-dy) % NY) * (NX * NC) + ((-dx) % NX) * NC + dc
                wait(metas.at[place(dy, dx, dc)], mrecv.at[k])
        for i, kind in enumerate("AB"):
            wait(block(kind, dy, dx, None, 1), core_recv.at[i, dy * NX + dx])
        chip = lax.rem(y + dy, NY) * NX + lax.rem(x + dx, NX)
        r8 = lax.broadcasted_iota(jnp.int32, (8, tok), 0)
        r = lax.broadcasted_iota(jnp.int32, (n_rows, tok), 0)
        at = lax.rem(r, cap).astype(F32)
        e_of, p_of = r // (2 * cap), lax.rem(r // cap, 2)
        pick, gates = [], jnp.zeros((n_rows, tok), F32)
        for p in range(2):
            ids, gate = metas[2 * chip + p, 0:8, :], metas[2 * chip + p, 8:16, :]
            member = jnp.zeros((8, tok), F32)
            for e in range(OWN):
                member = jnp.where(r8 == e, hits(ids, base + e, 1.0), member)
            before = dot(member.astype(BF16), tri[...])
            key = jnp.where(member > 0.0, before, -1.0)
            mine = jnp.full((n_rows, tok), -1.0, F32)
            for e in range(OWN):
                here = jnp.logical_and(e_of == e, p_of == p)
                mine = jnp.where(here, jnp.broadcast_to(key[e:e + 1, :], (n_rows, tok)), mine)
                gates = jnp.where(here, jnp.broadcast_to(hits(ids, base + e, gate), (n_rows, tok)), gates)
            pick.append((at == mine).astype(F32))
        both = pick[0] + pick[1]
        scale = jnp.sum(both * gates, axis=1, keepdims=True)
        ss[slot] = both.astype(BF16).reshape(ss.shape[1:])
        pick = [p.astype(BF16) for p in pick]
        x_rows = dot(pick[0], rows[2 * chip, 0:tok, :]) + dot(pick[1], rows[2 * chip + 1, 0:tok, :])
        sx[slot] = x_rows.astype(BF16).reshape(sx.shape[1:])
        u_rows = dot(pick[0], rows[2 * chip, tok:2 * tok, :]) + dot(pick[1], rows[2 * chip + 1, tok:2 * tok, :])
        su[slot] = u_rows.astype(BF16).reshape(su.shape[1:])
        sg[slot] = (scale * u_rows).astype(BF16).reshape(sg.shape[1:])
        span = pl.ds(pl.multiple_of(chip * 2 * cap, 2 * cap), 2 * cap)
        out = [pltpu.make_async_copy(s.at[slot], d.at[:, span], store_sem.at[slot, i]) for i, (s, d) in enumerate(((sx, xr), (su, ur), (sg, gr), (ss, sel)))]
        for copy in out:
            copy.start()
        stores.append(out)

    wstores = []

    def keep(src, dz, dy):
        copy = pltpu.make_async_copy(src, wa.at[lax.rem(z + dz, NZ), lax.rem(y + dy, NY)], wstore.at[len(wstores)])
        copy.start()
        wstores.append(copy)

    parts = {}
    for name, sends in order:
        if name is None:
            pass
        elif name[0] == "place":
            put(*name[1:])
        elif name[0] == "R":
            wait(relay.at[name[1]], relay_recv.at[name[1]])
        elif name[0] == "W":
            _, dz, dy, part = name
            wait(piece(dz, dy, part), wrecv.at[dz, dy, part or 0])
        else:
            wait(block(*name), bsem(*name))
        for send in sends:
            issue(*send)
        if name is None:
            keep(wown.at[y], 0, 0)

            @pl.loop(1, GROUP)
            def _(k):
                meta_copy(k).start()
        elif name[0] == "W":
            parts[name[1:3]] = parts.get(name[1:3], 0) + (2 if name[3] is None else 1)
            if parts[name[1:3]] == 2:
                keep(piece(name[1], name[2]), name[1], name[2])

    for out in stores[-2:]:
        for copy in out:
            copy.wait()
    for copy in wstores:
        copy.wait()

    @pl.loop(1, GROUP)
    def _(k):
        meta_copy(k).wait_send()

    for copy in copies:
        copy.wait_send()


def gather(cap, x, u, ids, gates, w1, w3, w2):
    tok, hidden = x.shape
    local_experts, d_loc, ff = w1.shape
    own = local_experts // NY
    cut = tok - tok // 8 if tok % 256 == 0 else tok
    piece = (3, own, d_loc, ff)
    piece_bytes = 2 * 3 * own * d_loc * ff
    order = gather_order(4 * tok * hidden, cut / (2 * tok), piece_bytes)
    sends = sum(len(s) for _, s in order)
    dma, v = pltpu.SemaphoreType.DMA, pltpu.VMEM
    rows = GROUP * cap
    out = lambda lanes: jax.ShapeDtypeStruct((OWN, rows, lanes), BF16)
    stage = lambda lanes: v((2, OWN, 2 * cap, lanes), BF16)
    return pl.pallas_call(
        functools.partial(gather_kernel, order, cap, cut),
        name="gather",
        out_shape=(out(hidden), out(hidden), out(hidden), out(tok), jax.ShapeDtypeStruct((NZ, NY) + piece, BF16)),
        in_specs=[ANY, ANY, VMEM, VMEM, ANY, ANY, ANY],
        out_specs=(ANY,) * 5,
        scratch_shapes=[
            v((GROUP, 2 * tok, hidden), BF16), v((GROUP, 16, tok), F32), v((NY,) + piece, BF16), v((NZ, NY) + piece, BF16),
            v((2, 3, own // 2, d_loc, ff), BF16), v((tok, tok), BF16), stage(hidden), stage(hidden), stage(hidden), stage(tok),
            dma((2, NY * NX, 2)), dma((2, NY * NX)), dma((NZ, NY, 2)), dma((2,)), dma((GROUP,)), dma((sends,)), dma((GROUP,)),
            dma((5,)), dma((2, 4)), dma((NZ * NY,)),
        ],
        compiler_params=pltpu.CompilerParams(collective_id=0, has_side_effects=True, vmem_limit_bytes=67043328),
    )(x, u, ids, gates, w1, w3, w2)


FAR, SUM3, NEW3, TWO, ONE = range(5)


def expert_kernel(cap, xr, ur, gr, sel, wa, ids_ref, grads, in_grad_ref, gate_ref, dxb, valb, dxs,
                  xb, ub, gb, sb, wb, a_s, d1_s, d3_s, y_s, dx_s, val_s, vb, key_s, acc_s, G, r4, r3, r2, r1,
                  lsem, wsem, rsend, rrecv, ysend, yrecv, dsend, drecv, vsem, osem):
    z, y, x, c = here()
    rows, hidden = xb.shape
    ff, tok = a_s.shape[-1], sb.shape[-1]
    d_loc = hidden // (NZ * NY)
    me = place_of(at_offset(0))

    def row_copies(e):
        pairs = ((xr, xb), (gr, gb), (ur, ub), (sel, sb))
        return [pltpu.make_async_copy(src.at[e], dst, lsem.at[i]) for i, (src, dst) in enumerate(pairs)]

    def weight_copies(e, slot):
        return [pltpu.make_async_copy(wa.at[:, :, m, e], wb.at[slot, m], wsem.at[slot, m]) for m in range(3)]

    for copy in weight_copies(0, 0) + row_copies(0):
        copy.start()

    enter()()

    def chunk(e, way, dist):
        return G.at[e, z_at(dist if way else NZ - dist)["z"]]

    def hop(e, way, kind):
        h = way
        src, dst = {
            FAR: lambda: (chunk(e, way, 4).at[h], r4.at[way, e]),
            SUM3: lambda: (r4.at[way, e], r3.at[way, e, h]),
            NEW3: lambda: (chunk(e, way, 3).at[1 - h], r3.at[way, e, 1 - h]),
            TWO: lambda: (r3.at[way, e], r2.at[way, e]),
            ONE: lambda: (r2.at[way, e], r1.at[way, e]),
        }[kind]()
        return remote(src, dst, rsend.at[way, e, kind], rrecv.at[way, e, kind], z_at(1 if way else NZ - 1))

    def add_into(dst, *others):
        parts = dst.shape[:-2]

        def flat(ref, i):
            index = []
            for n in reversed(parts):
                index.append(lax.rem(i, n))
                i = i // n
            return ref.at[tuple(reversed(index))]

        n = 1
        for p in parts:
            n *= p

        @pl.loop(0, n)
        def _(i):
            total = flat(dst, i)[...]
            for other in others:
                total = total + flat(other, i)[...]
            flat(dst, i)[...] = total

    def dx_copy(e, k):
        to = at_offset(k)
        src = dxs.at[e, pl.ds(pl.multiple_of(place_of(to) * cap, 8), cap)]
        return remote(src, dxb.at[me, pl.ds(pl.multiple_of(e * cap, 8), cap)], dsend.at[e], drecv.at[e], to)

    def own_dx_copy(e):
        src = dxs.at[e, pl.ds(pl.multiple_of(me * cap, 8), cap)]
        return pltpu.make_async_copy(src, dxb.at[me, pl.ds(pl.multiple_of(e * cap, 8), cap)], drecv.at[e])

    tile = 256 if rows % 256 == 0 else rows
    dtile = 2 * hidden // NZ
    half = hidden // NZ // 2

    @pl.loop(0, OWN)
    def _(e):
        slot = lax.rem(e, 2)
        for copy in weight_copies(e, slot) + row_copies(e):
            copy.wait()

        @pl.when(e < OWN - 1)
        def _():
            for copy in weight_copies(e + 1, 1 - slot):
                copy.start()

        def w(m):
            return wb[slot, m].reshape(hidden, ff)

        @pl.loop(0, rows // tile)
        def _(i):
            at = pl.ds(pl.multiple_of(i * tile, tile), tile)
            x_rows = xb[at, :]
            h1, h3 = dot(x_rows, w(0)), dot(x_rows, w(1))
            sig = jax.nn.sigmoid(h1)
            silu = h1 * sig
            act = (silu * h3).astype(BF16)
            a_s[at, :] = act
            y_rows = dot(act, w(2), 1, 1)
            y_s[at, :] = jnp.sum(ub[at, :].astype(F32) * y_rows, axis=1, keepdims=True)
            da = dot(gb[at, :], w(2))
            d1 = (da * h3 * sig * (1.0 + h1 * (1.0 - sig))).astype(BF16)
            d3 = (da * silu).astype(BF16)
            d1_s[at, :] = d1
            d3_s[at, :] = d3
            dx_s[at, :] = (dot(d1, w(0), 1, 1) + dot(d3, w(1), 1, 1)).astype(BF16)

        out = pltpu.make_async_copy(dx_s, dxs.at[e], osem.at[0])
        out.start()

        @pl.loop(0, NZ // 2)
        def _(i):
            at = pl.ds(pl.multiple_of(i * dtile, dtile), dtile)
            x_cols, g_cols = xb[:, at], gb[:, at]
            for m, part in enumerate((dot(x_cols, d1_s[...], 0, 0), dot(x_cols, d3_s[...], 0, 0), dot(g_cols, a_s[...], 0, 0))):
                for j in range(4):
                    G[e, 2 * i + j // 2, j % 2, m] = part[j * half:(j + 1) * half]

        for way in (0, 1):
            for kind in (FAR, NEW3):
                hop(e, way, kind).start()
        val = sb[...].astype(F32) * y_s[...]
        val_s[e] = jnp.sum(val.reshape(rows // cap, cap, tok), axis=1)
        out.wait()

        @pl.when(e < OWN - 1)
        def _():
            for copy in row_copies(e + 1):
                copy.start()

        own_dx_copy(e).start()

        @pl.loop(1, GROUP)
        def _(k):
            dx_copy(e, k).start()

    def val_copy(k):
        to = at_offset(k)
        return remote(val_s.at[:, place_of(to)], valb.at[:, me], vsem.at[0, k], vsem.at[1, k], to)

    own_val = pltpu.make_async_copy(val_s.at[:, me], valb.at[:, me], vsem.at[0, 0])
    own_val.start()

    @pl.loop(1, GROUP)
    def _(k):
        val_copy(k).start()

    def step(arrived, dist, leaves):
        @pl.loop(0, OWN)
        def _(e):
            for way in (0, 1):
                for kind in arrived:
                    hop(e, way, kind).wait_recv()
                if leaves == SUM3:
                    add_into(r4.at[way, e], chunk(e, way, dist).at[way])
                else:
                    add_into((r3 if leaves == TWO else r2).at[way, e], chunk(e, way, dist))
                hop(e, way, leaves).start()

    step((FAR,), 3, SUM3)
    step((SUM3, NEW3), 2, TWO)

    group, places = dxb.shape[:2]
    ids = ids_ref[...].astype(F32)
    r = lax.broadcasted_iota(jnp.int32, (group * 8, tok), 0)
    d_of, e_of = r // 8, lax.rem(r, 8)
    expert = lax.rem(d_of, NX * NC) * (NY * OWN) + d_of // (NX * NC) * OWN + e_of
    expert = jnp.where(e_of < OWN, expert, -1).astype(F32)
    member = jnp.zeros((group * 8, tok), F32)
    for j in range(8):
        member = member + (jnp.broadcast_to(ids[j:j + 1, :], member.shape) == expert).astype(F32)
    before = dot(member.astype(BF16), strict_upper(tok))
    key_s[...] = jnp.where(member > 0.0, before, -1.0).reshape(key_s.shape)
    rr = lax.broadcasted_iota(jnp.int32, (places, tok), 0)
    place, e_row = lax.rem(rr, cap).astype(F32), rr // cap
    some = rows // places

    @pl.loop(0, OWN)
    def _(e):
        pltpu.make_async_copy(dxb.at[:, pl.ds(pl.multiple_of(e * cap, 8), cap)], dxb.at[:, pl.ds(pl.multiple_of(e * cap, 8), cap)], drecv.at[e]).wait()

    own_val.wait()

    @pl.loop(1, GROUP)
    def _(k):
        val_copy(k).wait()

    back = [pltpu.make_async_copy(dxb.at[pl.ds(i * some, some)], (xb if i % 2 == 0 else gb).reshape(some, places, hidden), lsem.at[i % 2]) for i in range(group // some)]
    vals = pltpu.make_async_copy(valb, vb, lsem.at[2])
    vals.start()
    back[0].start()
    for i in range(group // some):
        if i + 1 < len(back):
            back[i + 1].start()

        @pl.loop(0, some)
        def _(k):
            key = key_s[i * some + k]
            mine = jnp.full((places, tok), -1.0, F32)
            for e in range(OWN):
                mine = jnp.where(e_row == e, jnp.broadcast_to(key[e:e + 1, :], (places, tok)), mine)
            sb[pl.ds(pl.multiple_of(k * places, places), places), :] = (place == mine).astype(F32).astype(BF16)

        back[i].wait()
        part = dot(sb[...], (xb if i % 2 == 0 else gb)[...], 0, 0)
        acc_s[...] = part if i == 0 else acc_s[...] + part

    in_grad_ref[...] = acc_s[...].astype(BF16)
    vals.wait()

    def gate_step(k, total):
        number = lax.rem(k, NX * NC) * (NY * OWN) + k // (NX * NC) * OWN
        for e in range(OWN):
            row = vb[e, pl.ds(k, 1), :]
            total = total + jnp.where(ids == (number + e).astype(F32), jnp.broadcast_to(row, ids.shape), 0.0)
        return total

    gate_ref[...] = lax.fori_loop(0, group, gate_step, jnp.zeros((8, tok), F32))

    step((TWO,), 1, ONE)

    def keep(e, dy):
        to = lax.rem(y + dy, NY)
        src = r1.at[0, e, to // 2, :, pl.ds(pl.multiple_of(lax.rem(to, 2) * d_loc, 8), d_loc)]
        dst = grads.at[:, y * OWN + e]
        if dy == 0:
            return pltpu.make_async_copy(src, dst, ysend.at[e, 0])
        return remote(src, dst, ysend.at[e, dy], yrecv.at[e, (-dy) % NY], {"y": to})

    @pl.loop(0, OWN)
    def _(e):
        for way in (0, 1):
            hop(e, way, ONE).wait_recv()
        add_into(r1.at[0, e], r1.at[1, e], G.at[e, z])
        for dy in range(NY):
            keep(e, dy).start()

    @pl.loop(0, OWN)
    def _(e):
        keep(e, 0).wait()
        for dy in range(1, NY):
            remote(grads.at[:, lax.rem(y + dy, NY) * OWN + e], grads.at[:, lax.rem(y + dy, NY) * OWN + e], ysend.at[e, dy], yrecv.at[e, dy], {"y": lax.rem(y + dy, NY)}).wait_recv()
            keep(e, dy).wait_send()
        for way in (0, 1):
            for kind in range(5):
                hop(e, way, kind).wait_send()

        sent = dxs.at[e, pl.ds(0, (GROUP - 1) * cap)]
        pltpu.make_async_copy(sent, sent, dsend.at[e]).wait()


def run_experts(cap, xr, ur, gr, sel, wa, ids):
    _, rows, hidden = xr.shape
    tok, ff = sel.shape[-1], wa.shape[-1]
    d_loc = hidden // (NZ * NY)
    half = hidden // NZ // 2
    dma = pltpu.SemaphoreType.DMA
    v = pltpu.VMEM
    shape = jax.ShapeDtypeStruct
    outs = pl.pallas_call(
        functools.partial(expert_kernel, cap),
        name="experts",
        out_shape=(
            shape((3, NY * OWN, d_loc, ff), F32),
            shape((tok, hidden), BF16),
            shape((8, tok), F32),
            shape((GROUP, OWN * cap, hidden), BF16),
            shape((OWN, GROUP, tok), F32),
            shape((OWN, rows, hidden), BF16),
        ),
        in_specs=[ANY] * 5 + [VMEM],
        out_specs=(ANY, VMEM, VMEM, ANY, ANY, ANY),
        scratch_shapes=[
            v((rows, hidden), BF16), v((rows, hidden), BF16), v((rows, hidden), BF16), v((rows, tok), BF16),
            v((2, 3, NZ, NY, d_loc, ff), BF16), v((rows, ff), BF16), v((rows, ff), BF16), v((rows, ff), BF16), v((rows, 1), F32),
            v((rows, hidden), BF16), v((OWN, GROUP, tok), F32), v((OWN, GROUP, tok), F32), v((GROUP, 8, tok), F32), v((tok, hidden), F32),
            v((OWN, NZ, 2, 3, half, ff), F32), v((2, OWN, 3, half, ff), F32),
            v((2, OWN, 2, 3, half, ff), F32), v((2, OWN, 2, 3, half, ff), F32), v((2, OWN, 2, 3, half, ff), F32),
            dma((4,)), dma((2, 3)), dma((2, OWN, 5)), dma((2, OWN, 5)), dma((OWN, NY)), dma((OWN, NY)),
            dma((OWN,)), dma((OWN,)), dma((2, GROUP)), dma((1,)),
        ],
        compiler_params=pltpu.CompilerParams(collective_id=1, has_side_effects=True, vmem_limit_bytes=67043328),
    )(xr, ur, gr, sel, wa, ids)
    return outs[:3]


def solution(mesh):
    mesh4 = Mesh(mesh.devices.reshape(NZ, NY, NX, NC), ("z", "y", "x", "core"))
    tok_spec = P(("z", "y", "x", "core"), None)
    up_spec = P(("x", "core"), ("z", "y"), None)
    down_spec = P(("x", "core"), None, ("z", "y"))

    def per_device(layer_in, out_grad, expert_ids, gate_vals, w_one, w_two, w_three):
        tok_dev, hidden = layer_in.shape
        top_k = expert_ids.shape[1]
        local_experts, d_loc, ff = w_one.shape
        cap = capacity_of(tok_dev, top_k, local_experts * NX * NC)
        ids = expert_ids.T
        xr, ur, gr, sel, wa = gather(cap, layer_in, out_grad, ids, gate_vals.T, w_one, w_three, w_two.swapaxes(1, 2))
        grads, in_grad, gate_out = run_experts(cap, xr, ur, gr, sel, wa, ids)
        return in_grad, gate_out.T, grads[0], grads[2].swapaxes(1, 2), grads[1]

    return jax.shard_map(per_device, mesh=mesh4, in_specs=(tok_spec, tok_spec, tok_spec, tok_spec, up_spec, down_spec, up_spec), out_specs=(tok_spec, tok_spec, up_spec, down_spec, up_spec), check_vma=False)
```

time: 364 us -> 330 us (0.907)
  Pallas kernels: 354 us -> 322 us
  other arithmetic: 4.48 us -> 0 us
    pallas_call x2 -> x1, Pallas kernels: 147 us -> 116 us  [gather(): pl.pallas_call(functools.partial(gather_kernel, order, cap, cut), name='g...]
where the time goes in v4:
time: 330 us; the launch traced here: 329 us
  Pallas kernels  322 us (98%)
  local copies, waits for them, and re-layouts  6.22 us (2%)
    pallas_call x1, Pallas kernels, run_experts(): pl.pallas_call(functools.partial(expert_kernel, cap), name='experts', out...  206 us
    pallas_call x1, Pallas kernels, gather(): pl.pallas_call(functools.partial(gather_kernel, order, cap, cut), name='g...  116 us

profile of v4, /device:TPU:1, one launch (start us, length us, event | category | flops | bytes accessed | tf_op | source)
XLA Modules:
  0.0 329.3 jit_solution(1067890785396730529)
XLA Ops:
  0.6 116.0 %gather.1 = (bf16[4,768,1024]{2,1,0:T(8,128)(2,1)}, bf16[4,768,1024]{2,1,0:T(8,128)(2,1)}, bf16[4,768,1024]{2,1,0:T(8,128)(2,1)}, bf16[4,768,256]{2,1,0:T(8,128)(2,1)}, bf16[8,4,3,4,32,384]{5,4,3,2,1,0:T(8,128)(2,1)}) custom-call(bf16[256,1024]{1,0:T(8,128)(2,1)} %x_hbm.1, bf16[256,1024]{1,0:T(8,128)(2,1)} %u_hbm.1, s32[8,256]{1,0:T(8,128)} %bitcast.13, ...), custom_call_target="tpu_custom_call" | custom-call | tf_op jit(solution)/shard_map/gather/pallas_call | solution.py:366
  116.7 206.4 %experts.1 = (f32[3,16,32,384]{3,2,1,0:T(8,128)}, bf16[256,1024]{1,0:T(8,128)(2,1)}, f32[8,256]{1,0:T(8,128)}, bf16[32,96,1024]{2,1,0:T(8,128)(2,1)}, f32[4,32,2...) custom-call(bf16[4,768,1024]{2,1,0:T(8,128)(2,1)} %get-tuple-element.13.xr, bf16[4,768,1024]{2,1,0:T(8,128)(2,1)} %get-tuple-element.14.ur, ...), custom_call_target="tpu_custom_call" | custom-call | tf_op jit(solution)/shard_map/experts/pallas_call | solution.py:638
  323.1 3.1 slice_bitcast_fusion
  326.1 1.9 copy.14
  328.0 1.3 copy.15

commit v5 on v4

--- a/solution.py
+++ b/solution.py
@@ -12,7 +12,6 @@
 PLANE = ("y", "x", "core")
 OWN = 4
 F32, BF16 = jnp.float32, jnp.bfloat16
-MESH = pl.DeviceIdType.MESH
 ANY = pl.BlockSpec(memory_space=pl.ANY)
 VMEM = pl.BlockSpec(memory_space=pltpu.VMEM)
 
@@ -21,13 +20,19 @@
     return max(8, ((tok_dev * top_k * 5) // (4 * experts) + 7) // 8 * 8)
 
 
-def dot(a, b, ca=1, cb=0):
-    return lax.dot_general(a, b, (((ca,), (cb,)), ((), ())), preferred_element_type=F32)
-
-
-def expert_base():
-    ep = lax.axis_index("x") * NC + lax.axis_index("core")
-    return ep * (NY * OWN) + lax.axis_index("y") * OWN
+def contract(ca, cb):
+    return lambda a, b: lax.dot_general(a, b, (((ca,), (cb,)), ((), ())), preferred_element_type=F32)
+
+
+dot, dot_nt, dot_tn = contract(1, 0), contract(1, 1), contract(0, 0)
+
+
+def params(number):
+    return pltpu.CompilerParams(collective_id=number, has_side_effects=True, vmem_limit_bytes=67043328)
+
+
+def each_other(body):
+    return pl.loop(1, GROUP)(body)
 
 
 def strict_upper(n):
@@ -55,18 +60,18 @@
 
 
 def remote(src, dst, send_sem, recv_sem, target):
-    return pltpu.make_async_remote_copy(src_ref=src, dst_ref=dst, send_sem=send_sem, recv_sem=recv_sem, device_id=target, device_id_type=MESH)
+    return pltpu.make_async_remote_copy(src_ref=src, dst_ref=dst, send_sem=send_sem, recv_sem=recv_sem, device_id=target, device_id_type=pl.DeviceIdType.MESH)
 
 
 def enter():
     barrier = pltpu.get_barrier_semaphore()
 
-    @pl.loop(1, GROUP)
+    @each_other
     def _(k):
-        pl.semaphore_signal(barrier, device_id=at_offset(k), device_id_type=MESH)
+        pl.semaphore_signal(barrier, device_id=at_offset(k), device_id_type=pl.DeviceIdType.MESH)
 
     for dz in (1, NZ - 1):
-        pl.semaphore_signal(barrier, device_id=z_at(dz), device_id_type=MESH)
+        pl.semaphore_signal(barrier, device_id=z_at(dz), device_id_type=pl.DeviceIdType.MESH)
     return lambda: pl.semaphore_wait(barrier, GROUP + 1)
 
 
@@ -161,12 +166,12 @@
     return order
 
 
-def hits(ids, expert, values):
-    return jnp.sum(jnp.where(ids == expert, values, 0.0), axis=0, keepdims=True)
+def first_expert(d):
+    return lax.rem(d, NX * NC) * (NY * OWN) + d // (NX * NC) * OWN
 
 
 def gather_kernel(order, cap, cut, x_hbm, u_hbm, ids_ref, gate_ref, w1_hbm, w3_hbm, w2_hbm, xr, ur, gr, sel, wa,
-                  rows, metas, wown, wv, relay, tri, sx, su, sg, ss,
+                  rows, metas, gates_out, wown, wv, relay, tri, sx, su, sg, ss,
                   recv, core_recv, wrecv, relay_recv, mrecv, send_sem, msend, load_sem, store_sem, wstore):
     z, y, x, c = here()
     tok = x_hbm.shape[0]
@@ -184,8 +189,17 @@
         loads.append(pltpu.make_async_copy(w.reshape(NY, own, *w.shape[1:]), wown.at[:, m], load_sem.at[2 + m]))
     for copy in loads:
         copy.start()
-    metas[me, 0:8, :] = ids_ref[...].astype(F32)
-    metas[me, 8:16, :] = gate_ref[...]
+
+    @pl.loop(0, GROUP)
+    def _(d):
+        number = first_expert(d) + lax.broadcasted_iota(jnp.int32, (OWN, tok), 0)
+        value = jnp.full((OWN, tok), -1.0, F32)
+        for j in range(ids_ref.shape[0]):
+            chosen = ids_ref[pl.ds(j, 1), :] == number
+            value = jnp.where(chosen, jnp.broadcast_to(gate_ref[pl.ds(j, 1), :], value.shape), value)
+        gates_out[d] = value
+
+    metas[me] = gates_out[me]
 
     all_in = enter()
     tri[...] = strict_upper(tok)
@@ -251,17 +265,16 @@
         remote(here, here, send_sem.at[0], sem, targets["core"]).wait_recv()
 
     def meta_copy(k):
-        return remote(metas.at[me], metas.at[me], msend.at[k], mrecv.at[k], at_offset(k))
-
-    base = expert_base().astype(F32)
+        to = at_offset(k)
+        return remote(gates_out.at[place_of(to)], metas.at[me], msend.at[k], mrecv.at[k], to)
+
     n_rows = OWN * 2 * cap
     stores = []
 
     def put(dy, dx):
-        n = len(stores)
-        slot = n % 2
-        if n >= 2:
-            for copy in stores[n - 2]:
+        slot = len(stores) % 2
+        if stores[1:]:
+            for copy in stores[-2]:
                 copy.wait()
         for dc in (0, 1):
             if (dy, dx, dc) != (0, 0, 0):
@@ -270,24 +283,22 @@
         for i, kind in enumerate("AB"):
             wait(block(kind, dy, dx, None, 1), core_recv.at[i, dy * NX + dx])
         chip = lax.rem(y + dy, NY) * NX + lax.rem(x + dx, NX)
-        r8 = lax.broadcasted_iota(jnp.int32, (8, tok), 0)
+        n = 2 * OWN
+        which = lax.broadcasted_iota(jnp.int32, (n, tok), 0)
+        gate = jnp.zeros((n, tok), F32)
+        for i in range(n):
+            gate = jnp.where(which == i, jnp.broadcast_to(metas[2 * chip + i // OWN, pl.ds(i % OWN, 1), :], gate.shape), gate)
+        member = gate >= 0.0
+        key = jnp.where(member, dot(member.astype(F32).astype(BF16), tri[...]), -1.0)
         r = lax.broadcasted_iota(jnp.int32, (n_rows, tok), 0)
         at = lax.rem(r, cap).astype(F32)
-        e_of, p_of = r // (2 * cap), lax.rem(r // cap, 2)
-        pick, gates = [], jnp.zeros((n_rows, tok), F32)
-        for p in range(2):
-            ids, gate = metas[2 * chip + p, 0:8, :], metas[2 * chip + p, 8:16, :]
-            member = jnp.zeros((8, tok), F32)
-            for e in range(OWN):
-                member = jnp.where(r8 == e, hits(ids, base + e, 1.0), member)
-            before = dot(member.astype(BF16), tri[...])
-            key = jnp.where(member > 0.0, before, -1.0)
-            mine = jnp.full((n_rows, tok), -1.0, F32)
-            for e in range(OWN):
-                here = jnp.logical_and(e_of == e, p_of == p)
-                mine = jnp.where(here, jnp.broadcast_to(key[e:e + 1, :], (n_rows, tok)), mine)
-                gates = jnp.where(here, jnp.broadcast_to(hits(ids, base + e, gate), (n_rows, tok)), gates)
-            pick.append((at == mine).astype(F32))
+        row_of = lax.rem(r // cap, 2) * OWN + r // (2 * cap)
+        mine, gates = jnp.full((n_rows, tok), -1.0, F32), jnp.zeros((n_rows, tok), F32)
+        for i in range(n):
+            mine = jnp.where(row_of == i, jnp.broadcast_to(key[i:i + 1, :], mine.shape), mine)
+            gates = jnp.where(row_of == i, jnp.broadcast_to(gate[i:i + 1, :], mine.shape), gates)
+        found = at == mine
+        pick = [jnp.logical_and(found, row_of // OWN == p).astype(F32) for p in range(2)]
         both = pick[0] + pick[1]
         scale = jnp.sum(both * gates, axis=1, keepdims=True)
         ss[slot] = both.astype(BF16).reshape(ss.shape[1:])
@@ -328,7 +339,7 @@
         if name is None:
             keep(wown.at[y], 0, 0)
 
-            @pl.loop(1, GROUP)
+            @each_other
             def _(k):
                 meta_copy(k).start()
         elif name[0] == "W":
@@ -342,7 +353,7 @@
     for copy in wstores:
         copy.wait()
 
-    @pl.loop(1, GROUP)
+    @each_other
     def _(k):
         meta_copy(k).wait_send()
 
@@ -370,16 +381,16 @@
         in_specs=[ANY, ANY, VMEM, VMEM, ANY, ANY, ANY],
         out_specs=(ANY,) * 5,
         scratch_shapes=[
-            v((GROUP, 2 * tok, hidden), BF16), v((GROUP, 16, tok), F32), v((NY,) + piece, BF16), v((NZ, NY) + piece, BF16),
+            v((GROUP, 2 * tok, hidden), BF16), v((GROUP, OWN, tok), F32), v((GROUP, OWN, tok), F32), v((NY,) + piece, BF16), v((NZ, NY) + piece, BF16),
             v((2, 3, own // 2, d_loc, ff), BF16), v((tok, tok), BF16), stage(hidden), stage(hidden), stage(hidden), stage(tok),
             dma((2, NY * NX, 2)), dma((2, NY * NX)), dma((NZ, NY, 2)), dma((2,)), dma((GROUP,)), dma((sends,)), dma((GROUP,)),
             dma((5,)), dma((2, 4)), dma((NZ * NY,)),
         ],
-        compiler_params=pltpu.CompilerParams(collective_id=0, has_side_effects=True, vmem_limit_bytes=67043328),
+        compiler_params=params(0),
     )(x, u, ids, gates, w1, w3, w2)
 
 
-FAR, SUM3, NEW3, TWO, ONE = range(5)
+FAR, SUM3, NEW3, TWO, ONE, HOPS = 0, 1, 2, 3, 4, 7
 
 
 def expert_kernel(cap, xr, ur, gr, sel, wa, ids_ref, grads, in_grad_ref, gate_ref, dxb, valb, dxs,
@@ -401,7 +412,7 @@
     for copy in weight_copies(0, 0) + row_copies(0):
         copy.start()
 
-    enter()()
+    all_in = enter()
 
     def chunk(e, way, dist):
         return G.at[e, z_at(dist if way else NZ - dist)["z"]]
@@ -413,8 +424,7 @@
             SUM3: lambda: (r4.at[way, e], r3.at[way, e, h]),
             NEW3: lambda: (chunk(e, way, 3).at[1 - h], r3.at[way, e, 1 - h]),
             TWO: lambda: (r3.at[way, e], r2.at[way, e]),
-            ONE: lambda: (r2.at[way, e], r1.at[way, e]),
-        }[kind]()
+        }.get(kind, lambda: (r2.at[way, e, :, kind - ONE], r1.at[way, e, :, kind - ONE]))()
         return remote(src, dst, rsend.at[way, e, kind], rrecv.at[way, e, kind], z_at(1 if way else NZ - 1))
 
     def add_into(dst, *others):
@@ -448,8 +458,8 @@
         return pltpu.make_async_copy(src, dxb.at[me, pl.ds(pl.multiple_of(e * cap, 8), cap)], drecv.at[e])
 
     tile = 256 if rows % 256 == 0 else rows
-    dtile = 2 * hidden // NZ
-    half = hidden // NZ // 2
+    dtile = hidden // NZ
+    half = dtile // 2
 
     @pl.loop(0, OWN)
     def _(e):
@@ -474,29 +484,43 @@
             silu = h1 * sig
             act = (silu * h3).astype(BF16)
             a_s[at, :] = act
-            y_rows = dot(act, w(2), 1, 1)
+            y_rows = dot_nt(act, w(2))
             y_s[at, :] = jnp.sum(ub[at, :].astype(F32) * y_rows, axis=1, keepdims=True)
             da = dot(gb[at, :], w(2))
             d1 = (da * h3 * sig * (1.0 + h1 * (1.0 - sig))).astype(BF16)
             d3 = (da * silu).astype(BF16)
             d1_s[at, :] = d1
             d3_s[at, :] = d3
-            dx_s[at, :] = (dot(d1, w(0), 1, 1) + dot(d3, w(1), 1, 1)).astype(BF16)
+            dx_s[at, :] = (dot_nt(d1, w(0)) + dot_nt(d3, w(1))).astype(BF16)
 
         out = pltpu.make_async_copy(dx_s, dxs.at[e], osem.at[0])
         out.start()
 
         @pl.loop(0, NZ // 2)
         def _(i):
-            at = pl.ds(pl.multiple_of(i * dtile, dtile), dtile)
-            x_cols, g_cols = xb[:, at], gb[:, at]
-            for m, part in enumerate((dot(x_cols, d1_s[...], 0, 0), dot(x_cols, d3_s[...], 0, 0), dot(g_cols, a_s[...], 0, 0))):
+            pair = [z_at(n + 2 * i)["z"] for n in (3, 4)]
+
+            def cols(ref):
+                return jnp.concatenate([ref[:, pl.ds(pl.multiple_of(k * dtile, dtile), dtile)] for k in pair], axis=1)
+
+            x_cols, g_cols = cols(xb), cols(gb)
+            for m, part in enumerate((dot_tn(x_cols, d1_s[...]), dot_tn(x_cols, d3_s[...]), dot_tn(g_cols, a_s[...]))):
                 for j in range(4):
-                    G[e, 2 * i + j // 2, j % 2, m] = part[j * half:(j + 1) * half]
-
-        for way in (0, 1):
-            for kind in (FAR, NEW3):
-                hop(e, way, kind).start()
+                    G[e, pair[j // 2], j % 2, m] = part[j * half:(j + 1) * half]
+
+            @pl.when(i == 0)
+            def _():
+                @pl.when(e == 0)
+                def _():
+                    all_in()
+
+                for way, kind in ((0, FAR), (1, FAR), (1, NEW3)):
+                    hop(e, way, kind).start()
+
+            @pl.when(i == 1)
+            def _():
+                hop(e, 0, NEW3).start()
+
         val = sb[...].astype(F32) * y_s[...]
         val_s[e] = jnp.sum(val.reshape(rows // cap, cap, tok), axis=1)
         out.wait()
@@ -508,7 +532,7 @@
 
         own_dx_copy(e).start()
 
-        @pl.loop(1, GROUP)
+        @each_other
         def _(k):
             dx_copy(e, k).start()
 
@@ -519,7 +543,7 @@
     own_val = pltpu.make_async_copy(val_s.at[:, me], valb.at[:, me], vsem.at[0, 0])
     own_val.start()
 
-    @pl.loop(1, GROUP)
+    @each_other
     def _(k):
         val_copy(k).start()
 
@@ -529,11 +553,18 @@
             for way in (0, 1):
                 for kind in arrived:
                     hop(e, way, kind).wait_recv()
+                mine = chunk(e, way, dist)
                 if leaves == SUM3:
-                    add_into(r4.at[way, e], chunk(e, way, dist).at[way])
-                else:
-                    add_into((r3 if leaves == TWO else r2).at[way, e], chunk(e, way, dist))
-                hop(e, way, leaves).start()
+                    add_into(r4.at[way, e], mine.at[way])
+                elif leaves == TWO:
+                    add_into(r3.at[way, e], mine)
+                if leaves < ONE:
+                    hop(e, way, leaves).start()
+            if leaves == ONE:
+                for m in range(3):
+                    for way in (0, 1):
+                        add_into(r2.at[way, e, :, m], chunk(e, way, dist).at[:, m])
+                        hop(e, way, ONE + m).start()
 
     step((FAR,), 3, SUM3)
     step((SUM3, NEW3), 2, TWO)
@@ -559,7 +590,7 @@
 
     own_val.wait()
 
-    @pl.loop(1, GROUP)
+    @each_other
     def _(k):
         val_copy(k).wait()
 
@@ -580,7 +611,7 @@
             sb[pl.ds(pl.multiple_of(k * places, places), places), :] = (place == mine).astype(F32).astype(BF16)
 
         back[i].wait()
-        part = dot(sb[...], (xb if i % 2 == 0 else gb)[...], 0, 0)
+        part = dot_tn(sb[...], (xb if i % 2 == 0 else gb)[...])
         acc_s[...] = part if i == 0 else acc_s[...] + part
 
     in_grad_ref[...] = acc_s[...].astype(BF16)
@@ -597,30 +628,33 @@
 
     step((TWO,), 1, ONE)
 
-    def keep(e, dy):
+    def keep(e, m, dy):
         to = lax.rem(y + dy, NY)
-        src = r1.at[0, e, to // 2, :, pl.ds(pl.multiple_of(lax.rem(to, 2) * d_loc, 8), d_loc)]
-        dst = grads.at[:, y * OWN + e]
+        src = r1.at[0, e, to // 2, m, pl.ds(pl.multiple_of(lax.rem(to, 2) * d_loc, 8), d_loc)]
+        dst = grads.at[m, y * OWN + e]
         if dy == 0:
-            return pltpu.make_async_copy(src, dst, ysend.at[e, 0])
-        return remote(src, dst, ysend.at[e, dy], yrecv.at[e, (-dy) % NY], {"y": to})
+            return pltpu.make_async_copy(src, dst, ysend.at[e, m, dy])
+        return remote(src, dst, ysend.at[e, m, dy], yrecv.at[e, m, (-dy) % NY], {"y": to})
 
     @pl.loop(0, OWN)
     def _(e):
-        for way in (0, 1):
-            hop(e, way, ONE).wait_recv()
-        add_into(r1.at[0, e], r1.at[1, e], G.at[e, z])
-        for dy in range(NY):
-            keep(e, dy).start()
+        for m in range(3):
+            for way in (0, 1):
+                hop(e, way, ONE + m).wait_recv()
+            add_into(r1.at[0, e, :, m], r1.at[1, e, :, m], G.at[e, z, :, m])
+            for dy in range(NY):
+                keep(e, m, dy).start()
 
     @pl.loop(0, OWN)
     def _(e):
-        keep(e, 0).wait()
-        for dy in range(1, NY):
-            remote(grads.at[:, lax.rem(y + dy, NY) * OWN + e], grads.at[:, lax.rem(y + dy, NY) * OWN + e], ysend.at[e, dy], yrecv.at[e, dy], {"y": lax.rem(y + dy, NY)}).wait_recv()
-            keep(e, dy).wait_send()
+        for m in range(3):
+            keep(e, m, 0).wait()
+            for dy in range(1, NY):
+                got = grads.at[m, lax.rem(y + dy, NY) * OWN + e]
+                remote(got, got, ysend.at[e, m, dy], yrecv.at[e, m, dy], z_at(1)).wait_recv()
+                keep(e, m, dy).wait_send()
         for way in (0, 1):
-            for kind in range(5):
+            for kind in range(HOPS):
                 hop(e, way, kind).wait_send()
 
         sent = dxs.at[e, pl.ds(0, (GROUP - 1) * cap)]
@@ -654,12 +688,40 @@
             v((rows, hidden), BF16), v((OWN, GROUP, tok), F32), v((OWN, GROUP, tok), F32), v((GROUP, 8, tok), F32), v((tok, hidden), F32),
             v((OWN, NZ, 2, 3, half, ff), F32), v((2, OWN, 3, half, ff), F32),
             v((2, OWN, 2, 3, half, ff), F32), v((2, OWN, 2, 3, half, ff), F32), v((2, OWN, 2, 3, half, ff), F32),
-            dma((4,)), dma((2, 3)), dma((2, OWN, 5)), dma((2, OWN, 5)), dma((OWN, NY)), dma((OWN, NY)),
+            dma((4,)), dma((2, 3)), dma((2, OWN, HOPS)), dma((2, OWN, HOPS)), dma((OWN, 3, NY)), dma((OWN, 3, NY)),
             dma((OWN,)), dma((OWN,)), dma((2, GROUP)), dma((1,)),
         ],
-        compiler_params=pltpu.CompilerParams(collective_id=1, has_side_effects=True, vmem_limit_bytes=67043328),
+        compiler_params=params(1),
     )(xr, ur, gr, sel, wa, ids)
     return outs[:3]
+
+
+def finish_kernel(grads, in_grad, gate, *refs):
+    n = 5
+    outs, bufs, sems = refs[:n], refs[n:2 * n], refs[-1]
+    ins = [grads.at[m] for m in range(3)] + [in_grad, gate]
+    load = [pltpu.make_async_copy(a, b, sems.at[0, i]) for i, (a, b) in enumerate(zip(ins, bufs))]
+    store = [pltpu.make_async_copy(b, o, sems.at[1, i]) for i, (b, o) in enumerate(zip(bufs, outs))]
+    for copy in load:
+        copy.start()
+    for i in range(n):
+        load[i].wait()
+        store[i].start()
+    for copy in store:
+        copy.wait()
+
+
+def finish(grads, in_grad, gate):
+    shapes = [grads.shape[1:]] * 3 + [in_grad.shape, gate.shape]
+    types = [grads.dtype] * 3 + [in_grad.dtype, gate.dtype]
+    return pl.pallas_call(
+        finish_kernel,
+        name="finish",
+        out_shape=[jax.ShapeDtypeStruct(s, t) for s, t in zip(shapes, types)],
+        in_specs=[ANY] * 3,
+        out_specs=[ANY] * len(shapes),
+        scratch_shapes=[pltpu.VMEM(s, t) for s, t in zip(shapes, types)] + [pltpu.SemaphoreType.DMA((2, len(shapes)))],
+    )(grads, in_grad, gate)
 
 
 def solution(mesh):
@@ -676,6 +738,7 @@
         ids = expert_ids.T
         xr, ur, gr, sel, wa = gather(cap, layer_in, out_grad, ids, gate_vals.T, w_one, w_three, w_two.swapaxes(1, 2))
         grads, in_grad, gate_out = run_experts(cap, xr, ur, gr, sel, wa, ids)
-        return in_grad, gate_out.T, grads[0], grads[2].swapaxes(1, 2), grads[1]
+        g1, g3, g2, in_grad, gate_out = finish(grads, in_grad, gate_out)
+        return in_grad, gate_out.T, g1, g2.swapaxes(1, 2), g3
 
     return jax.shard_map(per_device, mesh=mesh4, in_specs=(tok_spec, tok_spec, tok_spec, tok_spec, up_spec, down_spec, up_spec), out_specs=(tok_spec, tok_spec, up_spec, down_spec, up_spec), check_vma=False)

time: 330 us -> 316 us (0.958)
  Pallas kernels: 322 us -> 315 us
  local copies, waits for them, and re-layouts: 6.22 us -> 0 us
    pallas_call x1, Pallas kernels: 206 us -> 199 us  [run_experts(): pl.pallas_call(functools.partial(expert_kernel, cap), name='experts', out...]
where the time goes in v5:
time: 316 us
  Pallas kernels  315 us (100%)
    pallas_call x1, Pallas kernels, run_experts(): pl.pallas_call(functools.partial(expert_kernel, cap), name='experts', out...  199 us
    pallas_call x1, Pallas kernels, gather(): pl.pallas_call(functools.partial(gather_kernel, order, cap, cut), name='g...  114 us

profile of v5, /device:TPU:1, one launch (start us, length us, event | category | flops | bytes accessed | tf_op | source)
XLA Modules:
  0.0 315.7 jit_solution(10854512163025042030)
XLA Ops:
  0.6 113.5 %gather.1 = (bf16[4,768,1024]{2,1,0:T(8,128)(2,1)}, bf16[4,768,1024]{2,1,0:T(8,128)(2,1)}, bf16[4,768,1024]{2,1,0:T(8,128)(2,1)}, bf16[4,768,256]{2,1,0:T(8,128)(2,1)}, bf16[8,4,3,4,32,384]{5,4,3,2,1,0:T(8,128)(2,1)}) custom-call(bf16[256,1024]{1,0:T(8,128)(2,1)} %x_hbm.1, bf16[256,1024]{1,0:T(8,128)(2,1)} %u_hbm.1, s32[8,256]{1,0:T(8,128)} %bitcast.6, ...), custom_call_target="tpu_custom_call" | custom-call | tf_op jit(solution)/shard_map/gather/pallas_call | solution.py:377
  114.2 198.6 %experts.1 = (f32[3,16,32,384]{3,2,1,0:T(8,128)}, bf16[256,1024]{1,0:T(8,128)(2,1)}, f32[8,256]{1,0:T(8,128)}, bf16[32,96,1024]{2,1,0:T(8,128)(2,1)}, f32[4,32,2...) custom-call(bf16[4,768,1024]{2,1,0:T(8,128)(2,1)} %get-tuple-element.18.xr, bf16[4,768,1024]{2,1,0:T(8,128)(2,1)} %get-tuple-element.19.ur, ...), custom_call_target="tpu_custom_call" | custom-call | tf_op jit(solution)/shard_map/experts/pallas_call | solution.py:672
  312.8 2.8 finish.1

commit v6 on v0

v6 whole, which is shorter than its diff:
```python
import functools

import jax
import jax.numpy as jnp
from jax import lax
from jax.experimental import pallas as pl
from jax.experimental.pallas import tpu as pltpu
from jax.sharding import Mesh, PartitionSpec as P

NZ, NY, NX, NC = 8, 4, 4, 2
GROUP = NY * NX * NC
PLANE = ("y", "x", "core")
OWN = 4
F32, BF16 = jnp.float32, jnp.bfloat16
ANY = pl.BlockSpec(memory_space=pl.ANY)
VMEM = pl.BlockSpec(memory_space=pltpu.VMEM)


def capacity_of(tok_dev, top_k, experts):
    return max(8, ((tok_dev * top_k * 5) // (4 * experts) + 7) // 8 * 8)


def rem(a, b):
    return a % b if isinstance(a, int) else lax.rem(a, b)


def contract(ca, cb):
    return lambda a, b: lax.dot_general(a, b, (((ca,), (cb,)), ((), ())), preferred_element_type=F32)


dot, dot_nt, dot_tn = contract(1, 0), contract(1, 1), contract(0, 0)


def params(number):
    return pltpu.CompilerParams(collective_id=number, has_side_effects=True, vmem_limit_bytes=67043328)


def each_other(body):
    return pl.loop(1, GROUP)(body)


def strict_upper(n):
    rows = lax.broadcasted_iota(jnp.int32, (n, n), 0)
    cols = lax.broadcasted_iota(jnp.int32, (n, n), 1)
    return (rows < cols).astype(F32).astype(BF16)


def here():
    return tuple(lax.axis_index(a) for a in ("z", "y", "x", "core"))


def at_offset(k):
    _, y, x, c = here()
    dy, dx, dc = k // (NX * NC), rem(k // NC, NX), rem(k, NC)
    return {"y": rem(y + dy, NY), "x": rem(x + dx, NX), "core": rem(c + dc, NC)}


def place_of(d):
    return d["y"] * (NX * NC) + d["x"] * NC + d["core"]


def z_at(dz):
    return {"z": rem(lax.axis_index("z") + dz, NZ)}


def remote(src, dst, send_sem, recv_sem, target):
    return pltpu.make_async_remote_copy(src_ref=src, dst_ref=dst, send_sem=send_sem, recv_sem=recv_sem, device_id=target, device_id_type=pl.DeviceIdType.MESH)


def enter():
    barrier = pltpu.get_barrier_semaphore()

    @each_other
    def _(k):
        pl.semaphore_signal(barrier, device_id=at_offset(k), device_id_type=pl.DeviceIdType.MESH)

    for dz in (1, NZ - 1):
        pl.semaphore_signal(barrier, device_id=z_at(dz), device_id_type=pl.DeviceIdType.MESH)
    return lambda: pl.semaphore_wait(barrier, GROUP + 1)


RATE, D2D, HOP, PUT, TILE = 46600.0, 300000.0, 2.0, 1.0, 2.5
CHIPS = 4

PIECE = {(0, None): (0, 1), (1, None): (1, 3), (1, 0): (1, 1), (1, 1): (2, 2)}
RELAYS = ((0, None, "y+"), (1, 0, "y+"), (1, 1, "y-"))


def gather_order(rows_bytes, cut, expert_bytes):
    size = {"A": rows_bytes * cut, "B": rows_bytes * (1.0 - cut)}
    free, coming, order, have, ready = {}, [], [], {}, {}

    def send(now, name, part, link, arrives, nbytes):
        t = max(now, free.get(link, 0.0)) + nbytes / (D2D if link == "core" else RATE)
        free[link] = t
        coming.append((t + HOP, len(order), len(coming), arrives))
        return (name, part, link)

    def on_rows(now, kind, dy, dx):
        out = []
        first, second = "xy" if kind == "A" else "yx"
        d = {"x": dx, "y": dy}

        def go(axis, sign, part):
            nd = dict(d)
            nd[axis] = (d[axis] - sign) % 4
            arrives = (kind, nd["y"], nd["x"], part)
            out.append(send(now, (kind, dy, dx), part, axis + "-+"[sign > 0], arrives, size[kind] / (1 if part is None else 2)))

        for axis in [first, second] if d[second] == 0 else [second]:
            if d[axis] == 0:
                go(axis, 1, None)
                go(axis, -1, None)
            elif d[axis] == 3:
                go(axis, 1, 0)
            elif d[axis] == 1:
                go(axis, -1, 1)
            if axis == first and d[first] != 0:
                go(second, 1, None)
                go(second, -1, None)
                break
        out.append(send(now, (kind, dy, dx), None, "core", ("core", kind, dy, dx), size[kind]))
        return out

    def weights(now, name, group, part, link, arrives):
        return send(now, name, part, link, arrives + (group, part), PIECE[group, part][1] * expert_bytes)

    def on_piece(now, dz, dy, group):
        out = []
        for link, step, far in (("z+", -1, dy < 2), ("z-", 1, dy >= 2)):
            if (step * dz) % NZ < 3 + far:
                out.append(weights(now, ("W", dz, dy, group), group, None, link, ("W", (dz + step) % NZ, dy)))
        return out

    def is_ready(dy, dx, now):
        return all(ready.get(key, 1e9) <= now for kind in "AB" for key in ((kind, dy, dx), ("core", kind, dy, dx)))

    first = []
    for group in range(2):
        for dy, link in ((1, "y+"), (3, "y-")):
            first.append(weights(0.0, ("w", dy, group), group, None, link, ("W", 0, (-dy) % NY)))
        for i, (g, part, link) in enumerate(RELAYS):
            if g == group:
                first.append((("r", i), part, link))
                weights(0.0, "r", g, part, link, ("R", i))
        first += on_piece(0.0, 0, 0, group)
    first += on_rows(0.0, "B", 0, 0) + on_rows(0.0, "A", 0, 0)
    ready["A", 0, 0] = ready["B", 0, 0] = 0.0
    order.append((None, first))
    todo, puts, tiles, now = [(dy, dx) for dy in range(NY) for dx in range(NX)], 0, 0, 0.0
    while coming or todo or tiles * CHIPS < puts:
        coming.sort()
        if not (coming and coming[0][0] <= now):
            place = next((p for p in todo if is_ready(*p, now)), None)
            if place is not None:
                todo.remove(place)
                order.append((("put",) + place, []))
                puts += 1
                now += PUT
                continue
            if puts >= (tiles + 1) * CHIPS and sum(key[0] == "W" and key[-1] == 0 for key in ready) == NZ * NY - 1:
                order.append((("tile", tiles), []))
                tiles += 1
                now += TILE
                continue
        t, _, _, name = coming.pop(0)
        now = max(now, t)
        if name[0] == "core":
            ready[name] = now
        elif name[0] == "R":
            i, group, part = name[1:]
            order.append((name[:2], [weights(now, name[:2], group, part, RELAYS[i][2], ("W", 0, 2))]))
        else:
            key, part = name[:-1], name[-1]
            have[key] = have.get(key, 0) + (2 if part is None else 1)
            sends = []
            if have[key] == 2:
                ready[key] = now
                sends = (on_piece if name[0] == "W" else on_rows)(now, *(key[1:] if name[0] == "W" else key))
            order.append((name, sends))
    return order


def first_expert(d):
    return rem(d, NX * NC) * (NY * OWN) + d // (NX * NC) * OWN


FAR, SUM3, NEW3, TWO, ONE, HOPS = 0, 1, 2, 3, 4, 7


def layer_kernel(order, cap, cut, scope_one, scope_two, x_hbm, u_hbm, ids_ref, gates_ref, w1_hbm, w3_hbm, w2_hbm,
                 grads, in_grad_ref, gate_ref, dxb, valb, dxs, xr, ur, gr, sel,
                 metas, gates_out, wown, wv, relay, xb, ub, gb, sb, a_s, d1_s, d3_s, y_s, dx_s, val_s, vb, key_s, acc_s,
                 recv, core_recv, wrecv, relay_recv, mrecv, send_sem, msend, load_sem, store_sem,
                 lsem, rsend, rrecv, ysend, yrecv, dsend, drecv, vsem, osem, in_scope):
    z, y, x, c = here()
    tok, hidden = x_hbm.shape
    rows, ff = xb.shape[0], a_s.shape[-1]
    d_loc = hidden // (NZ * NY)
    me = place_of(at_offset(0))

    def place(dy, dx, dc=0):
        return place_of(at_offset(dy * (NX * NC) + dx * NC + dc))

    targets = {"core": {"core": 1 - c}}
    for sign, n in (("+", 1), ("-", -1)):
        targets["x" + sign] = {"x": rem(x + n + NX, NX)}
        targets["y" + sign] = {"y": rem(y + n + NY, NY)}
        targets["z" + sign] = z_at(n + NZ)

    def wait(ref, sem):
        remote(ref, ref, send_sem.at[0], sem, targets["core"]).wait_recv()

    def w(e, m):
        return wv[:, :, e, m].reshape(hidden, ff)

    def expert_rows(e, spans):
        def cut_of(ref):
            return jnp.concatenate([ref[s, :] for s in spans]) if spans[1:] else ref[spans[0], :]

        def save(ref, value):
            n = value.shape[0] // len(spans)
            for i, s in enumerate(spans):
                ref[s, :] = value[i * n:(i + 1) * n]

        x_rows = cut_of(xb)
        h1, h3 = dot(x_rows, w(e, 0)), dot(x_rows, w(e, 1))
        sig = jax.nn.sigmoid(h1)
        silu = h1 * sig
        act = (silu * h3).astype(BF16)
        save(a_s, act)
        y_rows = dot_nt(act, w(e, 2))
        save(y_s, jnp.sum(cut_of(ub).astype(F32) * y_rows, axis=1, keepdims=True))
        da = dot(cut_of(gb), w(e, 2))
        d1 = (da * h3 * sig * (1.0 + h1 * (1.0 - sig))).astype(BF16)
        d3 = (da * silu).astype(BF16)
        save(d1_s, d1)
        save(d3_s, d3)
        save(dx_s, (dot_nt(d1, w(e, 0)) + dot_nt(d3, w(e, 1))).astype(BF16))

    def gather(all_rows, tri, sx, su, sg, ss):
        loads = [
            pltpu.make_async_copy(x_hbm, all_rows.at[me, pl.ds(0, tok)], load_sem.at[0]),
            pltpu.make_async_copy(u_hbm, all_rows.at[me, pl.ds(tok, tok)], load_sem.at[1]),
        ]
        for m, ref in enumerate((w1_hbm, w3_hbm, w2_hbm)):
            loads.append(pltpu.make_async_copy(ref.reshape(NY, OWN, d_loc, ff), wown.at[:, :, m], load_sem.at[2 + m]))
        for copy in loads:
            copy.start()
        all_in = enter()

        @pl.loop(0, GROUP)
        def _(d):
            number = first_expert(d) + lax.broadcasted_iota(jnp.int32, (OWN, tok), 0)
            value = jnp.full((OWN, tok), -1.0, F32)
            for j in range(ids_ref.shape[0]):
                chosen = ids_ref[pl.ds(j, 1), :] == number
                value = jnp.where(chosen, jnp.broadcast_to(gates_ref[pl.ds(j, 1), :], value.shape), value)
            gates_out[d] = value

        metas[me] = gates_out[me]
        tri[...] = strict_upper(tok)
        for copy in loads:
            copy.wait()
        all_in()

        back = {"x+": (0, 3), "x-": (0, 1), "y+": (3, 0), "y-": (1, 0)}
        spans = {"A": (0, cut), "B": (cut, 2 * tok - cut)}

        def block(kind, dy, dx, part=None, dc=0):
            start, size = spans[kind]
            if part is not None:
                size //= 2
                start += part * size
            return all_rows.at[place(dy, dx, dc), pl.ds(start, size)]

        def bsem(kind, dy, dx, part):
            return recv.at[0 if kind == "A" else 1, dy * NX + dx, part or 0]

        def piece(dz, dy, group, part=None):
            return wv.at[z_at(dz)["z"], rem(y + dy, NY), pl.ds(*PIECE[group, part])]

        row_copies = []

        def issue(name, part, link):
            number = len(row_copies) + len(weight_copies)
            sem = send_sem.at[number]
            group, part_of = None, None
            if name[0] == "w":
                _, dy, group = name
                src = wown.at[rem(y + dy, NY), pl.ds(*PIECE[group, None])]
                copy = remote(src, piece(0, 0, group), sem, wrecv.at[0, (-dy) % NY, group, 0], targets[link])
            elif name[0] in "rR":
                group, part_of, _ = RELAYS[name[1]]
                span = pl.ds(*PIECE[group, part_of])
                if name[0] == "r":
                    copy = remote(wown.at[rem(y + 2, NY), span], relay.at[span], sem, relay_recv.at[name[1]], targets[link])
                else:
                    dst = piece(0, back[link][0], group, part_of)
                    copy = remote(relay.at[span], dst, sem, wrecv.at[0, 2, group, part_of or 0], targets[link])
            elif name[0] == "W":
                _, dz, dy, group = name
                ndz = (dz - 1) % NZ if link == "z+" else (dz + 1) % NZ
                own = wown.at[y, pl.ds(*PIECE[group, None])]
                copy = remote(own if dz == dy == 0 else piece(dz, dy, group), piece(dz, dy, group), sem, wrecv.at[ndz, dy, group, 0], targets[link])
            else:
                kind, dy, dx = name
                ref = block(kind, dy, dx, part)
                if link == "core":
                    rsem = core_recv.at[0 if kind == "A" else 1, dy * NX + dx]
                else:
                    oy, ox = back[link]
                    rsem = bsem(kind, (dy + oy) % NY, (dx + ox) % NX, part)
                copy = remote(ref, ref, sem, rsem, targets[link])
            copy.start()
            if group is None:
                row_copies.append(copy)
            else:
                weight_copies.append((number, group, part_of))

        def meta_copy(k):
            to = at_offset(k)
            return remote(gates_out.at[place_of(to)], metas.at[me], msend.at[k], mrecv.at[k], to)

        n_rows = OWN * 2 * cap
        stores, chips = [], []

        def put(dy, dx):
            slot = len(stores) % 2
            if stores[1:]:
                for copy in stores[-2]:
                    copy.wait()
            for dc in (0, 1):
                if dy or dx or dc:
                    k = ((-dy) % NY) * (NX * NC) + ((-dx) % NX) * NC + dc
                    wait(metas.at[place(dy, dx, dc)], mrecv.at[k])
            for i, kind in enumerate("AB"):
                wait(block(kind, dy, dx, None, 1), core_recv.at[i, dy * NX + dx])
            chip = rem(y + dy, NY) * NX + rem(x + dx, NX)
            n = 2 * OWN
            which = lax.broadcasted_iota(jnp.int32, (n, tok), 0)
            gate = jnp.zeros((n, tok), F32)
            for i in range(n):
                gate = jnp.where(which == i, jnp.broadcast_to(metas[2 * chip + i // OWN, pl.ds(i % OWN, 1), :], gate.shape), gate)
            member = gate >= 0.0
            key = jnp.where(member, dot(member.astype(F32).astype(BF16), tri[...]), -1.0)
            r = lax.broadcasted_iota(jnp.int32, (n_rows, tok), 0)
            at = rem(r, cap).astype(F32)
            row_of = rem(r // cap, 2) * OWN + r // (2 * cap)
            mine, gates = jnp.full((n_rows, tok), -1.0, F32), jnp.zeros((n_rows, tok), F32)
            for i in range(n):
                mine = jnp.where(row_of == i, jnp.broadcast_to(key[i:i + 1, :], mine.shape), mine)
                gates = jnp.where(row_of == i, jnp.broadcast_to(gate[i:i + 1, :], mine.shape), gates)
            found = at == mine
            pick = [jnp.logical_and(found, row_of // OWN == p).astype(F32) for p in range(2)]
            both = pick[0] + pick[1]
            scale = jnp.sum(both * gates, axis=1, keepdims=True)
            pick = [p.astype(BF16) for p in pick]
            x_rows = dot(pick[0], all_rows[2 * chip, 0:tok, :]) + dot(pick[1], all_rows[2 * chip + 1, 0:tok, :])
            u_rows = dot(pick[0], all_rows[2 * chip, tok:2 * tok, :]) + dot(pick[1], all_rows[2 * chip + 1, tok:2 * tok, :])
            span = pl.ds(pl.multiple_of(chip * 2 * cap, 2 * cap), 2 * cap)
            out = []
            for i, (value, first, stage, far) in enumerate(((x_rows, xb, sx, xr), (u_rows, ub, su, ur), (scale * u_rows, gb, sg, gr), (both, sb, ss, sel))):
                value = value.astype(BF16)
                first[span, :] = value[:2 * cap]
                stage[slot] = value[2 * cap:].reshape(stage.shape[1:])
                out.append(pltpu.make_async_copy(stage.at[slot], far.at[:, span], store_sem.at[slot, i]))
                out[-1].start()
            stores.append(out)
            chips.append(span)

        for name, sends in order:
            if name is None:
                pass
            elif name[0] == "put":
                put(*name[1:])
            elif name[0] == "tile":
                expert_rows(0, chips[name[1] * CHIPS:(name[1] + 1) * CHIPS])
            elif name[0] == "R":
                group, part, _ = RELAYS[name[1]]
                wait(relay.at[pl.ds(*PIECE[group, part])], relay_recv.at[name[1]])
            elif name[0] == "W":
                _, dz, dy, group, part = name
                wait(piece(dz, dy, group, part), wrecv.at[dz, dy, group, part or 0])
            else:
                wait(block(*name), bsem(*name))
            for send in sends:
                issue(*send)
            if name is None:
                wv[z, y] = wown[y]

                @each_other
                def _(k):
                    meta_copy(k).start()

        for out in stores[-2:]:
            for copy in out:
                copy.wait()

        @each_other
        def _(k):
            meta_copy(k).wait_send()

        for copy in row_copies:
            copy.wait_send()

    def reduce(G, r4, r3, r2, r1):
        for dz in (1, NZ - 1):
            pl.semaphore_signal(in_scope, device_id=z_at(dz), device_id_type=pl.DeviceIdType.MESH)

        def row_loads(e):
            pairs = ((xr, xb), (gr, gb), (ur, ub), (sel, sb))
            return [pltpu.make_async_copy(src.at[e - 1], dst, lsem.at[i]) for i, (src, dst) in enumerate(pairs)]

        def chunk(e, way, dist):
            return G.at[e, z_at(dist if way else NZ - dist)["z"]]

        def hop(e, way, kind):
            h = way
            src, dst = {
                FAR: lambda: (chunk(e, way, 4).at[h], r4.at[way, e]),
                SUM3: lambda: (r4.at[way, e], r3.at[way, e, h]),
                NEW3: lambda: (chunk(e, way, 3).at[1 - h], r3.at[way, e, 1 - h]),
                TWO: lambda: (r3.at[way, e], r2.at[way, e]),
            }.get(kind, lambda: (r2.at[way, e, :, kind - ONE], r1.at[way, e, :, kind - ONE]))()
            return remote(src, dst, rsend.at[way, e, kind], rrecv.at[way, e, kind], z_at(1 if way else NZ - 1))

        def add_into(dst, *others):
            parts = dst.shape[:-2]

            def flat(ref, i):
                index = []
                for n in reversed(parts):
                    index.append(rem(i, n))
                    i = i // n
                return ref.at[tuple(reversed(index))]

            n = 1
            for p in parts:
                n *= p

            @pl.loop(0, n)
            def _(i):
                total = flat(dst, i)[...]
                for other in others:
                    total = total + flat(other, i)[...]
                flat(dst, i)[...] = total

        def own_rows(s):
            return pl.ds(pl.multiple_of(s * cap, 8), cap)

        def dx_copy(e, k):
            to = at_offset(k)
            return remote(dxs.at[e, own_rows(place_of(to))], dxb.at[me, own_rows(e)], dsend.at[e], drecv.at[e], to)

        tile = 256 if rows % 256 == 0 else rows
        dtile = hidden // NZ
        half = dtile // 2

        def weight_gradients(e):
            out = pltpu.make_async_copy(dx_s, dxs.at[e], osem.at[0])
            out.start()

            @pl.loop(0, NZ // 2)
            def _(i):
                pair = [z_at(n + 2 * i)["z"] for n in (3, 4)]

                def cols(ref):
                    return jnp.concatenate([ref[:, pl.ds(pl.multiple_of(k * dtile, dtile), dtile)] for k in pair], axis=1)

                x_cols, g_cols = cols(xb), cols(gb)
                for m, part in enumerate((dot_tn(x_cols, d1_s[...]), dot_tn(x_cols, d3_s[...]), dot_tn(g_cols, a_s[...]))):
                    for j in range(4):
                        G[e, pair[j // 2], j % 2, m] = part[j * half:(j + 1) * half]

                @pl.when(i == 0)
                def _():
                    if isinstance(e, int):
                        pl.semaphore_wait(in_scope, 2)
                    for way, kind in ((0, FAR), (1, FAR), (1, NEW3)):
                        hop(e, way, kind).start()

                @pl.when(i == 1)
                def _():
                    hop(e, 0, NEW3).start()

            val = sb[...].astype(F32) * y_s[...]
            val_s[e] = jnp.sum(val.reshape(rows // cap, cap, tok), axis=1)
            out.wait()

        def send_back(e):
            pltpu.make_async_copy(dxs.at[e, own_rows(me)], dxb.at[me, own_rows(e)], drecv.at[e]).start()

            @each_other
            def _(k):
                dx_copy(e, k).start()

        weight_gradients(0)
        for copy in row_loads(1):
            copy.start()
        send_back(0)

        @pl.loop(1, OWN)
        def _(e):
            for copy in row_loads(e):
                copy.wait()

            @pl.loop(0, rows // tile)
            def _(i):
                expert_rows(e, [pl.ds(pl.multiple_of(i * tile, tile), tile)])

            weight_gradients(e)

            @pl.when(e < OWN - 1)
            def _():
                for copy in row_loads(e + 1):
                    copy.start()

            send_back(e)

        def val_copy(k):
            to = at_offset(k)
            return remote(val_s.at[:, place_of(to)], valb.at[:, me], vsem.at[0, k], vsem.at[1, k], to)

        own_val = pltpu.make_async_copy(val_s.at[:, me], valb.at[:, me], vsem.at[0, 0])
        own_val.start()

        @each_other
        def _(k):
            val_copy(k).start()

        def step(arrived, dist, leaves):
            @pl.loop(0, OWN)
            def _(e):
                for way in (0, 1):
                    for kind in arrived:
                        hop(e, way, kind).wait_recv()
                    mine = chunk(e, way, dist)
                    if leaves == SUM3:
                        add_into(r4.at[way, e], mine.at[way])
                    elif leaves == TWO:
                        add_into(r3.at[way, e], mine)
                    if leaves < ONE:
                        hop(e, way, leaves).start()
                if leaves == ONE:
                    for m in range(3):
                        for way in (0, 1):
                            add_into(r2.at[way, e, :, m], chunk(e, way, dist).at[:, m])
                            hop(e, way, ONE + m).start()

        step((FAR,), 3, SUM3)
        step((SUM3, NEW3), 2, TWO)

        group, places = dxb.shape[:2]
        ids = ids_ref[...].astype(F32)
        r = lax.broadcasted_iota(jnp.int32, (group * 8, tok), 0)
        e_of = rem(r, 8)
        expert = jnp.where(e_of < OWN, first_expert(r // 8) + e_of, -1).astype(F32)
        member = jnp.zeros((group * 8, tok), F32)
        for j in range(ids.shape[0]):
            member = member + (jnp.broadcast_to(ids[j:j + 1, :], member.shape) == expert).astype(F32)
        before = dot(member.astype(BF16), strict_upper(tok))
        key_s[...] = jnp.where(member > 0.0, before, -1.0).reshape(key_s.shape)
        rr = lax.broadcasted_iota(jnp.int32, (places, tok), 0)
        at, e_row = rem(rr, cap).astype(F32), rr // cap
        some = rows // places

        @pl.loop(0, OWN)
        def _(e):
            got = dxb.at[:, own_rows(e)]
            pltpu.make_async_copy(got, got, drecv.at[e]).wait()

        own_val.wait()

        @each_other
        def _(k):
            val_copy(k).wait()

        bufs = (xb, gb)
        loads = [pltpu.make_async_copy(dxb.at[pl.ds(i * some, some)], bufs[i % 2].reshape(some, places, hidden), lsem.at[i % 2]) for i in range(group // some)]
        vals = pltpu.make_async_copy(valb, vb, lsem.at[2])
        vals.start()
        loads[0].start()
        for i, load in enumerate(loads):
            for later in loads[i + 1:i + 2]:
                later.start()

            @pl.loop(0, some)
            def _(k):
                key = key_s[i * some + k]
                mine = jnp.full((places, tok), -1.0, F32)
                for e in range(OWN):
                    mine = jnp.where(e_row == e, jnp.broadcast_to(key[e:e + 1, :], (places, tok)), mine)
                sb[pl.ds(pl.multiple_of(k * places, places), places), :] = (at == mine).astype(F32).astype(BF16)

            load.wait()
            part = dot_tn(sb[...], bufs[i % 2][...])
            acc_s[...] = acc_s[...] + part if i else part

        in_grad_ref[...] = acc_s[...].astype(BF16)
        vals.wait()

        def gate_step(k, total):
            for e in range(OWN):
                row = vb[e, pl.ds(k, 1), :]
                total = total + jnp.where(ids == (first_expert(k) + e).astype(F32), jnp.broadcast_to(row, ids.shape), 0.0)
            return total

        gate_ref[...] = lax.fori_loop(0, group, gate_step, jnp.zeros(ids.shape, F32))

        step((TWO,), 1, ONE)

        def keep(e, m, dy):
            to = rem(y + dy, NY)
            src = r1.at[0, e, to // 2, m, pl.ds(pl.multiple_of(rem(to, 2) * d_loc, 8), d_loc)]
            dst = grads.at[m, y * OWN + e]
            if dy == 0:
                return pltpu.make_async_copy(src, dst, ysend.at[e, m, dy])
            return remote(src, dst, ysend.at[e, m, dy], yrecv.at[e, m, (-dy) % NY], {"y": to})

        @pl.loop(0, OWN)
        def _(e):
            for m in range(3):
                for way in (0, 1):
                    hop(e, way, ONE + m).wait_recv()
                add_into(r1.at[0, e, :, m], r1.at[1, e, :, m], G.at[e, z, :, m])
                for dy in range(NY):
                    keep(e, m, dy).start()

        @pl.loop(0, OWN)
        def _(e):
            for m in range(3):
                keep(e, m, 0).wait()
                for dy in range(1, NY):
                    wait(grads.at[m, rem(y + dy, NY) * OWN + e], yrecv.at[e, m, dy])
                    keep(e, m, dy).wait_send()
            for way in (0, 1):
                for kind in range(HOPS):
                    hop(e, way, kind).wait_send()

            sent = dxs.at[e, pl.ds(0, (GROUP - 1) * cap)]
            pltpu.make_async_copy(sent, sent, dsend.at[e]).wait()

    weight_copies = []
    pl.run_scoped(gather, *scope_one)
    pl.run_scoped(reduce, *scope_two)
    for number, group, part in weight_copies:
        ref = wown.at[0, pl.ds(*PIECE[group, part])]
        remote(ref, ref, send_sem.at[number], relay_recv.at[0], targets["core"]).wait_send()


def layer(cap, x, u, ids, gates, w1, w3, w2):
    tok, hidden = x.shape
    local_experts, d_loc, ff = w1.shape
    rows = GROUP * cap
    half = hidden // NZ // 2
    cut = tok - tok // 8 if tok % 256 == 0 else tok
    order = gather_order(4 * tok * hidden, cut / (2 * tok), 2 * w1.size * 3 // local_experts)
    sends = sum(len(s) for _, s in order)
    dma, v, shape = pltpu.SemaphoreType.DMA, pltpu.VMEM, jax.ShapeDtypeStruct
    far = lambda lanes: shape((OWN - 1, rows, lanes), BF16)
    near = lambda lanes: v((rows, lanes), BF16)
    stage = lambda lanes: v((2, OWN - 1, 2 * cap, lanes), BF16)
    sums = [v((2, OWN, 2, 3, half, ff), F32)] * 3
    scope_one = [v((GROUP, 2 * tok, hidden), BF16), v((tok, tok), BF16), stage(hidden), stage(hidden), stage(hidden), stage(tok)]
    scope_two = [v((OWN, NZ, 2, 3, half, ff), F32), v((2, OWN, 3, half, ff), F32)] + sums
    per_expert = v((OWN, GROUP, tok), F32)
    gate_rows = v((GROUP, OWN, tok), F32)
    outs = pl.pallas_call(
        functools.partial(layer_kernel, order, cap, cut, scope_one, scope_two),
        name="layer",
        out_shape=(
            shape((3, local_experts, d_loc, ff), F32), shape((tok, hidden), BF16), shape(ids.shape, F32),
            shape((GROUP, OWN * cap, hidden), BF16), shape((OWN, GROUP, tok), F32), shape((OWN, rows, hidden), BF16),
            far(hidden), far(hidden), far(hidden), far(tok),
        ),
        in_specs=[ANY, ANY, VMEM, VMEM, ANY, ANY, ANY],
        out_specs=(ANY, VMEM, VMEM) + (ANY,) * 7,
        scratch_shapes=[
            gate_rows, gate_rows, v((NY, OWN, 3, d_loc, ff), BF16), v((NZ, NY, OWN, 3, d_loc, ff), BF16), v((OWN, 3, d_loc, ff), BF16),
            near(hidden), near(hidden), near(hidden), near(tok), near(ff), near(ff), near(ff), v((rows, 1), F32),
            near(hidden), per_expert, per_expert, v((GROUP, 8, tok), F32), v((tok, hidden), F32),
            dma((2, NY * NX, 2)), dma((2, NY * NX)), dma((NZ, NY, 2, 2)), dma((len(RELAYS),)), dma((GROUP,)), dma((sends,)), dma((GROUP,)),
            dma((5,)), dma((2, 4)),
            dma((4,)), dma((2, OWN, HOPS)), dma((2, OWN, HOPS)), dma((OWN, 3, NY)), dma((OWN, 3, NY)),
            dma((OWN,)), dma((OWN,)), dma((2, GROUP)), dma((1,)), pltpu.SemaphoreType.REGULAR,
        ],
        compiler_params=params(0),
    )(x, u, ids, gates, w1, w3, w2)
    return outs[:3]


def finish_kernel(grads, in_grad, gate, *refs):
    n = 5
    outs, bufs, sems = refs[:n], refs[n:2 * n], refs[-1]
    ins = [grads.at[m] for m in range(3)] + [in_grad, gate]
    load = [pltpu.make_async_copy(a, b, sems.at[0, i]) for i, (a, b) in enumerate(zip(ins, bufs))]
    store = [pltpu.make_async_copy(b, o, sems.at[1, i]) for i, (b, o) in enumerate(zip(bufs, outs))]
    for copy in load:
        copy.start()
    for i in range(n):
        load[i].wait()
        store[i].start()
    for copy in store:
        copy.wait()


def finish(grads, in_grad, gate):
    shapes = [grads.shape[1:]] * 3 + [in_grad.shape, gate.shape]
    types = [grads.dtype] * 3 + [in_grad.dtype, gate.dtype]
    return pl.pallas_call(
        finish_kernel,
        name="finish",
        out_shape=[jax.ShapeDtypeStruct(s, t) for s, t in zip(shapes, types)],
        in_specs=[ANY] * 3,
        out_specs=[ANY] * len(shapes),
        scratch_shapes=[pltpu.VMEM(s, t) for s, t in zip(shapes, types)] + [pltpu.SemaphoreType.DMA((2, len(shapes)))],
    )(grads, in_grad, gate)


def solution(mesh):
    mesh4 = Mesh(mesh.devices.reshape(NZ, NY, NX, NC), ("z", "y", "x", "core"))
    tok_spec = P(("z", "y", "x", "core"), None)
    up_spec = P(("x", "core"), ("z", "y"), None)
    down_spec = P(("x", "core"), None, ("z", "y"))

    def per_device(layer_in, out_grad, expert_ids, gate_vals, w_one, w_two, w_three):
        tok_dev, hidden = layer_in.shape
        top_k = expert_ids.shape[1]
        local_experts, d_loc, ff = w_one.shape
        cap = capacity_of(tok_dev, top_k, local_experts * NX * NC)
        ids = expert_ids.T
        grads, in_grad, gate_out = layer(cap, layer_in, out_grad, ids, gate_vals.T, w_one, w_three, w_two.swapaxes(1, 2))
        g1, g3, g2, in_grad, gate_out = finish(grads, in_grad, gate_out)
        return in_grad, gate_out.T, g1, g2.swapaxes(1, 2), g3

    return jax.shard_map(per_device, mesh=mesh4, in_specs=(tok_spec, tok_spec, tok_spec, tok_spec, up_spec, down_spec, up_spec), out_specs=(tok_spec, tok_spec, up_spec, down_spec, up_spec), check_vma=False)
```

time: 1220 us -> 308 us (0.25); the launches traced: 1210 us -> 308 us
  waiting for transfers between devices: 866 us -> 0 us
  Pallas kernels: 0 us -> 307 us
  matrix products: 125 us -> 0 us
  local copies, waits for them, and re-layouts: 83.3 us -> 0 us
  blocking collectives: 76.3 us -> 0 us
  starting transfers between devices: 24.1 us -> 0 us
  other arithmetic: 17.7 us -> 0 us
  between operations: 14.7 us -> 0.82 us
    reduce_scatter x3 -> x0, waiting for transfers between devices: 622 us -> none  [the longest x1 270 us: per_device(): lax.psum_scatter(grad_one, 'fsdp', scatter_dimension=1, tiled=True)]
    pallas_call x0 -> x2, Pallas kernels: none -> 307 us  [the longest x1 304 us: layer(): pl.pallas_call(functools.partial(layer_kernel, order, cap, cut, scope_one...]
    all_gather x3 -> x0, waiting for transfers between devices: 127 us -> none  [the longest x1 106 us: per_device(): w_three_full = lax.all_gather(w_three, 'fsdp', axis=1, tiled=True)]
    dot_general x9 -> x0, matrix products: 125 us -> none  [the longest x1 16.5 us: expert_grads(): jnp.einsum('pecf,pecd->efd', act_bf, g_rows, preferred_element_type=jnp.f...]
    all_to_all x4 -> x0, waiting for transfers between devices: 114 us -> none  [the longest x1 57.4 us: per_device(): lax.all_to_all(dx_rows, 'ep', 0, 0, tiled=True).reshape(places, hidden)]
    all_to_all x1 -> x0, blocking collectives: 76.3 us -> none  [per_device(): x_rows = lax.all_to_all(x_send, 'ep', 0, 0, tiled=True)]
    gather x5 -> x0, local copies, waits for them, and re-layouts: 54.4 us -> none  [take_rows(): return jnp.take(rows, row_index, axis=0, mode='fill', fill_value=0)]
    all_to_all x4 -> x0, starting transfers between devices: 23.1 us -> none  [the longest x1 6.41 us: per_device(): gate_rows = lax.all_to_all(gate_send, 'ep', 0, 0, tiled=True)]
  transfers between devices with their start and end apart: 10 -> 0, of which waited for: 7 -> 0; matrix products, arithmetic and copies ran while one was open for 16% -> 0% of each run, Pallas kernels for 0% -> 0%
where the time goes in v6:
time: 308 us
  Pallas kernels  307 us (100%)
    pallas_call x1, Pallas kernels, layer(): pl.pallas_call(functools.partial(layer_kernel, order, cap, cut, scope_one...  304 us

profile of v6, /device:TPU:1, one launch (start us, length us, event | category | flops | bytes accessed | tf_op | source)
XLA Modules:
  0.0 308.1 jit_solution(5114819187253742752)
XLA Ops:
  0.6 304.5 %layer.1 = (f32[3,16,32,384]{3,2,1,0:T(8,128)}, bf16[256,1024]{1,0:T(8,128)(2,1)}, f32[8,256]{1,0:T(8,128)}, bf16[32,96,1024]{2,1,0:T(8,128)(2,1)}, f32[4,32,256...) custom-call(bf16[256,1024]{1,0:T(8,128)(2,1)} %x_hbm.1, ...), custom_call_target="tpu_custom_call" | custom-call | tf_op jit(solution)/shard_map/layer/pallas_call | solution.py:669
  305.1 2.8 finish.1

commit v7 on v6

--- a/solution.py
+++ b/solution.py
@@ -67,6 +67,10 @@
     return pltpu.make_async_remote_copy(src_ref=src, dst_ref=dst, send_sem=send_sem, recv_sem=recv_sem, device_id=target, device_id_type=pl.DeviceIdType.MESH)
 
 
+def start(copy):
+    copy.start()
+
+
 def enter():
     barrier = pltpu.get_barrier_semaphore()
 
@@ -79,8 +83,10 @@
     return lambda: pl.semaphore_wait(barrier, GROUP + 1)
 
 
-RATE, D2D, HOP, PUT, TILE = 46600.0, 300000.0, 2.0, 1.0, 2.5
-CHIPS = 4
+RATE, D2D, HOP = 46600.0, 400000.0, 2.3
+PUT, TILE, ROWS = 1.0, 1.0, 0.4
+STEP = 5
+AHEAD = 5.0
 
 PIECE = {(0, None): (0, 1), (1, None): (1, 3), (1, 0): (1, 1), (1, 1): (2, 2)}
 RELAYS = ((0, None, "y+"), (1, 0, "y+"), (1, 1, "y-"))
@@ -88,7 +94,7 @@
 
 def gather_order(rows_bytes, cut, expert_bytes):
     size = {"A": rows_bytes * cut, "B": rows_bytes * (1.0 - cut)}
-    free, coming, order, have, ready = {}, [], [], {}, {}
+    free, pending, coming, order, have, ready = {}, {}, [], [], {}, {}
 
     def send(now, name, part, link, arrives, nbytes):
         t = max(now, free.get(link, 0.0)) + nbytes / (D2D if link == "core" else RATE)
@@ -96,88 +102,105 @@
         coming.append((t + HOP, len(order), len(coming), arrives))
         return (name, part, link)
 
-    def on_rows(now, kind, dy, dx):
+    def later(rank, name, part, link, arrives, nbytes):
+        queue = pending.setdefault(link, [])
+        queue.append((rank, len(order), len(queue), (name, part, link, arrives, nbytes)))
+
+    def turn(now):
         out = []
+        for link, queue in pending.items():
+            queue.sort()
+            while queue and free.get(link, 0.0) - now < AHEAD:
+                out.append(send(now, *queue.pop(0)[-1]))
+        return out
+
+    def on_rows(kind, dy, dx):
         first, second = "xy" if kind == "A" else "yx"
         d = {"x": dx, "y": dy}
 
         def go(axis, sign, part):
             nd = dict(d)
             nd[axis] = (d[axis] - sign) % 4
-            arrives = (kind, nd["y"], nd["x"], part)
-            out.append(send(now, (kind, dy, dx), part, axis + "-+"[sign > 0], arrives, size[kind] / (1 if part is None else 2)))
+            rank = 4 + (axis == second) + (part is not None)
+            later(rank, (kind, dy, dx), part, axis + "-+"[sign > 0], (kind, nd["y"], nd["x"], part), size[kind] / (1 if part is None else 2))
 
         for axis in [first, second] if d[second] == 0 else [second]:
-            if d[axis] == 0:
-                go(axis, 1, None)
-                go(axis, -1, None)
-            elif d[axis] == 3:
+            if d[axis] == 3:
                 go(axis, 1, 0)
             elif d[axis] == 1:
                 go(axis, -1, 1)
-            if axis == first and d[first] != 0:
-                go(second, 1, None)
-                go(second, -1, None)
-                break
-        out.append(send(now, (kind, dy, dx), None, "core", ("core", kind, dy, dx), size[kind]))
-        return out
-
-    def weights(now, name, group, part, link, arrives):
-        return send(now, name, part, link, arrives + (group, part), PIECE[group, part][1] * expert_bytes)
-
-    def on_piece(now, dz, dy, group):
-        out = []
+            elif d[axis] == 0:
+                go(axis, 1, None)
+                go(axis, -1, None)
+
+    def core(now, key, part):
+        return send(now, key, part, "core", ("core",) + key + (part,), size[key[0]] / (1 if part is None else 2))
+
+    def weights(rank, name, group, part, link, arrives):
+        later(rank, name, part, link, arrives + (group, part), PIECE[group, part][1] * expert_bytes)
+
+    def on_piece(dz, dy, group):
         for link, step, far in (("z+", -1, dy < 2), ("z-", 1, dy >= 2)):
-            if (step * dz) % NZ < 3 + far:
-                out.append(weights(now, ("W", dz, dy, group), group, None, link, ("W", (dz + step) % NZ, dy)))
-        return out
-
-    def is_ready(dy, dx, now):
-        return all(ready.get(key, 1e9) <= now for kind in "AB" for key in ((kind, dy, dx), ("core", kind, dy, dx)))
-
-    first = []
+            gone = (step * dz) % NZ
+            if gone < 3 + far:
+                weights(4 * group + gone, ("W", dz, dy, group), group, None, link, ("W", (dz + step) % NZ, dy))
+
+    def arrived(key, part):
+        have[key] = have.get(key, 0) + (2 if part is None else 1)
+        if have[key] == 2:
+            ready[key] = True
+        return have[key] == 2
+
+    for i, (group, part, link) in enumerate(RELAYS):
+        weights(0, ("r", i), group, part, link, ("R", i))
     for group in range(2):
         for dy, link in ((1, "y+"), (3, "y-")):
-            first.append(weights(0.0, ("w", dy, group), group, None, link, ("W", 0, (-dy) % NY)))
-        for i, (g, part, link) in enumerate(RELAYS):
-            if g == group:
-                first.append((("r", i), part, link))
-                weights(0.0, "r", g, part, link, ("R", i))
-        first += on_piece(0.0, 0, 0, group)
-    first += on_rows(0.0, "B", 0, 0) + on_rows(0.0, "A", 0, 0)
-    ready["A", 0, 0] = ready["B", 0, 0] = 0.0
-    order.append((None, first))
-    todo, puts, tiles, now = [(dy, dx) for dy in range(NY) for dx in range(NX)], 0, 0, 0.0
-    while coming or todo or tiles * CHIPS < puts:
+            weights(2, ("w", dy, group), group, None, link, ("W", 0, (-dy) % NY))
+        on_piece(0, 0, group)
+    sends = []
+    for kind in "BA":
+        arrived((kind, 0, 0), None)
+        on_rows(kind, 0, 0)
+        sends.append(core(0.0, (kind, 0, 0), None))
+    order.append((None, turn(0.0) + sends))
+    todo, puts, done, now = [(dy, dx) for dy in range(NY) for dx in range(NX)], 0, 0, 0.0
+    while coming or todo or done < puts:
         coming.sort()
-        if not (coming and coming[0][0] <= now):
-            place = next((p for p in todo if is_ready(*p, now)), None)
+        soon = coming[0][0] if coming else 1e9
+        if soon > now:
+            place = next((p for p in todo if all(pre + (kind,) + p in ready for kind in "AB" for pre in ((), ("core",)))), None)
             if place is not None:
                 todo.remove(place)
-                order.append((("put",) + place, []))
+                order.append((("put",) + place, turn(now)))
                 puts += 1
                 now += PUT
                 continue
-            if puts >= (tiles + 1) * CHIPS and sum(key[0] == "W" and key[-1] == 0 for key in ready) == NZ * NY - 1:
-                order.append((("tile", tiles), []))
-                tiles += 1
-                now += TILE
+            step = min(STEP, puts - done)
+            weights_in = sum(key[0] == "W" and key[-1] == 0 for key in ready) == NZ * NY - 1
+            if weights_in and (step >= 3 and soon - now > TILE or not todo):
+                order.append((("tile", done, done + step), turn(now)))
+                done += step
+                now += TILE + ROWS * step
                 continue
         t, _, _, name = coming.pop(0)
         now = max(now, t)
+        key, part = name[:-1], name[-1]
         if name[0] == "core":
-            ready[name] = now
-        elif name[0] == "R":
+            arrived(key, part)
+            continue
+        sends = []
+        if name[0] == "R":
             i, group, part = name[1:]
-            order.append((name[:2], [weights(now, name[:2], group, part, RELAYS[i][2], ("W", 0, 2))]))
+            weights(1, name[:2], group, part, RELAYS[i][2], ("W", 0, 2))
+            name = name[:2]
+        elif name[0] == "W":
+            if arrived(key, part):
+                on_piece(*key[1:])
         else:
-            key, part = name[:-1], name[-1]
-            have[key] = have.get(key, 0) + (2 if part is None else 1)
-            sends = []
-            if have[key] == 2:
-                ready[key] = now
-                sends = (on_piece if name[0] == "W" else on_rows)(now, *(key[1:] if name[0] == "W" else key))
-            order.append((name, sends))
+            sends = [core(now, key, part)]
+            if arrived(key, part):
+                on_rows(*key)
+        order.append((name, sends + turn(now)))
     return order
 
 
@@ -185,7 +208,7 @@
     return rem(d, NX * NC) * (NY * OWN) + d // (NX * NC) * OWN
 
 
-FAR, SUM3, NEW3, TWO, ONE, HOPS = 0, 1, 2, 3, 4, 7
+FAR, SUM3, NEW3, TWO, ONE, HOPS = 0, 1, 2, 3, 4, 10
 
 
 def layer_kernel(order, cap, cut, scope_one, scope_two, x_hbm, u_hbm, ids_ref, gates_ref, w1_hbm, w3_hbm, w2_hbm,
@@ -307,7 +330,7 @@
                 kind, dy, dx = name
                 ref = block(kind, dy, dx, part)
                 if link == "core":
-                    rsem = core_recv.at[0 if kind == "A" else 1, dy * NX + dx]
+                    rsem = core_recv.at[0 if kind == "A" else 1, dy * NX + dx, part or 0]
                 else:
                     oy, ox = back[link]
                     rsem = bsem(kind, (dy + oy) % NY, (dx + ox) % NX, part)
@@ -334,8 +357,9 @@
                 if dy or dx or dc:
                     k = ((-dy) % NY) * (NX * NC) + ((-dx) % NX) * NC + dc
                     wait(metas.at[place(dy, dx, dc)], mrecv.at[k])
-            for i, kind in enumerate("AB"):
-                wait(block(kind, dy, dx, None, 1), core_recv.at[i, dy * NX + dx])
+            for i, (kind, last) in enumerate((("A", dx if dy == 0 else dy), ("B", dy if dx == 0 else dx))):
+                for part in (0, 1) if last == 2 else (None,):
+                    wait(block(kind, dy, dx, part, 1), core_recv.at[i, dy * NX + dx, part or 0])
             chip = rem(y + dy, NY) * NX + rem(x + dx, NX)
             n = 2 * OWN
             which = lax.broadcasted_iota(jnp.int32, (n, tok), 0)
@@ -375,7 +399,7 @@
             elif name[0] == "put":
                 put(*name[1:])
             elif name[0] == "tile":
-                expert_rows(0, chips[name[1] * CHIPS:(name[1] + 1) * CHIPS])
+                expert_rows(0, chips[name[1]:name[2]])
             elif name[0] == "R":
                 group, part, _ = RELAYS[name[1]]
                 wait(relay.at[pl.ds(*PIECE[group, part])], relay_recv.at[name[1]])
@@ -415,6 +439,9 @@
         def chunk(e, way, dist):
             return G.at[e, z_at(dist if way else NZ - dist)["z"]]
 
+        def half_of(ref, way, e, kind):
+            return ref.at[way, e, (kind - ONE) % 2, (kind - ONE) // 2]
+
         def hop(e, way, kind):
             h = way
             src, dst = {
@@ -422,11 +449,17 @@
                 SUM3: lambda: (r4.at[way, e], r3.at[way, e, h]),
                 NEW3: lambda: (chunk(e, way, 3).at[1 - h], r3.at[way, e, 1 - h]),
                 TWO: lambda: (r3.at[way, e], r2.at[way, e]),
-            }.get(kind, lambda: (r2.at[way, e, :, kind - ONE], r1.at[way, e, :, kind - ONE]))()
+            }.get(kind, lambda: (half_of(r2, way, e, kind), half_of(r1, way, e, kind)))()
             return remote(src, dst, rsend.at[way, e, kind], rrecv.at[way, e, kind], z_at(1 if way else NZ - 1))
 
         def add_into(dst, *others):
             parts = dst.shape[:-2]
+            if not parts:
+                total = dst[...]
+                for other in others:
+                    total = total + other[...]
+                dst[...] = total
+                return
 
             def flat(ref, i):
                 index = []
@@ -543,10 +576,10 @@
                     if leaves < ONE:
                         hop(e, way, leaves).start()
                 if leaves == ONE:
-                    for m in range(3):
+                    for kind in range(ONE, HOPS):
                         for way in (0, 1):
-                            add_into(r2.at[way, e, :, m], chunk(e, way, dist).at[:, m])
-                            hop(e, way, ONE + m).start()
+                            add_into(half_of(r2, way, e, kind), half_of(G, e, z_at(dist if way else NZ - dist)["z"], kind))
+                            hop(e, way, kind).start()
 
         step((FAR,), 3, SUM3)
         step((SUM3, NEW3), 2, TWO)
@@ -610,30 +643,37 @@
 
         step((TWO,), 1, ONE)
 
-        def keep(e, m, dy):
-            to = rem(y + dy, NY)
-            src = r1.at[0, e, to // 2, m, pl.ds(pl.multiple_of(rem(to, 2) * d_loc, 8), d_loc)]
+        def keep(e, m, to, then_remote, then_local):
+            src = r1.at[0, e, to // 2, m, pl.ds(to % 2 * d_loc, d_loc)]
             dst = grads.at[m, y * OWN + e]
-            if dy == 0:
-                return pltpu.make_async_copy(src, dst, ysend.at[e, m, dy])
-            return remote(src, dst, ysend.at[e, m, dy], yrecv.at[e, m, (-dy) % NY], {"y": to})
+
+            @pl.when(y != to)
+            def _():
+                then_remote(remote(src, dst, ysend.at[e, m, to], yrecv.at[e, m, y], {"y": to}))
+
+            @pl.when(y == to)
+            def _():
+                then_local(pltpu.make_async_copy(src, dst, ysend.at[e, m, to]))
+
+        @pl.loop(0, OWN)
+        def _(e):
+            for kind in range(ONE, HOPS):
+                for way in (0, 1):
+                    hop(e, way, kind).wait_recv()
+                add_into(half_of(r1, 0, e, kind), half_of(r1, 1, e, kind), half_of(G, e, z, kind))
+                m, h = (kind - ONE) // 2, (kind - ONE) % 2
+                for to in (2 * h, 2 * h + 1):
+                    keep(e, m, to, start, start)
 
         @pl.loop(0, OWN)
         def _(e):
             for m in range(3):
-                for way in (0, 1):
-                    hop(e, way, ONE + m).wait_recv()
-                add_into(r1.at[0, e, :, m], r1.at[1, e, :, m], G.at[e, z, :, m])
-                for dy in range(NY):
-                    keep(e, m, dy).start()
-
-        @pl.loop(0, OWN)
-        def _(e):
-            for m in range(3):
-                keep(e, m, 0).wait()
-                for dy in range(1, NY):
-                    wait(grads.at[m, rem(y + dy, NY) * OWN + e], yrecv.at[e, m, dy])
-                    keep(e, m, dy).wait_send()
+                for at in range(NY):
+                    def both(copy):
+                        wait(grads.at[m, at * OWN + e], yrecv.at[e, m, at])
+                        copy.wait_send()
+
+                    keep(e, m, at, both, lambda copy: copy.wait())
             for way in (0, 1):
                 for kind in range(HOPS):
                     hop(e, way, kind).wait_send()
@@ -680,7 +720,7 @@
             gate_rows, gate_rows, v((NY, OWN, 3, d_loc, ff), BF16), v((NZ, NY, OWN, 3, d_loc, ff), BF16), v((OWN, 3, d_loc, ff), BF16),
             near(hidden), near(hidden), near(hidden), near(tok), near(ff), near(ff), near(ff), v((rows, 1), F32),
             near(hidden), per_expert, per_expert, v((GROUP, 8, tok), F32), v((tok, hidden), F32),
-            dma((2, NY * NX, 2)), dma((2, NY * NX)), dma((NZ, NY, 2, 2)), dma((len(RELAYS),)), dma((GROUP,)), dma((sends,)), dma((GROUP,)),
+            dma((2, NY * NX, 2)), dma((2, NY * NX, 2)), dma((NZ, NY, 2, 2)), dma((len(RELAYS),)), dma((GROUP,)), dma((sends,)), dma((GROUP,)),
             dma((5,)), dma((2, 4)),
             dma((4,)), dma((2, OWN, HOPS)), dma((2, OWN, HOPS)), dma((OWN, 3, NY)), dma((OWN, 3, NY)),
             dma((OWN,)), dma((OWN,)), dma((2, GROUP)), dma((1,)), pltpu.SemaphoreType.REGULAR,

time: 308 us -> 307 us (level)
  no operation moved by 1% of the time
where the time goes in v7:
time: 307 us
  Pallas kernels  306 us (100%)
    pallas_call x1, Pallas kernels, layer(): pl.pallas_call(functools.partial(layer_kernel, order, cap, cut, scope_one...  303 us

profile of v7, /device:TPU:1, one launch (start us, length us, event | category | flops | bytes accessed | tf_op | source)
XLA Modules:
  0.0 306.7 jit_solution(2031907822799324789)
XLA Ops:
  0.6 303.1 %layer.1 = (f32[3,16,32,384]{3,2,1,0:T(8,128)}, bf16[256,1024]{1,0:T(8,128)(2,1)}, f32[8,256]{1,0:T(8,128)}, bf16[32,96,1024]{2,1,0:T(8,128)(2,1)}, f32[4,32,256...) custom-call(bf16[256,1024]{1,0:T(8,128)(2,1)} %x_hbm.1, ...), custom_call_target="tpu_custom_call" | custom-call | tf_op jit(solution)/shard_map/layer/pallas_call | solution.py:709
  303.7 2.8 finish.1

commit v8 on v7

--- a/solution.py
+++ b/solution.py
@@ -13,7 +13,6 @@
 OWN = 4
 F32, BF16 = jnp.float32, jnp.bfloat16
 ANY = pl.BlockSpec(memory_space=pl.ANY)
-VMEM = pl.BlockSpec(memory_space=pltpu.VMEM)
 
 
 def capacity_of(tok_dev, top_k, experts):
@@ -86,7 +85,7 @@
 RATE, D2D, HOP = 46600.0, 400000.0, 2.3
 PUT, TILE, ROWS = 1.0, 1.0, 0.4
 STEP = 5
-AHEAD = 5.0
+AHEAD, MORE = 5.0, 0.2
 
 PIECE = {(0, None): (0, 1), (1, None): (1, 3), (1, 0): (1, 1), (1, 1): (2, 2)}
 RELAYS = ((0, None, "y+"), (1, 0, "y+"), (1, 1, "y-"))
@@ -110,7 +109,7 @@
         out = []
         for link, queue in pending.items():
             queue.sort()
-            while queue and free.get(link, 0.0) - now < AHEAD:
+            while queue and free.get(link, 0.0) - now < AHEAD + MORE * now:
                 out.append(send(now, *queue.pop(0)[-1]))
         return out
 
@@ -204,6 +203,10 @@
     return order
 
 
+def passed_on(dz, dy):
+    return dz != NZ // 2 and dz not in ((3,) if dy < 2 else (5,))
+
+
 def first_expert(d):
     return rem(d, NX * NC) * (NY * OWN) + d // (NX * NC) * OWN
 
@@ -211,9 +214,9 @@
 FAR, SUM3, NEW3, TWO, ONE, HOPS = 0, 1, 2, 3, 4, 10
 
 
-def layer_kernel(order, cap, cut, scope_one, scope_two, x_hbm, u_hbm, ids_ref, gates_ref, w1_hbm, w3_hbm, w2_hbm,
-                 grads, in_grad_ref, gate_ref, dxb, valb, dxs, xr, ur, gr, sel,
-                 metas, gates_out, wown, wv, relay, xb, ub, gb, sb, a_s, d1_s, d3_s, y_s, dx_s, val_s, vb, key_s, acc_s,
+def layer_kernel(order, cap, cut, scope_one, scope_two, x_hbm, u_hbm, ids_hbm, gates_hbm, w1_hbm, w3_hbm, w2_hbm,
+                 grads, in_grad_hbm, gate_hbm, dxb, valb, dxs, xr, ur, gr, sel,
+                 ids_ref, gates_ref, in_grad_ref, gate_ref, metas, gates_out, wown, wv, relay, xb, ub, gb, sb, a_s, d1_s, d3_s, y_s, dx_s, val_s, vb, key_s, acc_s,
                  recv, core_recv, wrecv, relay_recv, mrecv, send_sem, msend, load_sem, store_sem,
                  lsem, rsend, rrecv, ysend, yrecv, dsend, drecv, vsem, osem, in_scope):
     z, y, x, c = here()
@@ -233,6 +236,12 @@
 
     def wait(ref, sem):
         remote(ref, ref, send_sem.at[0], sem, targets["core"]).wait_recv()
+
+    def piece(dz, dy, group, part=None):
+        return wv.at[z_at(dz)["z"], rem(y + dy, NY), pl.ds(*PIECE[group, part])]
+
+    def wait_weights(dz, dy, group, part):
+        wait(piece(dz, dy, group, part), wrecv.at[dz, dy, group, part or 0])
 
     def w(e, m):
         return wv[:, :, e, m].reshape(hidden, ff)
@@ -268,9 +277,12 @@
         ]
         for m, ref in enumerate((w1_hbm, w3_hbm, w2_hbm)):
             loads.append(pltpu.make_async_copy(ref.reshape(NY, OWN, d_loc, ff), wown.at[:, :, m], load_sem.at[2 + m]))
-        for copy in loads:
+        tables = [pltpu.make_async_copy(a, b, load_sem.at[i]) for i, a, b in ((5, ids_hbm, ids_ref), (6, gates_hbm, gates_ref))]
+        for copy in tables + loads:
             copy.start()
         all_in = enter()
+        for copy in tables:
+            copy.wait()
 
         @pl.loop(0, GROUP)
         def _(d):
@@ -299,9 +311,6 @@
 
         def bsem(kind, dy, dx, part):
             return recv.at[0 if kind == "A" else 1, dy * NX + dx, part or 0]
-
-        def piece(dz, dy, group, part=None):
-            return wv.at[z_at(dz)["z"], rem(y + dy, NY), pl.ds(*PIECE[group, part])]
 
         row_copies = []
 
@@ -404,8 +413,10 @@
                 group, part, _ = RELAYS[name[1]]
                 wait(relay.at[pl.ds(*PIECE[group, part])], relay_recv.at[name[1]])
             elif name[0] == "W":
-                _, dz, dy, group, part = name
-                wait(piece(dz, dy, group, part), wrecv.at[dz, dy, group, part or 0])
+                if passed_on(*name[1:3]) or not name[3]:
+                    wait_weights(*name[1:])
+                else:
+                    last_weights.append(name[1:])
             else:
                 wait(block(*name), bsem(*name))
             for send in sends:
@@ -528,10 +539,18 @@
             def _(k):
                 dx_copy(e, k).start()
 
+        def far_sums(e):
+            for way in (0, 1):
+                hop(e, way, FAR).wait_recv()
+                add_into(r4.at[way, e], chunk(e, way, 3).at[way])
+                hop(e, way, SUM3).start()
+
         weight_gradients(0)
         for copy in row_loads(1):
             copy.start()
         send_back(0)
+        for name in last_weights:
+            wait_weights(*name)
 
         @pl.loop(1, OWN)
         def _(e):
@@ -550,6 +569,9 @@
                     copy.start()
 
             send_back(e)
+            far_sums(e - 1)
+
+        far_sums(OWN - 1)
 
         def val_copy(k):
             to = at_offset(k)
@@ -568,20 +590,15 @@
                 for way in (0, 1):
                     for kind in arrived:
                         hop(e, way, kind).wait_recv()
-                    mine = chunk(e, way, dist)
-                    if leaves == SUM3:
-                        add_into(r4.at[way, e], mine.at[way])
-                    elif leaves == TWO:
-                        add_into(r3.at[way, e], mine)
-                    if leaves < ONE:
-                        hop(e, way, leaves).start()
+                    if leaves == TWO:
+                        add_into(r3.at[way, e], chunk(e, way, dist))
+                        hop(e, way, TWO).start()
                 if leaves == ONE:
                     for kind in range(ONE, HOPS):
                         for way in (0, 1):
                             add_into(half_of(r2, way, e, kind), half_of(G, e, z_at(dist if way else NZ - dist)["z"], kind))
                             hop(e, way, kind).start()
 
-        step((FAR,), 3, SUM3)
         step((SUM3, NEW3), 2, TWO)
 
         group, places = dxb.shape[:2]
@@ -640,6 +657,9 @@
             return total
 
         gate_ref[...] = lax.fori_loop(0, group, gate_step, jnp.zeros(ids.shape, F32))
+        results = [pltpu.make_async_copy(a, b, load_sem.at[i]) for i, a, b in ((0, in_grad_ref, in_grad_hbm), (1, gate_ref, gate_hbm))]
+        for copy in results:
+            copy.start()
 
         step((TWO,), 1, ONE)
 
@@ -681,7 +701,10 @@
             sent = dxs.at[e, pl.ds(0, (GROUP - 1) * cap)]
             pltpu.make_async_copy(sent, sent, dsend.at[e]).wait()
 
-    weight_copies = []
+        for copy in results:
+            copy.wait()
+
+    weight_copies, last_weights = [], []
     pl.run_scoped(gather, *scope_one)
     pl.run_scoped(reduce, *scope_two)
     for number, group, part in weight_copies:
@@ -714,14 +737,14 @@
             shape((GROUP, OWN * cap, hidden), BF16), shape((OWN, GROUP, tok), F32), shape((OWN, rows, hidden), BF16),
             far(hidden), far(hidden), far(hidden), far(tok),
         ),
-        in_specs=[ANY, ANY, VMEM, VMEM, ANY, ANY, ANY],
-        out_specs=(ANY, VMEM, VMEM) + (ANY,) * 7,
+        in_specs=[ANY] * 7,
+        out_specs=(ANY,) * 10,
         scratch_shapes=[
-            gate_rows, gate_rows, v((NY, OWN, 3, d_loc, ff), BF16), v((NZ, NY, OWN, 3, d_loc, ff), BF16), v((OWN, 3, d_loc, ff), BF16),
+            v(ids.shape, ids.dtype), v(ids.shape, F32), v((tok, hidden), BF16), v(ids.shape, F32), gate_rows, gate_rows, v((NY, OWN, 3, d_loc, ff), BF16), v((NZ, NY, OWN, 3, d_loc, ff), BF16), v((OWN, 3, d_loc, ff), BF16),
             near(hidden), near(hidden), near(hidden), near(tok), near(ff), near(ff), near(ff), v((rows, 1), F32),
             near(hidden), per_expert, per_expert, v((GROUP, 8, tok), F32), v((tok, hidden), F32),
             dma((2, NY * NX, 2)), dma((2, NY * NX, 2)), dma((NZ, NY, 2, 2)), dma((len(RELAYS),)), dma((GROUP,)), dma((sends,)), dma((GROUP,)),
-            dma((5,)), dma((2, 4)),
+            dma((7,)), dma((2, 4)),
             dma((4,)), dma((2, OWN, HOPS)), dma((2, OWN, HOPS)), dma((OWN, 3, NY)), dma((OWN, 3, NY)),
             dma((OWN,)), dma((OWN,)), dma((2, GROUP)), dma((1,)), pltpu.SemaphoreType.REGULAR,
         ],

time: 307 us -> 306 us (level)
  no operation moved by 1% of the time
where the time goes in v8:
time: 306 us
  Pallas kernels  305 us (100%)
    pallas_call x1, Pallas kernels, layer(): pl.pallas_call(functools.partial(layer_kernel, order, cap, cut, scope_one...  302 us

profile of v8, /device:TPU:1, one launch (start us, length us, event | category | flops | bytes accessed | tf_op | source)
XLA Modules:
  0.0 305.6 jit_solution(11193686035725739508)
XLA Ops:
  0.6 301.9 %layer.1 = (f32[3,16,32,384]{3,2,1,0:T(8,128)}, bf16[256,1024]{1,0:T(8,128)(2,1)}, f32[8,256]{1,0:T(8,128)}, bf16[32,96,1024]{2,1,0:T(8,128)(2,1)}, f32[4,32,256...) custom-call(bf16[256,1024]{1,0:T(8,128)(2,1)} %x_hbm.1, ...), custom_call_target="tpu_custom_call" | custom-call | tf_op jit(solution)/shard_map/layer/pallas_call | solution.py:732
  302.6 2.8 finish.1

commit v9 on v8

--- a/solution.py
+++ b/solution.py
@@ -82,28 +82,30 @@
     return lambda: pl.semaphore_wait(barrier, GROUP + 1)
 
 
-RATE, D2D, HOP = 46600.0, 400000.0, 2.3
+RATE, D2D, HOP = 44700.0, 400000.0, 2.3
 PUT, TILE, ROWS = 1.0, 1.0, 0.4
 STEP = 5
-AHEAD, MORE = 5.0, 0.2
+AHEAD, MORE = 5.0, 0.05
 
 PIECE = {(0, None): (0, 1), (1, None): (1, 3), (1, 0): (1, 1), (1, 1): (2, 2)}
 RELAYS = ((0, None, "y+"), (1, 0, "y+"), (1, 1, "y-"))
 
 
-def gather_order(rows_bytes, cut, expert_bytes):
-    size = {"A": rows_bytes * cut, "B": rows_bytes * (1.0 - cut)}
+KINDS = ("A0", "A1", "B0", "B1")
+
+
+def gather_order(sizes, expert_bytes):
     free, pending, coming, order, have, ready = {}, {}, [], [], {}, {}
 
-    def send(now, name, part, link, arrives, nbytes):
+    def send(now, name, link, arrives, nbytes):
         t = max(now, free.get(link, 0.0)) + nbytes / (D2D if link == "core" else RATE)
         free[link] = t
         coming.append((t + HOP, len(order), len(coming), arrives))
-        return (name, part, link)
-
-    def later(rank, name, part, link, arrives, nbytes):
+        return (name, link)
+
+    def later(rank, name, link, arrives, nbytes):
         queue = pending.setdefault(link, [])
-        queue.append((rank, len(order), len(queue), (name, part, link, arrives, nbytes)))
+        queue.append((rank, len(order), len(queue), (name, link, arrives, nbytes)))
 
     def turn(now):
         out = []
@@ -114,29 +116,21 @@
         return out
 
     def on_rows(kind, dy, dx):
-        first, second = "xy" if kind == "A" else "yx"
+        first, second = "xy" if kind[0] == "A" else "yx"
         d = {"x": dx, "y": dy}
-
-        def go(axis, sign, part):
-            nd = dict(d)
-            nd[axis] = (d[axis] - sign) % 4
-            rank = 4 + (axis == second) + (part is not None)
-            later(rank, (kind, dy, dx), part, axis + "-+"[sign > 0], (kind, nd["y"], nd["x"], part), size[kind] / (1 if part is None else 2))
-
         for axis in [first, second] if d[second] == 0 else [second]:
-            if d[axis] == 3:
-                go(axis, 1, 0)
-            elif d[axis] == 1:
-                go(axis, -1, 1)
-            elif d[axis] == 0:
-                go(axis, 1, None)
-                go(axis, -1, None)
-
-    def core(now, key, part):
-        return send(now, key, part, "core", ("core",) + key + (part,), size[key[0]] / (1 if part is None else 2))
+            for sign in (1, -1):
+                if d[axis] == 0 or d[axis] == -sign % 4 and kind[1] == "10"[sign > 0]:
+                    nd = dict(d)
+                    nd[axis] = (d[axis] - sign) % 4
+                    rank = 4 + (axis == second) + (d[axis] != 0)
+                    later(rank, (kind, dy, dx), axis + "-+"[sign > 0], (kind, nd["y"], nd["x"]), sizes[kind])
+
+    def core(now, key):
+        return send(now, key, "core", ("core",) + key, sizes[key[0]])
 
     def weights(rank, name, group, part, link, arrives):
-        later(rank, name, part, link, arrives + (group, part), PIECE[group, part][1] * expert_bytes)
+        later(rank, name, link, arrives + (group, part), PIECE[group, part][1] * expert_bytes)
 
     def on_piece(dz, dy, group):
         for link, step, far in (("z+", -1, dy < 2), ("z-", 1, dy >= 2)):
@@ -144,7 +138,7 @@
             if gone < 3 + far:
                 weights(4 * group + gone, ("W", dz, dy, group), group, None, link, ("W", (dz + step) % NZ, dy))
 
-    def arrived(key, part):
+    def arrived(key, part=None):
         have[key] = have.get(key, 0) + (2 if part is None else 1)
         if have[key] == 2:
             ready[key] = True
@@ -157,17 +151,17 @@
             weights(2, ("w", dy, group), group, None, link, ("W", 0, (-dy) % NY))
         on_piece(0, 0, group)
     sends = []
-    for kind in "BA":
-        arrived((kind, 0, 0), None)
+    for kind in KINDS[::-1]:
+        arrived((kind, 0, 0))
         on_rows(kind, 0, 0)
-        sends.append(core(0.0, (kind, 0, 0), None))
+        sends.append(core(0.0, (kind, 0, 0)))
     order.append((None, turn(0.0) + sends))
     todo, puts, done, now = [(dy, dx) for dy in range(NY) for dx in range(NX)], 0, 0, 0.0
     while coming or todo or done < puts:
         coming.sort()
         soon = coming[0][0] if coming else 1e9
         if soon > now:
-            place = next((p for p in todo if all(pre + (kind,) + p in ready for kind in "AB" for pre in ((), ("core",)))), None)
+            place = next((p for p in todo if all(pre + (kind,) + p in ready for kind in KINDS for pre in ((), ("core",)))), None)
             if place is not None:
                 todo.remove(place)
                 order.append((("put",) + place, turn(now)))
@@ -183,9 +177,8 @@
                 continue
         t, _, _, name = coming.pop(0)
         now = max(now, t)
-        key, part = name[:-1], name[-1]
         if name[0] == "core":
-            arrived(key, part)
+            arrived(name)
             continue
         sends = []
         if name[0] == "R":
@@ -193,12 +186,12 @@
             weights(1, name[:2], group, part, RELAYS[i][2], ("W", 0, 2))
             name = name[:2]
         elif name[0] == "W":
-            if arrived(key, part):
-                on_piece(*key[1:])
+            if arrived(name[:-1], name[-1]):
+                on_piece(*name[1:-1])
         else:
-            sends = [core(now, key, part)]
-            if arrived(key, part):
-                on_rows(*key)
+            sends = [core(now, name)]
+            arrived(name)
+            on_rows(*name)
         order.append((name, sends + turn(now)))
     return order
 
@@ -214,7 +207,7 @@
 FAR, SUM3, NEW3, TWO, ONE, HOPS = 0, 1, 2, 3, 4, 10
 
 
-def layer_kernel(order, cap, cut, scope_one, scope_two, x_hbm, u_hbm, ids_hbm, gates_hbm, w1_hbm, w3_hbm, w2_hbm,
+def layer_kernel(order, cap, spans, scope_one, scope_two, x_hbm, u_hbm, ids_hbm, gates_hbm, w1_hbm, w3_hbm, w2_hbm,
                  grads, in_grad_hbm, gate_hbm, dxb, valb, dxs, xr, ur, gr, sel,
                  ids_ref, gates_ref, in_grad_ref, gate_ref, metas, gates_out, wown, wv, relay, xb, ub, gb, sb, a_s, d1_s, d3_s, y_s, dx_s, val_s, vb, key_s, acc_s,
                  recv, core_recv, wrecv, relay_recv, mrecv, send_sem, msend, load_sem, store_sem,
@@ -300,21 +293,12 @@
         all_in()
 
         back = {"x+": (0, 3), "x-": (0, 1), "y+": (3, 0), "y-": (1, 0)}
-        spans = {"A": (0, cut), "B": (cut, 2 * tok - cut)}
-
-        def block(kind, dy, dx, part=None, dc=0):
-            start, size = spans[kind]
-            if part is not None:
-                size //= 2
-                start += part * size
-            return all_rows.at[place(dy, dx, dc), pl.ds(start, size)]
-
-        def bsem(kind, dy, dx, part):
-            return recv.at[0 if kind == "A" else 1, dy * NX + dx, part or 0]
+        def block(kind, dy, dx, dc=0):
+            return all_rows.at[place(dy, dx, dc), pl.ds(*spans[kind])]
 
         row_copies = []
 
-        def issue(name, part, link):
+        def issue(name, link):
             number = len(row_copies) + len(weight_copies)
             sem = send_sem.at[number]
             group, part_of = None, None
@@ -337,12 +321,10 @@
                 copy = remote(own if dz == dy == 0 else piece(dz, dy, group), piece(dz, dy, group), sem, wrecv.at[ndz, dy, group, 0], targets[link])
             else:
                 kind, dy, dx = name
-                ref = block(kind, dy, dx, part)
-                if link == "core":
-                    rsem = core_recv.at[0 if kind == "A" else 1, dy * NX + dx, part or 0]
-                else:
-                    oy, ox = back[link]
-                    rsem = bsem(kind, (dy + oy) % NY, (dx + ox) % NX, part)
+                ref = block(*name)
+                oy, ox = back.get(link, (0, 0))
+                arrivals = core_recv if link == "core" else recv
+                rsem = arrivals.at[KINDS.index(kind), (dy + oy) % NY * NX + (dx + ox) % NX]
                 copy = remote(ref, ref, sem, rsem, targets[link])
             copy.start()
             if group is None:
@@ -366,9 +348,8 @@
                 if dy or dx or dc:
                     k = ((-dy) % NY) * (NX * NC) + ((-dx) % NX) * NC + dc
                     wait(metas.at[place(dy, dx, dc)], mrecv.at[k])
-            for i, (kind, last) in enumerate((("A", dx if dy == 0 else dy), ("B", dy if dx == 0 else dx))):
-                for part in (0, 1) if last == 2 else (None,):
-                    wait(block(kind, dy, dx, part, 1), core_recv.at[i, dy * NX + dx, part or 0])
+            for i, kind in enumerate(KINDS):
+                wait(block(kind, dy, dx, 1), core_recv.at[i, dy * NX + dx])
             chip = rem(y + dy, NY) * NX + rem(x + dx, NX)
             n = 2 * OWN
             which = lax.broadcasted_iota(jnp.int32, (n, tok), 0)
@@ -418,7 +399,8 @@
                 else:
                     last_weights.append(name[1:])
             else:
-                wait(block(*name), bsem(*name))
+                kind, dy, dx = name
+                wait(block(*name), recv.at[KINDS.index(kind), dy * NX + dx])
             for send in sends:
                 issue(*send)
             if name is None:
@@ -718,7 +700,9 @@
     rows = GROUP * cap
     half = hidden // NZ // 2
     cut = tok - tok // 8 if tok % 256 == 0 else tok
-    order = gather_order(4 * tok * hidden, cut / (2 * tok), 2 * w1.size * 3 // local_experts)
+    halves = [cut // 2] * 2 + [tok - cut // 2] * 2
+    spans = {kind: (sum(halves[:i]), halves[i]) for i, kind in enumerate(KINDS)}
+    order = gather_order({kind: 2 * hidden * n for kind, (_, n) in spans.items()}, 2 * w1.size * 3 // local_experts)
     sends = sum(len(s) for _, s in order)
     dma, v, shape = pltpu.SemaphoreType.DMA, pltpu.VMEM, jax.ShapeDtypeStruct
     far = lambda lanes: shape((OWN - 1, rows, lanes), BF16)
@@ -730,7 +714,7 @@
     per_expert = v((OWN, GROUP, tok), F32)
     gate_rows = v((GROUP, OWN, tok), F32)
     outs = pl.pallas_call(
-        functools.partial(layer_kernel, order, cap, cut, scope_one, scope_two),
+        functools.partial(layer_kernel, order, cap, spans, scope_one, scope_two),
         name="layer",
         out_shape=(
             shape((3, local_experts, d_loc, ff), F32), shape((tok, hidden), BF16), shape(ids.shape, F32),
@@ -743,7 +727,7 @@
             v(ids.shape, ids.dtype), v(ids.shape, F32), v((tok, hidden), BF16), v(ids.shape, F32), gate_rows, gate_rows, v((NY, OWN, 3, d_loc, ff), BF16), v((NZ, NY, OWN, 3, d_loc, ff), BF16), v((OWN, 3, d_loc, ff), BF16),
             near(hidden), near(hidden), near(hidden), near(tok), near(ff), near(ff), near(ff), v((rows, 1), F32),
             near(hidden), per_expert, per_expert, v((GROUP, 8, tok), F32), v((tok, hidden), F32),
-            dma((2, NY * NX, 2)), dma((2, NY * NX, 2)), dma((NZ, NY, 2, 2)), dma((len(RELAYS),)), dma((GROUP,)), dma((sends,)), dma((GROUP,)),
+            dma((len(KINDS), NY * NX)), dma((len(KINDS), NY * NX)), dma((NZ, NY, 2, 2)), dma((len(RELAYS),)), dma((GROUP,)), dma((sends,)), dma((GROUP,)),
             dma((7,)), dma((2, 4)),
             dma((4,)), dma((2, OWN, HOPS)), dma((2, OWN, HOPS)), dma((OWN, 3, NY)), dma((OWN, 3, NY)),
             dma((OWN,)), dma((OWN,)), dma((2, GROUP)), dma((1,)), pltpu.SemaphoreType.REGULAR,

time: 306 us -> 305 us (level)
  no operation moved by 1% of the time
where the time goes in v9:
time: 305 us
  Pallas kernels  304 us (100%)
    pallas_call x1, Pallas kernels, layer(): pl.pallas_call(functools.partial(layer_kernel, order, cap, spans, scope_o...  301 us

profile of v9, /device:TPU:1, one launch (start us, length us, event | category | flops | bytes accessed | tf_op | source)
XLA Modules:
  0.0 305.1 jit_solution(16870528660448852824)
XLA Ops:
  0.6 301.5 %layer.1 = (f32[3,16,32,384]{3,2,1,0:T(8,128)}, bf16[256,1024]{1,0:T(8,128)(2,1)}, f32[8,256]{1,0:T(8,128)}, bf16[32,96,1024]{2,1,0:T(8,128)(2,1)}, f32[4,32,256...) custom-call(bf16[256,1024]{1,0:T(8,128)(2,1)} %x_hbm.1, ...), custom_call_target="tpu_custom_call" | custom-call | tf_op jit(solution)/shard_map/layer/pallas_call | solution.py:716
  302.1 2.8 finish.1

commit v10 on v9

--- a/solution.py
+++ b/solution.py
@@ -70,16 +70,9 @@
     copy.start()
 
 
-def enter():
-    barrier = pltpu.get_barrier_semaphore()
-
-    @each_other
-    def _(k):
-        pl.semaphore_signal(barrier, device_id=at_offset(k), device_id_type=pl.DeviceIdType.MESH)
-
-    for dz in (1, NZ - 1):
-        pl.semaphore_signal(barrier, device_id=z_at(dz), device_id_type=pl.DeviceIdType.MESH)
-    return lambda: pl.semaphore_wait(barrier, GROUP + 1)
+def tell(semaphore, targets):
+    for target in targets:
+        pl.semaphore_signal(semaphore, device_id=target, device_id_type=pl.DeviceIdType.MESH)
 
 
 RATE, D2D, HOP = 44700.0, 400000.0, 2.3
@@ -100,7 +93,7 @@
     def send(now, name, link, arrives, nbytes):
         t = max(now, free.get(link, 0.0)) + nbytes / (D2D if link == "core" else RATE)
         free[link] = t
-        coming.append((t + HOP, len(order), len(coming), arrives))
+        coming.append((t + (HOP / 2 if link == "core" else HOP), len(order), len(coming), arrives))
         return (name, link)
 
     def later(rank, name, link, arrives, nbytes):
@@ -170,7 +163,8 @@
                 continue
             step = min(STEP, puts - done)
             weights_in = sum(key[0] == "W" and key[-1] == 0 for key in ready) == NZ * NY - 1
-            if weights_in and (step >= 3 and soon - now > TILE or not todo):
+            calm = all(c[-1][0] == "core" for c in coming)
+            if weights_in and step and (step >= 3 and soon - now > TILE or calm):
                 order.append((("tile", done, done + step), turn(now)))
                 done += step
                 now += TILE + ROWS * step
@@ -204,14 +198,14 @@
     return rem(d, NX * NC) * (NY * OWN) + d // (NX * NC) * OWN
 
 
-FAR, SUM3, NEW3, TWO, ONE, HOPS = 0, 1, 2, 3, 4, 10
+FAR, SUM3, NEW3, TWO, ONE, HOPS = 0, 1, 2, 3, 4, 16
 
 
 def layer_kernel(order, cap, spans, scope_one, scope_two, x_hbm, u_hbm, ids_hbm, gates_hbm, w1_hbm, w3_hbm, w2_hbm,
                  grads, in_grad_hbm, gate_hbm, dxb, valb, dxs, xr, ur, gr, sel,
                  ids_ref, gates_ref, in_grad_ref, gate_ref, metas, gates_out, wown, wv, relay, xb, ub, gb, sb, a_s, d1_s, d3_s, y_s, dx_s, val_s, vb, key_s, acc_s,
                  recv, core_recv, wrecv, relay_recv, mrecv, send_sem, msend, load_sem, store_sem,
-                 lsem, rsend, rrecv, ysend, yrecv, dsend, drecv, vsem, osem, in_scope):
+                 lsem, rsend, rrecv, ysend, yrecv, dsend, drecv, vsem, osem, in_scope, in_plane):
     z, y, x, c = here()
     tok, hidden = x_hbm.shape
     rows, ff = xb.shape[0], a_s.shape[-1]
@@ -273,7 +267,8 @@
         tables = [pltpu.make_async_copy(a, b, load_sem.at[i]) for i, a, b in ((5, ids_hbm, ids_ref), (6, gates_hbm, gates_ref))]
         for copy in tables + loads:
             copy.start()
-        all_in = enter()
+        barrier = pltpu.get_barrier_semaphore()
+        tell(barrier, targets.values())
         for copy in tables:
             copy.wait()
 
@@ -290,7 +285,7 @@
         tri[...] = strict_upper(tok)
         for copy in loads:
             copy.wait()
-        all_in()
+        pl.semaphore_wait(barrier, len(targets))
 
         back = {"x+": (0, 3), "x-": (0, 1), "y+": (3, 0), "y-": (1, 0)}
         def block(kind, dy, dx, dc=0):
@@ -405,6 +400,10 @@
                 issue(*send)
             if name is None:
                 wv[z, y] = wown[y]
+                near = [t for link, t in targets.items() if link[0] != "z"]
+                for far in range(NY // 2 + NX // 2):
+                    tell(in_plane.at[far], near)
+                    pl.semaphore_wait(in_plane.at[far], len(near))
 
                 @each_other
                 def _(k):
@@ -422,8 +421,7 @@
             copy.wait_send()
 
     def reduce(G, r4, r3, r2, r1):
-        for dz in (1, NZ - 1):
-            pl.semaphore_signal(in_scope, device_id=z_at(dz), device_id_type=pl.DeviceIdType.MESH)
+        tell(in_scope, [targets["z+"], targets["z-"]])
 
         def row_loads(e):
             pairs = ((xr, xb), (gr, gb), (ur, ub), (sel, sb))
@@ -432,8 +430,9 @@
         def chunk(e, way, dist):
             return G.at[e, z_at(dist if way else NZ - dist)["z"]]
 
-        def half_of(ref, way, e, kind):
-            return ref.at[way, e, (kind - ONE) % 2, (kind - ONE) // 2]
+        def part_of(ref, way, e, kind):
+            m, q = (kind - ONE) // NY, (kind - ONE) % NY
+            return ref.at[way, e, q // 2, m, pl.ds(q % 2 * d_loc, d_loc)]
 
         def hop(e, way, kind):
             h = way
@@ -442,7 +441,7 @@
                 SUM3: lambda: (r4.at[way, e], r3.at[way, e, h]),
                 NEW3: lambda: (chunk(e, way, 3).at[1 - h], r3.at[way, e, 1 - h]),
                 TWO: lambda: (r3.at[way, e], r2.at[way, e]),
-            }.get(kind, lambda: (half_of(r2, way, e, kind), half_of(r1, way, e, kind)))()
+            }.get(kind, lambda: (part_of(r2, way, e, kind), part_of(r1, way, e, kind)))()
             return remote(src, dst, rsend.at[way, e, kind], rrecv.at[way, e, kind], z_at(1 if way else NZ - 1))
 
         def add_into(dst, *others):
@@ -578,7 +577,7 @@
                 if leaves == ONE:
                     for kind in range(ONE, HOPS):
                         for way in (0, 1):
-                            add_into(half_of(r2, way, e, kind), half_of(G, e, z_at(dist if way else NZ - dist)["z"], kind))
+                            add_into(part_of(r2, way, e, kind), part_of(G, e, z_at(dist if way else NZ - dist)["z"], kind))
                             hop(e, way, kind).start()
 
         step((SUM3, NEW3), 2, TWO)
@@ -646,7 +645,7 @@
         step((TWO,), 1, ONE)
 
         def keep(e, m, to, then_remote, then_local):
-            src = r1.at[0, e, to // 2, m, pl.ds(to % 2 * d_loc, d_loc)]
+            src = part_of(r1, 0, e, ONE + NY * m + to)
             dst = grads.at[m, y * OWN + e]
 
             @pl.when(y != to)
@@ -662,10 +661,8 @@
             for kind in range(ONE, HOPS):
                 for way in (0, 1):
                     hop(e, way, kind).wait_recv()
-                add_into(half_of(r1, 0, e, kind), half_of(r1, 1, e, kind), half_of(G, e, z, kind))
-                m, h = (kind - ONE) // 2, (kind - ONE) % 2
-                for to in (2 * h, 2 * h + 1):
-                    keep(e, m, to, start, start)
+                add_into(part_of(r1, 0, e, kind), part_of(r1, 1, e, kind), part_of(G, e, z, kind))
+                keep(e, (kind - ONE) // NY, (kind - ONE) % NY, start, start)
 
         @pl.loop(0, OWN)
         def _(e):
@@ -730,7 +727,7 @@
             dma((len(KINDS), NY * NX)), dma((len(KINDS), NY * NX)), dma((NZ, NY, 2, 2)), dma((len(RELAYS),)), dma((GROUP,)), dma((sends,)), dma((GROUP,)),
             dma((7,)), dma((2, 4)),
             dma((4,)), dma((2, OWN, HOPS)), dma((2, OWN, HOPS)), dma((OWN, 3, NY)), dma((OWN, 3, NY)),
-            dma((OWN,)), dma((OWN,)), dma((2, GROUP)), dma((1,)), pltpu.SemaphoreType.REGULAR,
+            dma((OWN,)), dma((OWN,)), dma((2, GROUP)), dma((1,)), pltpu.SemaphoreType.REGULAR, pltpu.SemaphoreType.REGULAR((NY // 2 + NX // 2,)),
         ],
         compiler_params=params(0),
     )(x, u, ids, gates, w1, w3, w2)
@@ -741,13 +738,18 @@
     n = 5
     outs, bufs, sems = refs[:n], refs[n:2 * n], refs[-1]
     ins = [grads.at[m] for m in range(3)] + [in_grad, gate]
-    load = [pltpu.make_async_copy(a, b, sems.at[0, i]) for i, (a, b) in enumerate(zip(ins, bufs))]
-    store = [pltpu.make_async_copy(b, o, sems.at[1, i]) for i, (b, o) in enumerate(zip(bufs, outs))]
+    load, store = [], []
+    for i, (a, b, o) in enumerate(zip(ins, bufs, outs)):
+        half = a.shape[0] // 2
+        for h in range(2):
+            at = pl.ds(h * half, half)
+            load.append(pltpu.make_async_copy(a.at[at], b.at[at], sems.at[0, i, h]))
+            store.append(pltpu.make_async_copy(b.at[at], o.at[at], sems.at[1, i, h]))
     for copy in load:
         copy.start()
-    for i in range(n):
-        load[i].wait()
-        store[i].start()
+    for before, after in zip(load, store):
+        before.wait()
+        after.start()
     for copy in store:
         copy.wait()
 
@@ -761,7 +763,7 @@
         out_shape=[jax.ShapeDtypeStruct(s, t) for s, t in zip(shapes, types)],
         in_specs=[ANY] * 3,
         out_specs=[ANY] * len(shapes),
-        scratch_shapes=[pltpu.VMEM(s, t) for s, t in zip(shapes, types)] + [pltpu.SemaphoreType.DMA((2, len(shapes)))],
+        scratch_shapes=[pltpu.VMEM(s, t) for s, t in zip(shapes, types)] + [pltpu.SemaphoreType.DMA((2, len(shapes), 2))],
     )(grads, in_grad, gate)
 
 

time: 305 us -> 307 us (level)
  no operation moved by 1% of the time
where the time goes in v10:
time: 307 us; the launch traced here: 306 us
  Pallas kernels  305 us (99%)
    pallas_call x1, Pallas kernels, layer(): pl.pallas_call(functools.partial(layer_kernel, order, cap, spans, scope_o...  302 us

profile of v10, /device:TPU:1, one launch (start us, length us, event | category | flops | bytes accessed | tf_op | source)
XLA Modules:
  0.0 305.8 jit_solution(5046672545347656687)
XLA Ops:
  0.6 302.3 %layer.1 = (f32[3,16,32,384]{3,2,1,0:T(8,128)}, bf16[256,1024]{1,0:T(8,128)(2,1)}, f32[8,256]{1,0:T(8,128)}, bf16[32,96,1024]{2,1,0:T(8,128)(2,1)}, f32[4,32,256...) custom-call(bf16[256,1024]{1,0:T(8,128)(2,1)} %x_hbm.1, ...), custom_call_target="tpu_custom_call" | custom-call | tf_op jit(solution)/shard_map/layer/pallas_call | solution.py:713
  302.9 2.7 finish.1

commit v11 on v10

--- a/solution.py
+++ b/solution.py
@@ -198,7 +198,7 @@
     return rem(d, NX * NC) * (NY * OWN) + d // (NX * NC) * OWN
 
 
-FAR, SUM3, NEW3, TWO, ONE, HOPS = 0, 1, 2, 3, 4, 16
+FAR, SUM3, NEW3, TWO, ONE, PART, HOPS = 0, 1, 2, 3, 4, 5, 11
 
 
 def layer_kernel(order, cap, spans, scope_one, scope_two, x_hbm, u_hbm, ids_hbm, gates_hbm, w1_hbm, w3_hbm, w2_hbm,
@@ -431,8 +431,7 @@
             return G.at[e, z_at(dist if way else NZ - dist)["z"]]
 
         def part_of(ref, way, e, kind):
-            m, q = (kind - ONE) // NY, (kind - ONE) % NY
-            return ref.at[way, e, q // 2, m, pl.ds(q % 2 * d_loc, d_loc)]
+            return ref.at[way, e, (kind - PART) % 2, (kind - PART) // 2]
 
         def hop(e, way, kind):
             h = way
@@ -441,6 +440,7 @@
                 SUM3: lambda: (r4.at[way, e], r3.at[way, e, h]),
                 NEW3: lambda: (chunk(e, way, 3).at[1 - h], r3.at[way, e, 1 - h]),
                 TWO: lambda: (r3.at[way, e], r2.at[way, e]),
+                ONE: lambda: (r2.at[way, e], r1.at[way, e]),
             }.get(kind, lambda: (part_of(r2, way, e, kind), part_of(r1, way, e, kind)))()
             return remote(src, dst, rsend.at[way, e, kind], rrecv.at[way, e, kind], z_at(1 if way else NZ - 1))
 
@@ -565,22 +565,13 @@
         def _(k):
             val_copy(k).start()
 
-        def step(arrived, dist, leaves):
-            @pl.loop(0, OWN)
-            def _(e):
-                for way in (0, 1):
-                    for kind in arrived:
-                        hop(e, way, kind).wait_recv()
-                    if leaves == TWO:
-                        add_into(r3.at[way, e], chunk(e, way, dist))
-                        hop(e, way, TWO).start()
-                if leaves == ONE:
-                    for kind in range(ONE, HOPS):
-                        for way in (0, 1):
-                            add_into(part_of(r2, way, e, kind), part_of(G, e, z_at(dist if way else NZ - dist)["z"], kind))
-                            hop(e, way, kind).start()
-
-        step((SUM3, NEW3), 2, TWO)
+        @pl.loop(0, OWN)
+        def _(e):
+            for way in (0, 1):
+                for kind in (SUM3, NEW3):
+                    hop(e, way, kind).wait_recv()
+                add_into(r3.at[way, e], chunk(e, way, 2))
+                hop(e, way, TWO).start()
 
         group, places = dxb.shape[:2]
         ids = ids_ref[...].astype(F32)
@@ -642,44 +633,72 @@
         for copy in results:
             copy.start()
 
-        step((TWO,), 1, ONE)
+        last = OWN - 1
+
+        @pl.loop(0, last)
+        def _(e):
+            for way in (0, 1):
+                hop(e, way, TWO).wait_recv()
+                add_into(r2.at[way, e], chunk(e, way, 1))
+                hop(e, way, ONE).start()
+
+        for way in (0, 1):
+            hop(last, way, TWO).wait_recv()
+        for kind in range(PART, HOPS):
+            for way in (0, 1):
+                add_into(part_of(r2, way, last, kind), part_of(G, last, z_at(1 if way else NZ - 1)["z"], kind))
+                hop(last, way, kind).start()
 
         def keep(e, m, to, then_remote, then_local):
-            src = part_of(r1, 0, e, ONE + NY * m + to)
+            src = r1.at[0, e, to // 2, m, pl.ds(to % 2 * d_loc, d_loc)]
             dst = grads.at[m, y * OWN + e]
+            n = 0 if isinstance(m, slice) else m
 
             @pl.when(y != to)
             def _():
-                then_remote(remote(src, dst, ysend.at[e, m, to], yrecv.at[e, m, y], {"y": to}))
+                then_remote(remote(src, dst, ysend.at[e, n, to], yrecv.at[e, n, y], {"y": to}))
 
             @pl.when(y == to)
             def _():
-                then_local(pltpu.make_async_copy(src, dst, ysend.at[e, m, to]))
-
-        @pl.loop(0, OWN)
+                then_local(pltpu.make_async_copy(src, dst, ysend.at[e, n, to]))
+
+        every = slice(None)
+
+        @pl.loop(0, last)
         def _(e):
-            for kind in range(ONE, HOPS):
-                for way in (0, 1):
-                    hop(e, way, kind).wait_recv()
-                add_into(part_of(r1, 0, e, kind), part_of(r1, 1, e, kind), part_of(G, e, z, kind))
-                keep(e, (kind - ONE) // NY, (kind - ONE) % NY, start, start)
-
-        @pl.loop(0, OWN)
-        def _(e):
-            for m in range(3):
+            for way in (0, 1):
+                hop(e, way, ONE).wait_recv()
+            add_into(r1.at[0, e], r1.at[1, e], G.at[e, z])
+            for to in range(NY):
+                keep(e, every, to, start, start)
+
+        for kind in range(PART, HOPS):
+            for way in (0, 1):
+                hop(last, way, kind).wait_recv()
+            add_into(part_of(r1, 0, last, kind), part_of(r1, 1, last, kind), part_of(G, last, z, kind))
+            m, h = (kind - PART) // 2, (kind - PART) % 2
+            for to in (2 * h, 2 * h + 1):
+                keep(last, m, to, start, start)
+
+        def finish_up(e, kinds, matrices):
+            for m in matrices:
                 for at in range(NY):
                     def both(copy):
-                        wait(grads.at[m, at * OWN + e], yrecv.at[e, m, at])
+                        wait(grads.at[m, at * OWN + e], yrecv.at[e, 0 if m is every else m, at])
                         copy.wait_send()
 
                     keep(e, m, at, both, lambda copy: copy.wait())
             for way in (0, 1):
-                for kind in range(HOPS):
+                for kind in kinds:
                     hop(e, way, kind).wait_send()
-
             sent = dxs.at[e, pl.ds(0, (GROUP - 1) * cap)]
             pltpu.make_async_copy(sent, sent, dsend.at[e]).wait()
 
+        @pl.loop(0, last)
+        def _(e):
+            finish_up(e, range(PART), [every])
+
+        finish_up(last, [FAR, SUM3, NEW3, TWO, *range(PART, HOPS)], range(3))
         for copy in results:
             copy.wait()
 

time: 307 us -> 306 us (level)
  no operation moved by 1% of the time
where the time goes in v11:
time: 306 us; the launch traced here: 305 us
  Pallas kernels  304 us (99%)
    pallas_call x1, Pallas kernels, layer(): pl.pallas_call(functools.partial(layer_kernel, order, cap, spans, scope_o...  302 us

profile of v11, /device:TPU:1, one launch (start us, length us, event | category | flops | bytes accessed | tf_op | source)
XLA Modules:
  0.0 305.2 jit_solution(11134292449869421347)
XLA Ops:
  0.6 301.6 %layer.1 = (f32[3,16,32,384]{3,2,1,0:T(8,128)}, bf16[256,1024]{1,0:T(8,128)(2,1)}, f32[8,256]{1,0:T(8,128)}, bf16[32,96,1024]{2,1,0:T(8,128)(2,1)}, f32[4,32,256...) custom-call(bf16[256,1024]{1,0:T(8,128)(2,1)} %x_hbm.1, ...), custom_call_target="tpu_custom_call" | custom-call | tf_op jit(solution)/shard_map/layer/pallas_call | solution.py:732
  302.3 2.7 finish.1

commit v12 on v11

--- a/solution.py
+++ b/solution.py
@@ -269,20 +269,22 @@
             copy.start()
         barrier = pltpu.get_barrier_semaphore()
         tell(barrier, targets.values())
-        for copy in tables:
-            copy.wait()
-
-        @pl.loop(0, GROUP)
-        def _(d):
-            number = first_expert(d) + lax.broadcasted_iota(jnp.int32, (OWN, tok), 0)
-            value = jnp.full((OWN, tok), -1.0, F32)
-            for j in range(ids_ref.shape[0]):
-                chosen = ids_ref[pl.ds(j, 1), :] == number
-                value = jnp.where(chosen, jnp.broadcast_to(gates_ref[pl.ds(j, 1), :], value.shape), value)
-            gates_out[d] = value
-
-        metas[me] = gates_out[me]
-        tri[...] = strict_upper(tok)
+        def make_tables():
+            for copy in tables:
+                copy.wait()
+
+            @pl.loop(0, GROUP)
+            def _(d):
+                number = first_expert(d) + lax.broadcasted_iota(jnp.int32, (OWN, tok), 0)
+                value = jnp.full((OWN, tok), -1.0, F32)
+                for j in range(ids_ref.shape[0]):
+                    chosen = ids_ref[pl.ds(j, 1), :] == number
+                    value = jnp.where(chosen, jnp.broadcast_to(gates_ref[pl.ds(j, 1), :], value.shape), value)
+                gates_out[d] = value
+
+            metas[me] = gates_out[me]
+            tri[...] = strict_upper(tok)
+
         for copy in loads:
             copy.wait()
         pl.semaphore_wait(barrier, len(targets))
@@ -399,6 +401,7 @@
             for send in sends:
                 issue(*send)
             if name is None:
+                make_tables()
                 wv[z, y] = wown[y]
                 near = [t for link, t in targets.items() if link[0] != "z"]
                 for far in range(NY // 2 + NX // 2):

time: 306 us -> 307 us (level)
  no operation moved by 1% of the time
where the time goes in v12:
time: 307 us; the launch traced here: 306 us
  Pallas kernels  305 us (99%)
    pallas_call x1, Pallas kernels, layer(): pl.pallas_call(functools.partial(layer_kernel, order, cap, spans, scope_o...  302 us

profile of v12, /device:TPU:1, one launch (start us, length us, event | category | flops | bytes accessed | tf_op | source)
XLA Modules:
  0.0 305.7 jit_solution(10771922252184400945)
XLA Ops:
  0.6 302.2 %layer.1 = (f32[3,16,32,384]{3,2,1,0:T(8,128)}, bf16[256,1024]{1,0:T(8,128)(2,1)}, f32[8,256]{1,0:T(8,128)}, bf16[32,96,1024]{2,1,0:T(8,128)(2,1)}, f32[4,32,256...) custom-call(bf16[256,1024]{1,0:T(8,128)(2,1)} %x_hbm.1, ...), custom_call_target="tpu_custom_call" | custom-call | tf_op jit(solution)/shard_map/layer/pallas_call | solution.py:735
  302.8 2.7 finish.1

commit v13 on v11

--- a/solution.py
+++ b/solution.py
@@ -205,7 +205,7 @@
                  grads, in_grad_hbm, gate_hbm, dxb, valb, dxs, xr, ur, gr, sel,
                  ids_ref, gates_ref, in_grad_ref, gate_ref, metas, gates_out, wown, wv, relay, xb, ub, gb, sb, a_s, d1_s, d3_s, y_s, dx_s, val_s, vb, key_s, acc_s,
                  recv, core_recv, wrecv, relay_recv, mrecv, send_sem, msend, load_sem, store_sem,
-                 lsem, rsend, rrecv, ysend, yrecv, dsend, drecv, vsem, osem, in_scope, in_plane):
+                 lsem, rsend, rrecv, ysend, yrecv, dsend, drecv, vsem, osem, in_scope):
     z, y, x, c = here()
     tok, hidden = x_hbm.shape
     rows, ff = xb.shape[0], a_s.shape[-1]
@@ -268,7 +268,12 @@
         for copy in tables + loads:
             copy.start()
         barrier = pltpu.get_barrier_semaphore()
-        tell(barrier, targets.values())
+        tell(barrier, [targets["z+"], targets["z-"]])
+
+        @each_other
+        def _(k):
+            tell(barrier, [at_offset(k)])
+
         for copy in tables:
             copy.wait()
 
@@ -285,7 +290,7 @@
         tri[...] = strict_upper(tok)
         for copy in loads:
             copy.wait()
-        pl.semaphore_wait(barrier, len(targets))
+        pl.semaphore_wait(barrier, GROUP + 1)
 
         back = {"x+": (0, 3), "x-": (0, 1), "y+": (3, 0), "y-": (1, 0)}
         def block(kind, dy, dx, dc=0):
@@ -400,10 +405,6 @@
                 issue(*send)
             if name is None:
                 wv[z, y] = wown[y]
-                near = [t for link, t in targets.items() if link[0] != "z"]
-                for far in range(NY // 2 + NX // 2):
-                    tell(in_plane.at[far], near)
-                    pl.semaphore_wait(in_plane.at[far], len(near))
 
                 @each_other
                 def _(k):
@@ -746,7 +747,7 @@
             dma((len(KINDS), NY * NX)), dma((len(KINDS), NY * NX)), dma((NZ, NY, 2, 2)), dma((len(RELAYS),)), dma((GROUP,)), dma((sends,)), dma((GROUP,)),
             dma((7,)), dma((2, 4)),
             dma((4,)), dma((2, OWN, HOPS)), dma((2, OWN, HOPS)), dma((OWN, 3, NY)), dma((OWN, 3, NY)),
-            dma((OWN,)), dma((OWN,)), dma((2, GROUP)), dma((1,)), pltpu.SemaphoreType.REGULAR, pltpu.SemaphoreType.REGULAR((NY // 2 + NX // 2,)),
+            dma((OWN,)), dma((OWN,)), dma((2, GROUP)), dma((1,)), pltpu.SemaphoreType.REGULAR,
         ],
         compiler_params=params(0),
     )(x, u, ids, gates, w1, w3, w2)

time: 306 us -> 305 us (level)
  no operation moved by 1% of the time
where the time goes in v13:
time: 305 us; the launch traced here: 304 us
  Pallas kernels  303 us (99%)
    pallas_call x1, Pallas kernels, layer(): pl.pallas_call(functools.partial(layer_kernel, order, cap, spans, scope_o...  301 us

profile of v13, /device:TPU:1, one launch (start us, length us, event | category | flops | bytes accessed | tf_op | source)
XLA Modules:
  0.0 304.3 jit_solution(10968792184888922854)
XLA Ops:
  0.6 300.7 %layer.1 = (f32[3,16,32,384]{3,2,1,0:T(8,128)}, bf16[256,1024]{1,0:T(8,128)(2,1)}, f32[8,256]{1,0:T(8,128)}, bf16[32,96,1024]{2,1,0:T(8,128)(2,1)}, f32[4,32,256...) custom-call(bf16[256,1024]{1,0:T(8,128)(2,1)} %x_hbm.1, ...), custom_call_target="tpu_custom_call" | custom-call | tf_op jit(solution)/shard_map/layer/pallas_call | solution.py:733
  301.4 2.7 finish.1

commit v14 on v13

--- a/solution.py
+++ b/solution.py
@@ -78,7 +78,7 @@
 RATE, D2D, HOP = 44700.0, 400000.0, 2.3
 PUT, TILE, ROWS = 1.0, 1.0, 0.4
 STEP = 5
-AHEAD, MORE = 5.0, 0.05
+AHEAD, MORE = 10.0, 0.0
 
 PIECE = {(0, None): (0, 1), (1, None): (1, 3), (1, 0): (1, 1), (1, 1): (2, 2)}
 RELAYS = ((0, None, "y+"), (1, 0, "y+"), (1, 1, "y-"))

time: 305 us -> 307 us (level)
  no operation moved by 1% of the time
where the time goes in v14:
time: 307 us
  Pallas kernels  306 us (100%)
    pallas_call x1, Pallas kernels, layer(): pl.pallas_call(functools.partial(layer_kernel, order, cap, spans, scope_o...  303 us

profile of v14, /device:TPU:1, one launch (start us, length us, event | category | flops | bytes accessed | tf_op | source)
XLA Modules:
  0.0 306.6 jit_solution(12406099902941913936)
XLA Ops:
  0.6 303.0 %layer.1 = (f32[3,16,32,384]{3,2,1,0:T(8,128)}, bf16[256,1024]{1,0:T(8,128)(2,1)}, f32[8,256]{1,0:T(8,128)}, bf16[32,96,1024]{2,1,0:T(8,128)(2,1)}, f32[4,32,256...) custom-call(bf16[256,1024]{1,0:T(8,128)(2,1)} %x_hbm.1, ...), custom_call_target="tpu_custom_call" | custom-call | tf_op jit(solution)/shard_map/layer/pallas_call | solution.py:733
  303.6 2.7 finish.1

commit v15 on v14

--- a/solution.py
+++ b/solution.py
@@ -78,7 +78,8 @@
 RATE, D2D, HOP = 44700.0, 400000.0, 2.3
 PUT, TILE, ROWS = 1.0, 1.0, 0.4
 STEP = 5
-AHEAD, MORE = 10.0, 0.0
+AHEAD, DEEP = 5.0, 12.0
+EARLY = {"z": 60.0, "y": 12.0, "x": 0.0}
 
 PIECE = {(0, None): (0, 1), (1, None): (1, 3), (1, 0): (1, 1), (1, 1): (2, 2)}
 RELAYS = ((0, None, "y+"), (1, 0, "y+"), (1, 1, "y-"))
@@ -104,7 +105,7 @@
         out = []
         for link, queue in pending.items():
             queue.sort()
-            while queue and free.get(link, 0.0) - now < AHEAD + MORE * now:
+            while queue and free.get(link, 0.0) - now < (AHEAD if now < EARLY[link[0]] else DEEP):
                 out.append(send(now, *queue.pop(0)[-1]))
         return out
 

time: 307 us -> 305 us (level)
  no operation moved by 1% of the time
where the time goes in v15:
time: 305 us; the launch traced here: 304 us
  Pallas kernels  303 us (99%)
    pallas_call x1, Pallas kernels, layer(): pl.pallas_call(functools.partial(layer_kernel, order, cap, spans, scope_o...  301 us

profile of v15, /device:TPU:1, one launch (start us, length us, event | category | flops | bytes accessed | tf_op | source)
XLA Modules:
  0.0 304.3 jit_solution(15029183741955992009)
XLA Ops:
  0.6 300.7 %layer.1 = (f32[3,16,32,384]{3,2,1,0:T(8,128)}, bf16[256,1024]{1,0:T(8,128)(2,1)}, f32[8,256]{1,0:T(8,128)}, bf16[32,96,1024]{2,1,0:T(8,128)(2,1)}, f32[4,32,256...) custom-call(bf16[256,1024]{1,0:T(8,128)(2,1)} %x_hbm.1, ...), custom_call_target="tpu_custom_call" | custom-call | tf_op jit(solution)/shard_map/layer/pallas_call | solution.py:734
  301.4 2.7 finish.1

commit v16 on v11

--- a/solution.py
+++ b/solution.py
@@ -84,6 +84,7 @@
 RELAYS = ((0, None, "y+"), (1, 0, "y+"), (1, 1, "y-"))
 
 
+ROUNDS = NY // 2 + NX // 2
 KINDS = ("A0", "A1", "B0", "B1")
 
 
@@ -150,12 +151,17 @@
         sends.append(core(0.0, (kind, 0, 0)))
     order.append((None, turn(0.0) + sends))
     todo, puts, done, now = [(dy, dx) for dy in range(NY) for dx in range(NX)], 0, 0, 0.0
+    known = 0
     while coming or todo or done < puts:
         coming.sort()
+        if known < ROUNDS and now > HOP * (known + 1):
+            order.append((("near", known), turn(now)))
+            known += 1
+            continue
         soon = coming[0][0] if coming else 1e9
         if soon > now:
             place = next((p for p in todo if all(pre + (kind,) + p in ready for kind in KINDS for pre in ((), ("core",)))), None)
-            if place is not None:
+            if place is not None and now > 15:
                 todo.remove(place)
                 order.append((("put",) + place, turn(now)))
                 puts += 1
@@ -291,6 +297,7 @@
         def block(kind, dy, dx, dc=0):
             return all_rows.at[place(dy, dx, dc), pl.ds(*spans[kind])]
 
+        near = [t for link, t in targets.items() if link[0] != "z"]
         row_copies = []
 
         def issue(name, link):
@@ -383,6 +390,15 @@
                 pass
             elif name[0] == "put":
                 put(*name[1:])
+            elif name[0] == "near":
+                _, k = name
+                pl.semaphore_wait(in_plane.at[k], len(near))
+                if k < ROUNDS - 1:
+                    tell(in_plane.at[k + 1], near)
+                else:
+                    @each_other
+                    def _(k):
+                        meta_copy(k).start()
             elif name[0] == "tile":
                 expert_rows(0, chips[name[1]:name[2]])
             elif name[0] == "R":
@@ -400,14 +416,7 @@
                 issue(*send)
             if name is None:
                 wv[z, y] = wown[y]
-                near = [t for link, t in targets.items() if link[0] != "z"]
-                for far in range(NY // 2 + NX // 2):
-                    tell(in_plane.at[far], near)
-                    pl.semaphore_wait(in_plane.at[far], len(near))
-
-                @each_other
-                def _(k):
-                    meta_copy(k).start()
+                tell(in_plane.at[0], near)
 
         for out in stores[-2:]:
             for copy in out:
@@ -746,7 +755,7 @@
             dma((len(KINDS), NY * NX)), dma((len(KINDS), NY * NX)), dma((NZ, NY, 2, 2)), dma((len(RELAYS),)), dma((GROUP,)), dma((sends,)), dma((GROUP,)),
             dma((7,)), dma((2, 4)),
             dma((4,)), dma((2, OWN, HOPS)), dma((2, OWN, HOPS)), dma((OWN, 3, NY)), dma((OWN, 3, NY)),
-            dma((OWN,)), dma((OWN,)), dma((2, GROUP)), dma((1,)), pltpu.SemaphoreType.REGULAR, pltpu.SemaphoreType.REGULAR((NY // 2 + NX // 2,)),
+            dma((OWN,)), dma((OWN,)), dma((2, GROUP)), dma((1,)), pltpu.SemaphoreType.REGULAR, pltpu.SemaphoreType.REGULAR((ROUNDS,)),
         ],
         compiler_params=params(0),
     )(x, u, ids, gates, w1, w3, w2)

time: 306 us -> 304 us (level)
  no operation moved by 1% of the time
where the time goes in v16:
time: 304 us
  Pallas kernels  303 us (100%)
    pallas_call x1, Pallas kernels, layer(): pl.pallas_call(functools.partial(layer_kernel, order, cap, spans, scope_o...  301 us

profile of v16, /device:TPU:1, one launch (start us, length us, event | category | flops | bytes accessed | tf_op | source)
XLA Modules:
  0.0 304.1 jit_solution(11908051180622604898)
XLA Ops:
  0.6 300.5 %layer.1 = (f32[3,16,32,384]{3,2,1,0:T(8,128)}, bf16[256,1024]{1,0:T(8,128)(2,1)}, f32[8,256]{1,0:T(8,128)}, bf16[32,96,1024]{2,1,0:T(8,128)(2,1)}, f32[4,32,256...) custom-call(bf16[256,1024]{1,0:T(8,128)(2,1)} %x_hbm.1, ...), custom_call_target="tpu_custom_call" | custom-call | tf_op jit(solution)/shard_map/layer/pallas_call | solution.py:741
  301.1 2.7 finish.1

commit v17 on v16

--- a/solution.py
+++ b/solution.py
@@ -275,20 +275,22 @@
             copy.start()
         barrier = pltpu.get_barrier_semaphore()
         tell(barrier, targets.values())
-        for copy in tables:
-            copy.wait()
-
-        @pl.loop(0, GROUP)
-        def _(d):
-            number = first_expert(d) + lax.broadcasted_iota(jnp.int32, (OWN, tok), 0)
-            value = jnp.full((OWN, tok), -1.0, F32)
-            for j in range(ids_ref.shape[0]):
-                chosen = ids_ref[pl.ds(j, 1), :] == number
-                value = jnp.where(chosen, jnp.broadcast_to(gates_ref[pl.ds(j, 1), :], value.shape), value)
-            gates_out[d] = value
-
-        metas[me] = gates_out[me]
-        tri[...] = strict_upper(tok)
+        def make_tables():
+            for copy in tables:
+                copy.wait()
+
+            @pl.loop(0, GROUP)
+            def _(d):
+                number = first_expert(d) + lax.broadcasted_iota(jnp.int32, (OWN, tok), 0)
+                value = jnp.full((OWN, tok), -1.0, F32)
+                for j in range(ids_ref.shape[0]):
+                    chosen = ids_ref[pl.ds(j, 1), :] == number
+                    value = jnp.where(chosen, jnp.broadcast_to(gates_ref[pl.ds(j, 1), :], value.shape), value)
+                gates_out[d] = value
+
+            metas[me] = gates_out[me]
+            tri[...] = strict_upper(tok)
+
         for copy in loads:
             copy.wait()
         pl.semaphore_wait(barrier, len(targets))
@@ -415,8 +417,9 @@
             for send in sends:
                 issue(*send)
             if name is None:
+                tell(in_plane.at[0], near)
+                make_tables()
                 wv[z, y] = wown[y]
-                tell(in_plane.at[0], near)
 
         for out in stores[-2:]:
             for copy in out:

time: 304 us -> 304 us (level)
  no operation moved by 1% of the time
where the time goes in v17:
time: 304 us
  Pallas kernels  303 us (100%)
    pallas_call x1, Pallas kernels, layer(): pl.pallas_call(functools.partial(layer_kernel, order, cap, spans, scope_o...  301 us

profile of v17, /device:TPU:1, one launch (start us, length us, event | category | flops | bytes accessed | tf_op | source)
XLA Modules:
  0.0 304.1 jit_solution(241906357402744872)
XLA Ops:
  0.6 300.5 %layer.1 = (f32[3,16,32,384]{3,2,1,0:T(8,128)}, bf16[256,1024]{1,0:T(8,128)(2,1)}, f32[8,256]{1,0:T(8,128)}, bf16[32,96,1024]{2,1,0:T(8,128)(2,1)}, f32[4,32,256...) custom-call(bf16[256,1024]{1,0:T(8,128)(2,1)} %x_hbm.1, ...), custom_call_target="tpu_custom_call" | custom-call | tf_op jit(solution)/shard_map/layer/pallas_call | solution.py:744
  301.1 2.7 finish.1

commit v18 on v17

--- a/solution.py
+++ b/solution.py
@@ -442,8 +442,11 @@
         def chunk(e, way, dist):
             return G.at[e, z_at(dist if way else NZ - dist)["z"]]
 
+        def half_in(kind):
+            return rem(y // 2 + 1 + kind - PART, 2)
+
         def part_of(ref, way, e, kind):
-            return ref.at[way, e, (kind - PART) % 2, (kind - PART) // 2]
+            return ref.at[way, e, half_in(kind), (kind - PART) // 2]
 
         def hop(e, way, kind):
             h = way
@@ -662,7 +665,8 @@
                 hop(last, way, kind).start()
 
         def keep(e, m, to, then_remote, then_local):
-            src = r1.at[0, e, to // 2, m, pl.ds(to % 2 * d_loc, d_loc)]
+            at = rem(to, 2) * d_loc
+            src = r1.at[0, e, to // 2, m, pl.ds(at if isinstance(at, int) else pl.multiple_of(at, 8), d_loc)]
             dst = grads.at[m, y * OWN + e]
             n = 0 if isinstance(m, slice) else m
 
@@ -684,14 +688,6 @@
             for to in range(NY):
                 keep(e, every, to, start, start)
 
-        for kind in range(PART, HOPS):
-            for way in (0, 1):
-                hop(last, way, kind).wait_recv()
-            add_into(part_of(r1, 0, last, kind), part_of(r1, 1, last, kind), part_of(G, last, z, kind))
-            m, h = (kind - PART) // 2, (kind - PART) % 2
-            for to in (2 * h, 2 * h + 1):
-                keep(last, m, to, start, start)
-
         def finish_up(e, kinds, matrices):
             for m in matrices:
                 for at in range(NY):
@@ -709,6 +705,13 @@
         @pl.loop(0, last)
         def _(e):
             finish_up(e, range(PART), [every])
+
+        for kind in range(PART, HOPS):
+            for way in (0, 1):
+                hop(last, way, kind).wait_recv()
+            add_into(part_of(r1, 0, last, kind), part_of(r1, 1, last, kind), part_of(G, last, z, kind))
+            for i in range(2):
+                keep(last, (kind - PART) // 2, 2 * half_in(kind) + i, start, start)
 
         finish_up(last, [FAR, SUM3, NEW3, TWO, *range(PART, HOPS)], range(3))
         for copy in results:

time: 304 us -> 306 us (level)
  no operation moved by 1% of the time
where the time goes in v18:
time: 306 us
  Pallas kernels  305 us (100%)
    pallas_call x1, Pallas kernels, layer(): pl.pallas_call(functools.partial(layer_kernel, order, cap, spans, scope_o...  302 us

profile of v18, /device:TPU:1, one launch (start us, length us, event | category | flops | bytes accessed | tf_op | source)
XLA Modules:
  0.0 305.7 jit_solution(11153971112355770643)
XLA Ops:
  0.6 302.2 %layer.1 = (f32[3,16,32,384]{3,2,1,0:T(8,128)}, bf16[256,1024]{1,0:T(8,128)(2,1)}, f32[8,256]{1,0:T(8,128)}, bf16[32,96,1024]{2,1,0:T(8,128)(2,1)}, f32[4,32,256...) custom-call(bf16[256,1024]{1,0:T(8,128)(2,1)} %x_hbm.1, ...), custom_call_target="tpu_custom_call" | custom-call | tf_op jit(solution)/shard_map/layer/pallas_call | solution.py:747
  302.8 2.7 finish.1
